TPU v7x, 256 devices: a whole 4x4x8 slice. The times are simulated.
256 devices in a mesh: row: 8 (over y, x_lo), col: 32 (over z, x_hi, core).
Axes of the slice: x: 4 (x_hi: 2, x_lo: 2; x = x_hi * 2 + x_lo), y: 4, z: 8, core: 2. Of those that a mesh axis runs over, the one named last changes fastest.
Arguments:
- pair_rep: bfloat16 [1024, 1024, 128], P('row', 'col'), may hold values from -6 to 6
- proj_weight: bfloat16 [2, 4, 128, 128], replicated, may hold values from -0.5 to 0.5
- gate_weight: bfloat16 [2, 128, 128], replicated, may hold values from -0.5 to 0.5
- out_weight: bfloat16 [2, 128, 128], replicated, may hold values from -0.5 to 0.5
- in_gain: float32 [2, 128], replicated, may hold values from 0.1 to 1.9
- out_gain: float32 [2, 128], replicated, may hold values from 0.1 to 1.9
Outputs:
- updated_pair: bfloat16 [1024, 1024, 128], P('row', 'col')
All inputs are finite; a program needn't handle non-finite values.
Results may differ from a plain program's by a relative error of at most 0.011.
Values may be sent and summed in bfloat16 or wider, within the bound.
No kernel may reach another device: no remote copies, remote signals or barrier semaphores. Data moves between devices by JAX's collectives and lax.ppermute only.
A program may use at most 64 MiB of HBM per device.

v0:
```python
import jax
import jax.numpy as jnp
from jax import lax
from jax.sharding import Mesh
from jax.sharding import PartitionSpec as P

ROW = ("row_0", "row_1")


epsilon = 1e-05


def sum_by_axis(terms, axes):
    subtotal = terms.astype(jnp.bfloat16)
    for axis in axes:
        subtotal = lax.psum_scatter(subtotal, axis, scatter_dimension=0, tiled=True)
    return subtotal.astype(jnp.float32)


def layer_norm(values, gain_row, reduce_axis):
    center = values - jnp.mean(values, axis=reduce_axis, keepdims=True)
    spread = jnp.mean(center * center, axis=reduce_axis, keepdims=True)
    return center * lax.rsqrt(spread + epsilon) * gain_row


def local(pair_rep, proj_weight, gate_weight, out_weight, in_gain, out_gain):
    current = pair_rep
    for update_index in range(2):
        widened = current.astype(jnp.float32)
        normed = layer_norm(widened, in_gain[update_index], 2).astype(jnp.bfloat16)
        projected = jnp.einsum(
            "ijc,pch->phij", normed, proj_weight[update_index], preferred_element_type=jnp.float32
        )
        left_hand = (jax.nn.sigmoid(projected[0]) * projected[1]).astype(jnp.bfloat16)
        right_hand = (jax.nn.sigmoid(projected[2]) * projected[3]).astype(jnp.bfloat16)
        gating = jax.nn.sigmoid(
            jnp.dot(normed, gate_weight[update_index], preferred_element_type=jnp.float32)
        )
        left_rows, right_rows = (
            lax.all_to_all(left_hand, "col", split_axis=0, concat_axis=2, tiled=True),
            lax.all_to_all(right_hand, "col", split_axis=0, concat_axis=2, tiled=True),
        )
        if update_index == 0:
            triangle = jnp.einsum(
                "gik,gjk->igj",
                left_rows,
                lax.all_gather(right_rows, ROW, axis=1, tiled=True),
                preferred_element_type=jnp.float32,
            )
        else:
            triangle = sum_by_axis(
                jnp.einsum(
                    "gki,gkj->igj", left_rows, right_rows, preferred_element_type=jnp.float32
                ),
                ROW,
            )
        returned = lax.all_to_all(
            triangle.astype(jnp.bfloat16), "col", split_axis=2, concat_axis=1, tiled=True
        )
        mixed_rows = layer_norm(
            returned.astype(jnp.float32), out_gain[update_index][None, :, None], 1
        ).astype(jnp.bfloat16)
        update = jnp.einsum(
            "ihj,hc->ijc", mixed_rows, out_weight[update_index], preferred_element_type=jnp.float32
        )
        current = (widened + gating * update).astype(jnp.bfloat16)
    return current


def solution(mesh):
    finer = Mesh(mesh.devices.reshape(4, 2, mesh.shape["col"]), ("row_0", "row_1", "col"))
    placed = (P(ROW, "col", None), P(), P(), P(), P(), P())
    return jax.shard_map(
        local, mesh=finer, in_specs=placed, out_specs=P(ROW, "col", None), check_vma=False
    )
```

profile of v0, /device:TPU:32, one launch (start us, length us, event | category | flops | bytes accessed | tf_op | source)
XLA Modules:
  0.0 534.2 jit_solution(13058157798516220307)
XLA Ops:
  6.5 2.0 copy.75
  9.1 1.4 convolution_bitcast_fusion.1
  10.5 1.1 fusion.49
  11.6 1.7 copy.79
  13.3 39.2 %all_to_all.90 = bf16[128,128,32]{1,2,0:T(8,128)(2,1)S(1)} all-to-all(bf16[128,128,32]{1,2,0:T(8,128)(2,1)} %copy.79), channel_id=1, replica_groups=mesh['row_0'=4,'row_1'=2,'col'=32] {'col'}, dimensions={0} | all-to-all | bytes 2097152 | tf_op jit(solution)/shard_map/all_to_all | solution.py:41
  52.6 1.3 copy.81
  54.9 33.7 %all_to_all.91 = bf16[128,128,32]{1,2,0:T(8,128)(2,1)S(1)} all-to-all(bf16[128,128,32]{1,2,0:T(8,128)(2,1)S(1)} %copy.82), channel_id=1, replica_groups=mesh['row_0'=4,'row_1'=2,'col'=32] {'col'}, dimensions={0} | all-to-all | bytes 2097152 | tf_op jit(solution)/shard_map/all_to_all | solution.py:40
  88.7 142.6 %all-gather.2.cloned.1.call-done = bf16[4,1024,1024]{2,1,0:T(8,128)(2,1)} async-done(((bf16[4,128,1024]{2,1,0:T(8,128)(2,1)}), bf16[4,1024,1024]{2,1,0:T(8,128)(2,1)}) %all-gather.2.cloned.1.call-update) | async-done | bytes 8388624 | tf_op jit(solution)/shard_map/all_gather | solution.py:47
  231.4 5.7 %fusion.42 = bf16[128,4,1024]{0,2,1:T(8,128)(2,1)S(1)} fusion(bf16[4,1024,1024]{2,1,0:T(8,128)(2,1)} %all-gather.2.cloned.1.call-done, bf16[4,128,1024]{1,2,0:T(8,128)(2,1)S(1)} %bitcast.134), kind=kOutput, calls=%fused_computation.62 | convolution fusion | flops 1074266112 | bytes 10485760 | tf_op jit(solution)/shard_map/gik,gjk->igj/dot_general | solution.py:44
  237.1 1.8 copy.85
  238.9 10.4 %all-to-all-start.2 = ((bf16[128,4,1024]{0,1,2:T(4,128)(2,1)}), bf16[128,4,1024]{0,1,2:T(4,128)(2,1)S(1)}, u32[]{:S(2)}, u32[]{:S(2)}) async-start(bf16[128,4,1024]{0,1,2:T(4,128)(2,1)} %copy.85), calls=%async_computation.2 | async-start | bytes 2097152 | tf_op jit(solution)/shard_map/all_to_all | solution.py:57
  249.5 27.8 %all-to-all-done.2 = bf16[128,4,1024]{0,1,2:T(4,128)(2,1)S(1)} async-done(((bf16[128,4,1024]{0,1,2:T(4,128)(2,1)}), bf16[128,4,1024]{0,1,2:T(4,128)(2,1)S(1)}, u32[]{:S(2)}, u32[]{:S(2)}) %all-to-all-start.2) | async-done | bytes 1048608 | tf_op jit(solution)/shard_map/all_to_all | solution.py:57
  279.3 1.2 convert_reduce_fusion
  280.9 1.4 convolution_bitcast_fusion
  282.2 1.1 fusion.51
  283.4 1.7 copy.94
  285.1 5.9 %all-to-all-start.3 = ((bf16[128,128,32]{1,2,0:T(8,128)(2,1)}), bf16[128,128,32]{1,2,0:T(8,128)(2,1)S(1)}, u32[]{:S(2)}, u32[]{:S(2)}) async-start(bf16[128,128,32]{1,2,0:T(8,128)(2,1)} %copy.94), calls=%async_computation.3 | async-start | bytes 2097152 | tf_op jit(solution)/shard_map/all_to_all | solution.py:41
  290.9 1.7 copy.96
  292.6 26.3 %all-to-all-done.3 = bf16[128,128,32]{1,2,0:T(8,128)(2,1)S(1)} async-done(((bf16[128,128,32]{1,2,0:T(8,128)(2,1)}), bf16[128,128,32]{1,2,0:T(8,128)(2,1)S(1)}, u32[]{:S(2)}, u32[]{:S(2)}) %all-to-all-start.3) | async-done | bytes 1048608 | tf_op jit(solution)/shard_map/all_to_all | solution.py:41
  319.0 5.9 %all-to-all-start.4 = ((bf16[128,128,32]{1,2,0:T(8,128)(2,1)}), bf16[128,128,32]{1,2,0:T(8,128)(2,1)}, u32[]{:S(2)}, u32[]{:S(2)}) async-start(bf16[128,128,32]{1,2,0:T(8,128)(2,1)} %copy.96), calls=%async_computation.4 | async-start | bytes 2097152 | tf_op jit(solution)/shard_map/all_to_all | solution.py:40
  325.0 27.9 %all-to-all-done.4 = bf16[128,128,32]{1,2,0:T(8,128)(2,1)} async-done(((bf16[128,128,32]{1,2,0:T(8,128)(2,1)}), bf16[128,128,32]{1,2,0:T(8,128)(2,1)}, u32[]{:S(2)}, u32[]{:S(2)}) %all-to-all-start.4) | async-done | bytes 1048608 | tf_op jit(solution)/shard_map/all_to_all | solution.py:40
  353.0 1.3 copy.97
  354.3 5.6 %convert_bitcast_fusion = bf16[1024,4,1024]{0,2,1:T(8,128)(2,1)} fusion(bf16[4,128,1024]{1,2,0:T(8,128)(2,1)S(1)} %bitcast.125, bf16[4,128,1024]{1,2,0:T(8,128)(2,1)S(1)} %bitcast.126), kind=kOutput, calls=%fused_computation | convolution fusion | flops 1077936128 | bytes 10485760 | tf_op jit(solution)/shard_map/gki,gkj->igj/dot_general | solution.py:52
  359.9 80.6 %reduce-scatter.5.cloned.1.call-done = bf16[256,4,1024]{0,2,1:T(8,128)(2,1)} async-done(((bf16[1024,4,1024]{0,2,1:T(8,128)(2,1)}), bf16[256,4,1024]{0,2,1:T(8,128)(2,1)}) %reduce-scatter.5.cloned.1.call-update) | async-done | bytes 2097168 | tf_op jit(solution)/shard_map/reduce_scatter | solution.py:16
  440.5 4.1 copy.120
  444.7 36.9 %reduce-scatter.7.cloned.1.call-done = bf16[128,4096]{1,0:T(8,128)(2,1)} async-done(((bf16[256,4096]{1,0:T(8,128)(2,1)}), bf16[128,4096]{1,0:T(8,128)(2,1)}) %reduce-scatter.7.cloned.1.call-update) | async-done | bytes 1048592
  481.6 1.6 copy.121
  483.2 1.8 copy.99
  485.0 9.8 %all-to-all-start.5 = ((bf16[128,4,1024]{0,1,2:T(4,128)(2,1)}), bf16[128,4,1024]{0,1,2:T(4,128)(2,1)S(1)}, u32[]{:S(2)}, u32[]{:S(2)}) async-start(bf16[128,4,1024]{0,1,2:T(4,128)(2,1)} %copy.99), calls=%async_computation.6 | async-start | bytes 2097152 | tf_op jit(solution)/shard_map/all_to_all | solution.py:57
  494.9 1.9 fusion.55
  496.8 25.9 %all-to-all-done.5 = bf16[128,4,1024]{0,1,2:T(4,128)(2,1)S(1)} async-done(((bf16[128,4,1024]{0,1,2:T(4,128)(2,1)}), bf16[128,4,1024]{0,1,2:T(4,128)(2,1)S(1)}, u32[]{:S(2)}, u32[]{:S(2)}) %all-to-all-start.5) | async-done | bytes 1048608 | tf_op jit(solution)/shard_map/all_to_all | solution.py:57
  526.0 1.7 copy.105
  (53 shorter events, 7.9 us)
Async XLA Ops:
  6.5 2.6 copy-start.5
  6.5 2.6 copy-start.1
  6.5 224.8 %all-gather.2.cloned.1.call-start = ((), (), s32[]{:S(2)}) async-start(), calls=%async_computation.8 | async-start | bytes 9437184 | tf_op jit(solution)/shard_map/all_gather | solution.py:47
  237.1 12.2 %copy-start.6 = (f32[2,128]{1,0:T(2,128)S(1)}, f32[2,128]{1,0:T(2,128)}, u32[]{:S(2)}) copy-start(f32[2,128]{1,0:T(2,128)} %param.11) | copy-start | bytes 3076
  238.9 38.4 %all-to-all-start.2 = ((bf16[128,4,1024]{0,1,2:T(4,128)(2,1)}), bf16[128,4,1024]{0,1,2:T(4,128)(2,1)S(1)}, u32[]{:S(2)}, u32[]{:S(2)}) async-start(bf16[128,4,1024]{0,1,2:T(4,128)(2,1)} %copy.85), calls=%async_computation.2 | async-start | bytes 2097152 | tf_op jit(solution)/shard_map/all_to_all | solution.py:57
  278.0 0.8 copy-start.3
  278.5 0.9 copy-start.2
  285.1 33.9 %all-to-all-start.3 = ((bf16[128,128,32]{1,2,0:T(8,128)(2,1)}), bf16[128,128,32]{1,2,0:T(8,128)(2,1)S(1)}, u32[]{:S(2)}, u32[]{:S(2)}) async-start(bf16[128,128,32]{1,2,0:T(8,128)(2,1)} %copy.94), calls=%async_computation.3 | async-start | bytes 2097152 | tf_op jit(solution)/shard_map/all_to_all | solution.py:41
  319.0 34.0 %all-to-all-start.4 = ((bf16[128,128,32]{1,2,0:T(8,128)(2,1)}), bf16[128,128,32]{1,2,0:T(8,128)(2,1)}, u32[]{:S(2)}, u32[]{:S(2)}) async-start(bf16[128,128,32]{1,2,0:T(8,128)(2,1)} %copy.96), calls=%async_computation.4 | async-start | bytes 2097152 | tf_op jit(solution)/shard_map/all_to_all | solution.py:40
  324.9 115.6 %reduce-scatter.5.cloned.1.call-start = ((), (), s32[]{:S(2)}) async-start(), calls=%async_computation.9 | async-start | bytes 10485760 | tf_op jit(solution)/shard_map/reduce_scatter | solution.py:16
  359.9 121.7 %reduce-scatter.7.cloned.1.call-start = ((), (), s32[]{:S(2)}) async-start(), calls=%async_computation.10 | async-start | bytes 3145728
  485.0 37.8 %all-to-all-start.5 = ((bf16[128,4,1024]{0,1,2:T(4,128)(2,1)}), bf16[128,4,1024]{0,1,2:T(4,128)(2,1)S(1)}, u32[]{:S(2)}, u32[]{:S(2)}) async-start(bf16[128,4,1024]{0,1,2:T(4,128)(2,1)} %copy.99), calls=%async_computation.6 | async-start | bytes 2097152 | tf_op jit(solution)/shard_map/all_to_all | solution.py:57
  523.4 1.6 copy-start
  523.4 1.6 copy-start.4
Sparse Core Ops, SparseCore 0:
  54.1 177.2 all-gather.1
  360.0 80.4 reduce-scatter.4
  444.8 36.7 reduce-scatter.6
where the time goes:
time: 536 us; the launch traced here: 534 us
  waiting for transfers between devices  368 us (69%)
  blocking collectives  72.9 us (14%)
  starting transfers between devices  32 us (6%)
  local copies, waits for them, and re-layouts  24.2 us (5%)
  matrix products  18.5 us (3%)
  between operations  13.4 us (2%)
    all_gather x1, waiting for transfers between devices, local(): lax.all_gather(right_rows, ROW, axis=1, tiled=True)  143 us
    reduce_scatter x1, waiting for transfers between devices, sum_by_axis(): subtotal = lax.psum_scatter(subtotal, axis, scatter_dimension=0, tiled=True)  80.6 us
    all_to_all x2, waiting for transfers between devices, local(): lax.all_to_all(triangle.astype(jnp.bfloat16), 'col', split_axis=2, concat...  53.7 us
    all_to_all x1, blocking collectives, local(): lax.all_to_all(right_hand, 'col', split_axis=0, concat_axis=2, tiled=True)  39.2 us
    unnamed x4, waiting for transfers between devices  36.9 us
    all_to_all x1, blocking collectives, local(): lax.all_to_all(left_hand, 'col', split_axis=0, concat_axis=2, tiled=True)  33.7 us
    all_to_all x1, waiting for transfers between devices, local(): lax.all_to_all(left_hand, 'col', split_axis=0, concat_axis=2, tiled=True)  27.9 us
    all_to_all x1, waiting for transfers between devices, local(): lax.all_to_all(right_hand, 'col', split_axis=0, concat_axis=2, tiled=True)  26.3 us
  transfers between devices with their start and end apart: 7, of which 7 were waited for; matrix products, arithmetic and copies ran while one was open for 1% of the time, Pallas kernels for 0%

commit v1 on v0

v1 whole, which is shorter than its diff:
```python
import jax
import jax.numpy as jnp
from jax import lax
from jax.sharding import Mesh
from jax.sharding import PartitionSpec as P

CHIPS = ("row", "half")
SWAP = [(0, 1), (1, 0)]


epsilon = 1e-05


def layer_norm(values, gain_row, reduce_axis):
    center = values - jnp.mean(values, axis=reduce_axis, keepdims=True)
    spread = jnp.mean(center * center, axis=reduce_axis, keepdims=True)
    return center * lax.rsqrt(spread + epsilon) * gain_row


def to_chips(pieces):
    return lax.all_to_all(pieces, CHIPS, split_axis=0, concat_axis=0, tiled=True)


def local(pair_rep, proj_weight, gate_weight, out_weight, in_gain, out_gain):
    core = lax.axis_index("core")
    current = pair_rep
    for update_index in range(2):
        widened = current.astype(jnp.float32)
        normed = layer_norm(widened, in_gain[update_index], 2).astype(jnp.bfloat16)
        projected = jnp.einsum(
            "ijc,pch->phji", normed, proj_weight[update_index], preferred_element_type=jnp.float32
        )
        left_hand = (jax.nn.sigmoid(projected[0]) * projected[1]).astype(jnp.bfloat16)
        right_hand = (jax.nn.sigmoid(projected[2]) * projected[3]).astype(jnp.bfloat16)
        gating = jax.nn.sigmoid(
            jnp.dot(normed, gate_weight[update_index], preferred_element_type=jnp.float32)
        )
        operands = to_chips(jnp.stack([left_hand, right_hand], axis=1)).reshape(8, 16, 2, 32, 128)
        left, right = operands[:, :, 0], operands[:, :, 1]
        if update_index == 0:
            product = jnp.einsum(
                "rqsf,tqsg->rtgf", left, right, preferred_element_type=jnp.float32
            ).reshape(8, 16, 2, 32, 128)
            kept = lax.dynamic_index_in_dim(product, core, 2, keepdims=False)
            given = lax.dynamic_index_in_dim(product, 1 - core, 2, keepdims=False)
            taken = lax.ppermute(given.astype(jnp.bfloat16), "core", SWAP)
            triangle = (kept + taken.astype(jnp.float32)).astype(jnp.bfloat16)
        else:
            other = lax.ppermute(left, "core", SWAP)
            first = core == 0
            whole = jnp.stack(
                [jnp.where(first, left, other), jnp.where(first, other, left)], axis=2
            ).reshape(8, 8, 128, 128)
            triangle = jnp.einsum(
                "rbif,rqsf->bqsi", whole, right, preferred_element_type=jnp.float32
            ).astype(jnp.bfloat16)
        returned = to_chips(triangle.reshape(128, 32, 128))
        mixed = layer_norm(
            returned.astype(jnp.float32), out_gain[update_index][:, None, None], 0
        ).astype(jnp.bfloat16)
        update = jnp.einsum(
            "hji,hc->ijc", mixed, out_weight[update_index], preferred_element_type=jnp.float32
        )
        current = (widened + gating * update).astype(jnp.bfloat16)
    return current


def solution(mesh):
    finer = Mesh(mesh.devices.reshape(8, 16, 2), ("row", "half", "core"))
    placed = (P("row", ("half", "core"), None), P(), P(), P(), P(), P())
    return jax.shard_map(
        local, mesh=finer, in_specs=placed, out_specs=P("row", ("half", "core"), None), check_vma=False
    )
```

time: 536 us -> 245 us (0.46)
  waiting for transfers between devices: 368 us -> 116 us
  blocking collectives: 72.9 us -> 58.5 us
  between operations: 13.4 us -> 0.3 us
  matrix products: 18.5 us -> 11.2 us
  local copies, waits for them, and re-layouts: 24.2 us -> 17.9 us
    all_gather x1 -> x0, waiting for transfers between devices: 143 us -> none  [local(): lax.all_gather(right_rows, ROW, axis=1, tiled=True)]
    reduce_scatter x1 -> x0, waiting for transfers between devices: 80.6 us -> none  [sum_by_axis(): subtotal = lax.psum_scatter(subtotal, axis, scatter_dimension=0, tiled=True)]
    unnamed x4 -> x0, waiting for transfers between devices: 36.9 us -> none
    all_to_all x2 -> x1, blocking collectives: 72.9 us -> 58.5 us  [to_chips(): lax.all_to_all(pieces, CHIPS, split_axis=0, concat_axis=0, tiled=True)]
    dot_general x6, matrix products: 15.5 us -> 7.42 us  [the longest x2 2.74 us: local(): jnp.einsum('ijc,pch->phji', normed, proj_weight[update_index], preferred_...]
    convert_element_type x7 -> x2, local copies, waits for them, and re-layouts: 8.05 us -> 1.32 us  [the longest x1 1.07 us: local(): triangle = jnp.einsum('rbif,rqsf->bqsi', whole, right, preferred_element_...]
    another operation x0 -> x3, local copies, waits for them, and re-layouts: none -> 6.71 us  [the longest x2 6.06 us: local(): jnp.stack([left_hand, right_hand], axis=1)]
    ppermute x0 -> x2, waiting for transfers between devices: none -> 5.65 us  [the longest x1 3 us: local(): other = lax.ppermute(left, 'core', SWAP)]
  transfers between devices with their start and end apart: 7 -> 5, of which waited for: 7 -> 5; matrix products, arithmetic and copies ran while one was open for 1% -> 2% of each run, Pallas kernels for 0% -> 0%
where the time goes in v1:
time: 245 us; the launch traced here: 244 us
  waiting for transfers between devices  116 us (47%)
  blocking collectives  58.5 us (24%)
  starting transfers between devices  29.8 us (12%)
  local copies, waits for them, and re-layouts  17.9 us (7%)
  matrix products  11.2 us (5%)
  other arithmetic  9.85 us (4%)
    all_to_all x3, waiting for transfers between devices, to_chips(): lax.all_to_all(pieces, CHIPS, split_axis=0, concat_axis=0, tiled=True)  111 us
    all_to_all x1, blocking collectives, to_chips(): lax.all_to_all(pieces, CHIPS, split_axis=0, concat_axis=0, tiled=True)  58.5 us
    all_to_all x3, starting transfers between devices, to_chips(): lax.all_to_all(pieces, CHIPS, split_axis=0, concat_axis=0, tiled=True)  29.7 us
    another operation x2, local copies, waits for them, and re-layouts, local(): jnp.stack([left_hand, right_hand], axis=1)  6.06 us
    unnamed x21, local copies, waits for them, and re-layouts  5.83 us
  transfers between devices with their start and end apart: 5, of which 5 were waited for; matrix products, arithmetic and copies ran while one was open for 2% of the time, Pallas kernels for 0%

profile of v1, /device:TPU:32, one launch (start us, length us, event | category | flops | bytes accessed | tf_op | source)
XLA Modules:
  0.0 244.1 jit_solution(3749618304182142776)
XLA Ops:
  0.0 2.0 copy.51
  2.6 1.4 convolution_bitcast_fusion.1
  4.0 0.6 fusion.56
  4.6 0.6 fusion.57
  5.3 3.0 %copy.59 = bf16[128,2,32,128]{3,2,1,0:T(8,128)(2,1)} copy(bf16[128,2,32,128]{0,3,2,1:T(8,128)(2,1)S(1)} %pad_maximum_fusion) | data formatting | bytes 4194304 | tf_op jit(solution)/shard_map/stack | solution.py:38
  8.4 15.0 %all-to-all-start = ((bf16[128,2,32,128]{3,2,1,0:T(8,128)(2,1)}), bf16[128,2,32,128]{3,2,1,0:T(8,128)(2,1)S(1)}, u32[]{:S(2)}, u32[]{:S(2)}) async-start(bf16[128,2,32,128]{3,2,1,0:T(8,128)(2,1)} %copy.59), calls=%async_computation | async-start | bytes 4194304 | tf_op jit(solution)/shard_map/all_to_all | solution.py:21
  23.4 52.6 %all-to-all-done = bf16[128,2,32,128]{3,2,1,0:T(8,128)(2,1)S(1)} async-done(((bf16[128,2,32,128]{3,2,1,0:T(8,128)(2,1)}), bf16[128,2,32,128]{3,2,1,0:T(8,128)(2,1)S(1)}, u32[]{:S(2)}, u32[]{:S(2)}) %all-to-all-start) | async-done | bytes 2097184 | tf_op jit(solution)/shard_map/all_to_all | solution.py:21
  75.9 1.3 convolution_bitcast_fusion.2
  77.7 1.9 copy-done
  80.0 2.6 %collective-permute-done = bf16[8,16,32,128]{3,2,1,0:T(8,128)(2,1)S(1)} collective-permute-done((bf16[8,16,32,128]{3,2,1,0:T(8,128)(2,1)S(1)}, bf16[8,16,32,128]{3,2,1,0:T(8,128)(2,1)S(1)}, u32[]{:S(2)}, u32[]{:S(2)}) %collective-permute-start) | collective-permute-done | bytes 1048608 | tf_op jit(solution)/shard_map/ppermute | solution.py:46
  82.7 2.9 %fusion.44 = bf16[8,16,32,128]{3,2,1,0:T(8,128)(2,1)} fusion(bf16[8,16,32,128]{3,2,1,0:T(8,128)(2,1)S(1)} %collective-permute-done, f32[8,16,2,32,128]{4,3,2,1,0:T(8,128)} %bitcast.174, s32[]{:T(128)S(6)} %select_n.19), kind=kLoop, calls=%fused_computation.72 | loop fusion | flops 1572864 | bytes 4194308 | tf_op jit(solution)/shard_map/convert_element_type | solution.py:47
  85.6 7.4 %all-to-all-start.1 = ((bf16[128,32,128]{2,1,0:T(8,128)(2,1)}), bf16[128,32,128]{2,1,0:T(8,128)(2,1)S(1)}, u32[]{:S(2)}, u32[]{:S(2)}) async-start(bf16[128,32,128]{2,1,0:T(8,128)(2,1)} %bitcast.22), calls=%async_computation.1 | async-start | bytes 2097152 | tf_op jit(solution)/shard_map/all_to_all | solution.py:21
  93.0 1.9 fusion.61
  94.9 29.1 %all-to-all-done.1 = bf16[128,32,128]{2,1,0:T(8,128)(2,1)S(1)} async-done(((bf16[128,32,128]{2,1,0:T(8,128)(2,1)}), bf16[128,32,128]{2,1,0:T(8,128)(2,1)S(1)}, u32[]{:S(2)}, u32[]{:S(2)}) %all-to-all-start.1) | async-done | bytes 1048608 | tf_op jit(solution)/shard_map/all_to_all | solution.py:21
  124.9 0.7 copy-done.1
  125.6 1.2 convert_reduce_fusion
  127.1 1.4 convolution_bitcast_fusion
  128.5 1.1 fusion.58
  129.9 3.0 %copy.69 = bf16[128,2,32,128]{3,2,1,0:T(8,128)(2,1)} copy(bf16[128,2,32,128]{0,3,2,1:T(8,128)(2,1)S(1)} %pad_maximum_fusion.1) | data formatting | bytes 4194304 | tf_op jit(solution)/shard_map/stack | solution.py:38
  132.9 58.5 %all_to_all.20 = bf16[128,2,32,128]{3,2,1,0:T(8,128)(2,1)S(1)} all-to-all(bf16[128,2,32,128]{3,2,1,0:T(8,128)(2,1)} %copy.69), channel_id=1, replica_groups=mesh['row'=8,'half'=16,'core'=2] {'row','half'}, dimensions={0} | all-to-all | bytes 4194304 | tf_op jit(solution)/shard_map/all_to_all | solution.py:21
  191.4 1.9 fusion.78
  193.3 3.0 %collective-permute-done.1 = bf16[8,16,32,128]{3,2,1,0:T(8,128)(2,1)} collective-permute-done((bf16[8,16,32,128]{3,2,1,0:T(8,128)(2,1)}, bf16[8,16,32,128]{3,2,1,0:T(8,128)(2,1)}, u32[]{:S(2)}, u32[]{:S(2)}) %collective-permute-start.1) | collective-permute-done | bytes 1048608 | tf_op jit(solution)/shard_map/ppermute | solution.py:49
  196.3 1.4 select_bitcast_fusion.1
  197.9 0.6 copy.71
  199.1 1.3 fusion.48
  200.4 1.1 copy.73
  201.5 7.3 %all-to-all-start.3 = ((bf16[128,32,128]{2,1,0:T(8,128)(2,1)}), bf16[128,32,128]{2,1,0:T(8,128)(2,1)S(1)}, u32[]{:S(2)}, u32[]{:S(2)}) async-start(bf16[128,32,128]{2,1,0:T(8,128)(2,1)} %bitcast.49), calls=%async_computation.3 | async-start | bytes 2097152 | tf_op jit(solution)/shard_map/all_to_all | solution.py:21
  208.8 1.9 fusion.64
  210.7 29.1 %all-to-all-done.3 = bf16[128,32,128]{2,1,0:T(8,128)(2,1)S(1)} async-done(((bf16[128,32,128]{2,1,0:T(8,128)(2,1)}), bf16[128,32,128]{2,1,0:T(8,128)(2,1)S(1)}, u32[]{:S(2)}, u32[]{:S(2)}) %all-to-all-start.3) | async-done | bytes 1048608 | tf_op jit(solution)/shard_map/all_to_all | solution.py:21
  240.8 0.6 copy-done.2
  241.4 1.0 fusion.21
  242.4 1.7 copy.76
  (43 shorter events, 4.8 us)
Async XLA Ops:
  0.0 2.6 %copy-start.6 = (f32[2,128]{1,0:T(2,128)S(1)}, f32[2,128]{1,0:T(2,128)}, u32[]{:S(2)}) copy-start(f32[2,128]{1,0:T(2,128)} %param.10) | copy-start | bytes 3076
  0.0 2.6 %copy-start.4 = (bf16[2,4,128,128]{3,2,1,0:T(8,128)(2,1)S(1)}, bf16[2,4,128,128]{3,2,1,0:T(8,128)(2,1)}, u32[]{:S(2)}) copy-start(bf16[2,4,128,128]{3,2,1,0:T(8,128)(2,1)} %param.7) | copy-start | bytes 786436
  8.4 67.6 %all-to-all-start = ((bf16[128,2,32,128]{3,2,1,0:T(8,128)(2,1)}), bf16[128,2,32,128]{3,2,1,0:T(8,128)(2,1)S(1)}, u32[]{:S(2)}, u32[]{:S(2)}) async-start(bf16[128,2,32,128]{3,2,1,0:T(8,128)(2,1)} %copy.59), calls=%async_computation | async-start | bytes 4194304 | tf_op jit(solution)/shard_map/all_to_all | solution.py:21
  77.7 1.9 copy-start
  79.9 2.7 %collective-permute-start = (bf16[8,16,32,128]{3,2,1,0:T(8,128)(2,1)S(1)}, bf16[8,16,32,128]{3,2,1,0:T(8,128)(2,1)S(1)}, u32[]{:S(2)}, u32[]{:S(2)}) collective-permute-start(bf16[8,16,32,128]{3,2,1,0:T(8,128)(2,1)S(1)} %fusion.51), channel_id=1, source_target_pairs={{0,1},{1,0},{2,3},{3,2},{4,5},{5,4},{6,7},{7,6},{8,9},{9,8},{10,11... | collective-permute-start | bytes 3145736 | tf_op jit(solution)/shard_map/ppermute | solution.py:46
  85.6 7.4 %copy-start.7 = (f32[2,128]{1,0:T(2,128)S(1)}, f32[2,128]{1,0:T(2,128)}, u32[]{:S(2)}) copy-start(f32[2,128]{1,0:T(2,128)} %param.11) | copy-start | bytes 3076
  85.6 7.4 %copy-start.5 = (bf16[2,128,128]{2,1,0:T(8,128)(2,1)S(1)}, bf16[2,128,128]{2,1,0:T(8,128)(2,1)}, u32[]{:S(2)}) copy-start(bf16[2,128,128]{2,1,0:T(8,128)(2,1)} %param.8) | copy-start | bytes 196612
  85.6 38.4 %all-to-all-start.1 = ((bf16[128,32,128]{2,1,0:T(8,128)(2,1)}), bf16[128,32,128]{2,1,0:T(8,128)(2,1)S(1)}, u32[]{:S(2)}, u32[]{:S(2)}) async-start(bf16[128,32,128]{2,1,0:T(8,128)(2,1)} %bitcast.22), calls=%async_computation.1 | async-start | bytes 2097152 | tf_op jit(solution)/shard_map/all_to_all | solution.py:21
  124.0 1.6 copy-start.1
  124.0 1.6 copy-start.8
  193.3 3.0 %collective-permute-start.1 = (bf16[8,16,32,128]{3,2,1,0:T(8,128)(2,1)}, bf16[8,16,32,128]{3,2,1,0:T(8,128)(2,1)}, u32[]{:S(2)}, u32[]{:S(2)}) collective-permute-start(bf16[8,16,32,128]{3,2,1,0:T(8,128)(2,1)} %get-tuple-element.10), channel_id=1, source_target_pairs={{0,1},{1,0},{2,3},{3,2},{4,5},{5,4},{6,7},{7,6},{8,9},{9,8},{10,11... | collective-permute-start | bytes 3145736 | tf_op jit(solution)/shard_map/ppermute | solution.py:49
  197.9 1.2 copy-start.3
  201.5 38.4 %all-to-all-start.3 = ((bf16[128,32,128]{2,1,0:T(8,128)(2,1)}), bf16[128,32,128]{2,1,0:T(8,128)(2,1)S(1)}, u32[]{:S(2)}, u32[]{:S(2)}) async-start(bf16[128,32,128]{2,1,0:T(8,128)(2,1)} %bitcast.49), calls=%async_computation.3 | async-start | bytes 2097152 | tf_op jit(solution)/shard_map/all_to_all | solution.py:21
  210.7 30.1 %copy-start.9 = (bf16[2,128,128]{2,1,0:T(8,128)(2,1)S(1)}, bf16[2,128,128]{2,1,0:T(8,128)(2,1)}, u32[]{:S(2)}) copy-start(bf16[2,128,128]{2,1,0:T(8,128)(2,1)} %param.9) | copy-start | bytes 196612
  239.8 1.6 copy-start.2

commit v2 on v1

v2 whole, which is shorter than its diff:
```python
import jax
import jax.numpy as jnp
from jax import lax
from jax.experimental import pallas as pl
from jax.experimental.pallas import tpu as pltpu
from jax.sharding import Mesh
from jax.sharding import PartitionSpec as P

CHIPS = ("row", "half")
SWAP = [(0, 1), (1, 0)]
F32 = jnp.float32
BF16 = jnp.bfloat16
PITCH = 40
WIDE = 136


epsilon = 1e-05


def dot(a, b):
    return lax.dot_general(a, b, (((1,), (0,)), ((), ())), preferred_element_type=F32)


def sigmoid(values):
    return 0.5 * jnp.tanh(0.5 * values) + 0.5


def layer_norm(values, gain):
    center = values - jnp.sum(values, axis=0, keepdims=True) * (1.0 / 128)
    spread = jnp.sum(center * center, axis=0, keepdims=True) * (1.0 / 128)
    return center * lax.rsqrt(spread + epsilon) * gain


def column(row):
    return jnp.broadcast_to(row, (128, 128)).T


def turn(matrix):
    return matrix.astype(F32).T.astype(BF16)


def spread_rows(source, scratch):
    def step(n, _):
        for part in range(4):
            at = n * 4 + part
            scratch[pl.ds(pl.multiple_of(at * PITCH, 8), 32), :] = source[at].astype(F32)
        return _

    lax.fori_loop(0, 32, step, 0)


def project(channels, gain, weights, hands, j):
    normed = layer_norm(channels, gain).astype(BF16)
    projected = dot(weights[...], normed)
    at = pl.ds(pl.multiple_of(j * WIDE, 8), 128)
    hands[0, at, :] = sigmoid(projected[0:128]) * projected[128:256]
    hands[1, at, :] = sigmoid(projected[256:384]) * projected[384:512]


def gather_hands(hands, send):
    def step(n, _):
        for part in range(4):
            h = n * 4 + part
            for side in range(2):
                send[h, side] = hands[side, pl.ds(h, 32, stride=WIDE), :].astype(BF16)
        return _

    lax.fori_loop(0, 32, step, 0)


def set_weights(weights, proj, update_index):
    for p in range(4):
        weights[p * 128 : (p + 1) * 128, :] = turn(proj[update_index, p])


def first_kernel(x, proj, in_gain, send, turned, rows, hands, weights):
    set_weights(weights, proj, 0)
    gain = column(in_gain[0:1, :])
    spread_rows(x, rows)

    def step(j, _):
        channels = rows[pl.ds(j, 128, stride=PITCH), :].T
        turned[j] = channels.astype(BF16)
        project(channels, gain, weights, hands, j)
        return _

    lax.fori_loop(0, 32, step, 0, unroll=2)
    gather_hands(hands, send)


def new_channels(update_index, tri, turned, gain_in, gain_out, gate, out, j):
    mixed = layer_norm(tri[pl.ds(j, 128, stride=PITCH), :], gain_out).astype(BF16)
    change = dot(out, mixed)
    old = turned[j].astype(F32)
    normed = layer_norm(old, gain_in).astype(BF16)
    return old + sigmoid(dot(gate, normed)) * change


def middle_kernel(returned, turned, proj, gate_w, out_w, in_gain, out_gain, send, newer, tri, hands, weights):
    set_weights(weights, proj, 1)
    gain_in, gain_out, gain_next = column(in_gain[0:1, :]), column(out_gain[0:1, :]), column(in_gain[1:2, :])
    gate, out = turn(gate_w[0]), turn(out_w[0])
    spread_rows(returned, tri)

    def step(j, _):
        channels = new_channels(0, tri, turned, gain_in, gain_out, gate, out, j).astype(BF16)
        newer[j] = channels
        project(channels.astype(F32), gain_next, weights, hands, j)
        return _

    lax.fori_loop(0, 32, step, 0, unroll=2)
    gather_hands(hands, send)


def last_kernel(returned, turned, gate_w, out_w, in_gain, out_gain, final, tri, rows):
    gain_in, gain_out = column(in_gain[1:2, :]), column(out_gain[1:2, :])
    gate, out = turn(gate_w[1]), turn(out_w[1])
    spread_rows(returned, tri)

    def step(j, _):
        channels = new_channels(1, tri, turned, gain_in, gain_out, gate, out, j)
        rows[pl.ds(j, 128, stride=PITCH), :] = channels.T
        return _

    lax.fori_loop(0, 32, step, 0, unroll=2)

    def collect(n, _):
        for part in range(4):
            at = n * 4 + part
            final[at] = rows[pl.ds(pl.multiple_of(at * PITCH, 8), 32), :].astype(BF16)
        return _

    lax.fori_loop(0, 32, collect, 0)


def side_of(operands, r, side):
    return operands[r, :, side].reshape(512, 128)


def given_kernel(core, operands, given, kept_rows, lefts, turned):
    for r in range(8):
        lefts[:, r * 128 : (r + 1) * 128] = side_of(operands, r, 0)
        turned[r * 128 : (r + 1) * 128, :] = turn(side_of(operands, r, 1))
    for q in range(16):
        kept_rows[q * 32 : (q + 1) * 32, :] = turned[
            pl.ds(pl.multiple_of(q * 64 + core[0] * 32, 32), 32), :
        ]
    for q in range(0, 16, 4):
        block = jnp.concatenate(
            [turned[pl.ds(pl.multiple_of(p * 64 + 32 - core[0] * 32, 32), 32), :] for p in range(q, q + 4)], axis=0
        )
        product = dot(block, lefts[...]).astype(BF16)
        for r in range(8):
            given[r, q : q + 4] = product[:, r * 128 : (r + 1) * 128].reshape(4, 32, 128)


def kept_kernel(kept_rows, operands, kept):
    lefts = jnp.concatenate([side_of(operands, r, 0) for r in range(8)], axis=1)
    for q in range(0, 16, 4):
        product = dot(kept_rows[q * 32 : (q + 4) * 32, :], lefts)
        for r in range(8):
            kept[r, q : q + 4] = product[:, r * 128 : (r + 1) * 128].reshape(4, 32, 128)


def incoming_kernel(core, operands, other, products, lefts):
    for r in range(8):
        for q in range(16):
            own = pl.multiple_of(q * 64 + core[0] * 32, 32)
            swapped = pl.multiple_of(q * 64 + 32 - core[0] * 32, 32)
            lefts[pl.ds(own, 32), r * 128 : (r + 1) * 128] = operands[r, q, 0]
            lefts[pl.ds(swapped, 32), r * 128 : (r + 1) * 128] = other[r, q]
    rights = jnp.concatenate([side_of(operands, r, 1) for r in range(8)], axis=1)
    for b in range(0, 8, 2):
        product = lax.dot_general(
            rights, lefts[b * 128 : (b + 2) * 128, :], (((1,), (1,)), ((), ())), preferred_element_type=F32
        ).astype(BF16)
        for part in range(2):
            products[b + part] = product[:, part * 128 : (part + 1) * 128].reshape(16, 32, 128)


def shape(dims, kind=BF16):
    return jax.ShapeDtypeStruct(dims, kind)


def call(body, outs, scratch, *args, scalars=0):
    vmem = pl.BlockSpec(memory_space=pltpu.VMEM)
    smem = pl.BlockSpec(memory_space=pltpu.SMEM)
    return pl.pallas_call(
        body,
        out_shape=outs,
        in_specs=[smem] * scalars + [vmem] * (len(args) - scalars),
        out_specs=[vmem] * len(outs),
        scratch_shapes=[pltpu.VMEM(dims, kind) for dims, kind in scratch],
        compiler_params=pltpu.CompilerParams(vmem_limit_bytes=48 * 1024 * 1024),
        name=body.__name__,
    )(*args)


def to_chips(pieces):
    return lax.all_to_all(pieces, CHIPS, split_axis=0, concat_axis=0, tiled=True)


ROWS = ((128 * PITCH, 128), F32)
HANDS = ((2, 32 * WIDE, 128), F32)
WEIGHTS = ((512, 128), BF16)
SEND = shape((128, 2, 32, 128))
TURNED = shape((32, 128, 128))
HALF = (8, 16, 32, 128)


def local(pair_rep, proj_weight, gate_weight, out_weight, in_gain, out_gain):
    core = lax.axis_index("core").astype(jnp.int32).reshape(1)
    send, turned = call(first_kernel, [SEND, TURNED], [ROWS, HANDS, WEIGHTS], pair_rep, proj_weight, in_gain)
    operands = to_chips(send).reshape(8, 16, 2, 32, 128)
    given, kept_rows = call(
        given_kernel,
        [shape(HALF), shape((512, 512))],
        [((512, 1024), BF16), ((1024, 512), BF16)],
        core,
        operands,
        scalars=1,
    )
    taken = lax.ppermute(given, "core", SWAP)
    (kept,) = call(kept_kernel, [shape(HALF, F32)], [], kept_rows, operands)
    triangle = (kept + taken.astype(F32)).astype(BF16)
    returned = to_chips(triangle.reshape(128, 32, 128))
    send, turned = call(
        middle_kernel,
        [SEND, TURNED],
        [ROWS, HANDS, WEIGHTS],
        returned,
        turned,
        proj_weight,
        gate_weight,
        out_weight,
        in_gain,
        out_gain,
    )
    operands = to_chips(send).reshape(8, 16, 2, 32, 128)
    other = lax.ppermute(operands[:, :, 0], "core", SWAP)
    (triangle,) = call(incoming_kernel, [shape(HALF)], [((1024, 1024), BF16)], core, operands, other, scalars=1)
    returned = to_chips(triangle.reshape(128, 32, 128))
    (final,) = call(
        last_kernel,
        [shape((128, 32, 128))],
        [ROWS, ROWS],
        returned,
        turned,
        gate_weight,
        out_weight,
        in_gain,
        out_gain,
    )
    return final


def solution(mesh):
    finer = Mesh(mesh.devices.reshape(8, 16, 2), ("row", "half", "core"))
    placed = (P("row", ("half", "core"), None), P(), P(), P(), P(), P())
    return jax.shard_map(
        local, mesh=finer, in_specs=placed, out_specs=P("row", ("half", "core"), None), check_vma=False
    )
```

time: 245 us -> 240 us (0.980)
  blocking collectives: 58.5 us -> 135 us
  waiting for transfers between devices: 116 us -> 57.1 us
  Pallas kernels: 0 us -> 27.7 us
  starting transfers between devices: 29.8 us -> 15.2 us
  local copies, waits for them, and re-layouts: 17.9 us -> 4.69 us
  matrix products: 11.2 us -> 0 us
  other arithmetic: 9.85 us -> 0.32 us
    all_to_all x1 -> x3, blocking collectives: 58.5 us -> 135 us  [to_chips(): lax.all_to_all(pieces, CHIPS, split_axis=0, concat_axis=0, tiled=True)]
    all_to_all x3 -> x1, waiting for transfers between devices: 111 us -> 52.6 us  [to_chips(): lax.all_to_all(pieces, CHIPS, split_axis=0, concat_axis=0, tiled=True)]
    pallas_call x0 -> x6, Pallas kernels: none -> 27.7 us  [call(): pl.pallas_call(body, out_shape=outs, in_specs=[smem] * scalars + [vmem] *...]
    all_to_all x3 -> x1, starting transfers between devices: 29.7 us -> 15 us  [to_chips(): lax.all_to_all(pieces, CHIPS, split_axis=0, concat_axis=0, tiled=True)]
    dot_general x8 -> x0, matrix products: 11.2 us -> none  [the longest x2 3.74 us: local(): jnp.dot(normed, gate_weight[update_index], preferred_element_type=jnp.flo...]
    another operation x3 -> x0, local copies, waits for them, and re-layouts: 6.71 us -> none  [the longest x2 6.06 us: local(): jnp.stack([left_hand, right_hand], axis=1)]
    convert_element_type x6 -> x1, other arithmetic: 5.93 us -> 0.32 us  [local(): triangle = (kept + taken.astype(F32)).astype(BF16)]
    convert_element_type x3 -> x0, local copies, waits for them, and re-layouts: 3 us -> none  [the longest x1 1.68 us: local(): current = (widened + gating * update).astype(jnp.bfloat16)]
  transfers between devices with their start and end apart: 5 -> 3, of which waited for: 5 -> 3; matrix products, arithmetic and copies ran while one was open for 2% -> 0% of each run, Pallas kernels for 0% -> 0%
where the time goes in v2:
time: 240 us
  blocking collectives  135 us (56%)
  waiting for transfers between devices  57.1 us (24%)
  Pallas kernels  27.7 us (12%)
  starting transfers between devices  15.2 us (6%)
  local copies, waits for them, and re-layouts  4.69 us (2%)
    all_to_all x3, blocking collectives, to_chips(): lax.all_to_all(pieces, CHIPS, split_axis=0, concat_axis=0, tiled=True)  135 us
    all_to_all x1, waiting for transfers between devices, to_chips(): lax.all_to_all(pieces, CHIPS, split_axis=0, concat_axis=0, tiled=True)  52.6 us
    pallas_call x6, Pallas kernels, call(): pl.pallas_call(body, out_shape=outs, in_specs=[smem] * scalars + [vmem] *...  27.7 us
    all_to_all x1, starting transfers between devices, to_chips(): lax.all_to_all(pieces, CHIPS, split_axis=0, concat_axis=0, tiled=True)  15 us
  transfers between devices with their start and end apart: 3, of which 3 were waited for; matrix products, arithmetic and copies ran while one was open for 0% of the time, Pallas kernels for 0%

profile of v2, /device:TPU:32, one launch (start us, length us, event | category | flops | bytes accessed | tf_op | source)
XLA Modules:
  0.0 239.9 jit_solution(12039538836111003707)
XLA Ops:
  0.0 1.2 copy-done.1
  1.2 0.9 copy-done.2
  2.2 0.7 copy-done.6
  2.9 6.9 %first_kernel.1 = (bf16[128,2,32,128]{3,2,1,0:T(8,128)(2,1)S(1)}, bf16[32,128,128]{2,1,0:T(8,128)(2,1)S(1)}) custom-call(bf16[128,32,128]{2,1,0:T(8,128)(2,1)S(1)} %copy-done.1, bf16[2,4,128,128]{3,2,1,0:T(8,128)(2,1)S(1)} %copy-done.2, f32[2,128]{1,0:T(2,128)S(1)} %copy-done.6), custom_call_target="tpu_custom_call" | custom-call | tf_op jit(solution)/shard_map/first_kernel/pallas_call | solution.py:188
  9.8 0.0 copy-start
  9.8 1.3 copy-done
  11.1 15.0 %all-to-all-start = ((bf16[128,2,32,128]{3,2,1,0:T(8,128)(2,1)}), bf16[128,2,32,128]{3,2,1,0:T(8,128)(2,1)S(1)}, u32[]{:S(2)}, u32[]{:S(2)}) async-start(bf16[128,2,32,128]{3,2,1,0:T(8,128)(2,1)} %copy-done), calls=%async_computation | async-start | bytes 4194304 | tf_op jit(solution)/shard_map/all_to_all | solution.py:200
  26.1 52.6 %all-to-all-done = bf16[128,2,32,128]{3,2,1,0:T(8,128)(2,1)S(1)} async-done(((bf16[128,2,32,128]{3,2,1,0:T(8,128)(2,1)}), bf16[128,2,32,128]{3,2,1,0:T(8,128)(2,1)S(1)}, u32[]{:S(2)}, u32[]{:S(2)}) %all-to-all-start) | async-done | bytes 2097184 | tf_op jit(solution)/shard_map/all_to_all | solution.py:200
  78.7 1.2 given_kernel.1
  79.9 0.1 collective-permute-start
  80.0 0.7 kept_kernel.1
  80.7 1.9 collective-permute-done
  82.6 0.3 add_convert_fusion
  82.9 0.0 copy-start.3
  83.0 0.0 copy-start.4
  83.0 0.0 copy-start.5
  83.0 0.0 copy-start.7
  83.0 0.0 copy-start.8
  83.0 38.2 %all_to_all.20.returned = bf16[128,32,128]{2,1,0:T(8,128)(2,1)S(1)} all-to-all(bf16[128,32,128]{2,1,0:T(8,128)(2,1)S(1)} %bitcast.13), channel_id=1, replica_groups=mesh['row'=8,'half'=16,'core'=2] {'row','half'}, dimensions={0} | all-to-all | bytes 2097152 | tf_op jit(solution)/shard_map/all_to_all | solution.py:200
  121.2 0.0 copy-done.3
  121.2 0.0 copy-done.4
  121.2 0.0 copy-done.5
  121.2 0.0 copy-done.7
  121.3 9.9 %middle_kernel.1 = (bf16[128,2,32,128]{3,2,1,0:T(8,128)(2,1)S(1)}, bf16[32,128,128]{2,1,0:T(8,128)(2,1)S(1)}) custom-call(bf16[128,32,128]{2,1,0:T(8,128)(2,1)S(1)} %all_to_all.20.returned, bf16[32,128,128]{2,1,0:T(8,128)(2,1)S(1)} %get-tuple-element.14.turned, bf16[2,4,128,128]{3,2,1,0:T(8,128)(2,1)S(1)} %copy-done.3, bf16[2,128,128]{2,1,0:T(8,128)(2,1)S(1)} %copy-done.4, ...), custom_call_target="tpu_custom_call" | custom-call | tf_op jit(solution)/shard_map/middle_kernel/pallas_call | solution.py:188
  131.2 58.3 %all_to_all.21 = bf16[128,2,32,128]{3,2,1,0:T(8,128)(2,1)S(1)} all-to-all(bf16[128,2,32,128]{3,2,1,0:T(8,128)(2,1)S(1)} %get-tuple-element.15), channel_id=1, replica_groups=mesh['row'=8,'half'=16,'core'=2] {'row','half'}, dimensions={0} | all-to-all | bytes 4194304 | tf_op jit(solution)/shard_map/all_to_all | solution.py:200
  189.5 0.4 copy.7
  189.9 0.1 slice_bitcast_fusion
  190.0 0.1 collective-permute-start.1
  190.1 2.6 %collective-permute-done.1.other = bf16[8,16,32,128]{3,2,1,0:T(8,128)(2,1)S(1)} collective-permute-done((bf16[8,16,32,128]{3,2,1,0:T(8,128)(2,1)S(1)}, bf16[8,16,32,128]{3,2,1,0:T(8,128)(2,1)S(1)}, u32[]{:S(2)}, u32[]{:S(2)}) %collective-permute-start.1) | collective-permute-done | bytes 1048608 | tf_op jit(solution)/shard_map/ppermute | solution.py:240
  192.8 1.9 incoming_kernel.1
  194.6 38.2 %all_to_all.22.returned = bf16[128,32,128]{2,1,0:T(8,128)(2,1)S(1)} all-to-all(bf16[128,32,128]{2,1,0:T(8,128)(2,1)S(1)} %bitcast.11), channel_id=1, replica_groups=mesh['row'=8,'half'=16,'core'=2] {'row','half'}, dimensions={0} | all-to-all | bytes 2097152 | tf_op jit(solution)/shard_map/all_to_all | solution.py:200
  232.8 7.1 %last_kernel.1 = bf16[128,32,128]{2,1,0:T(8,128)(2,1)} custom-call(bf16[128,32,128]{2,1,0:T(8,128)(2,1)S(1)} %all_to_all.22.returned, bf16[32,128,128]{2,1,0:T(8,128)(2,1)S(1)} %get-tuple-element.16.turned, bf16[2,128,128]{2,1,0:T(8,128)(2,1)S(1)} %copy-done.4, bf16[2,128,128]{2,1,0:T(8,128)(2,1)S(1)} %copy-done.5, f32[2,128]{1,0:T(2,128)S(1)} %copy-done.7, ...), custom_call_target="tpu_custom_call" | custom-call | tf_op jit(solution)/shard_map/last_kernel/pallas_call | solution.py:188
  (4 shorter events, 0.0 us)
Async XLA Ops:
  0.0 1.2 copy-start.1
  1.2 0.9 copy-start.2
  2.2 0.7 copy-start.6
  9.8 1.3 copy-start
  11.1 67.6 %all-to-all-start = ((bf16[128,2,32,128]{3,2,1,0:T(8,128)(2,1)}), bf16[128,2,32,128]{3,2,1,0:T(8,128)(2,1)S(1)}, u32[]{:S(2)}, u32[]{:S(2)}) async-start(bf16[128,2,32,128]{3,2,1,0:T(8,128)(2,1)} %copy-done), calls=%async_computation | async-start | bytes 4194304 | tf_op jit(solution)/shard_map/all_to_all | solution.py:200
  79.9 2.7 %collective-permute-start = (bf16[8,16,32,128]{3,2,1,0:T(8,128)(2,1)S(1)}, bf16[8,16,32,128]{3,2,1,0:T(8,128)(2,1)S(1)}, u32[]{:S(2)}, u32[]{:S(2)}) collective-permute-start(bf16[8,16,32,128]{3,2,1,0:T(8,128)(2,1)S(1)} %get-tuple-element.13), channel_id=1, source_target_pairs={{0,1},{1,0},{2,3},{3,2},{4,5},{5,4},{6,7},{7,6},{8,9},{9,8},{10,11... | collective-permute-start | bytes 3145736 | tf_op jit(solution)/shard_map/ppermute | solution.py:223
  82.9 38.3 %copy-start.3 = (bf16[2,4,128,128]{3,2,1,0:T(8,128)(2,1)S(1)}, bf16[2,4,128,128]{3,2,1,0:T(8,128)(2,1)}, u32[]{:S(2)}) copy-start(bf16[2,4,128,128]{3,2,1,0:T(8,128)(2,1)} %proj.3) | copy-start | bytes 786436
  83.0 38.3 %copy-start.4 = (bf16[2,128,128]{2,1,0:T(8,128)(2,1)S(1)}, bf16[2,128,128]{2,1,0:T(8,128)(2,1)}, u32[]{:S(2)}) copy-start(bf16[2,128,128]{2,1,0:T(8,128)(2,1)} %gate_w.3) | copy-start | bytes 196612
  83.0 38.3 %copy-start.5 = (bf16[2,128,128]{2,1,0:T(8,128)(2,1)S(1)}, bf16[2,128,128]{2,1,0:T(8,128)(2,1)}, u32[]{:S(2)}) copy-start(bf16[2,128,128]{2,1,0:T(8,128)(2,1)} %out_w.3) | copy-start | bytes 196612
  83.0 38.3 %copy-start.7 = (f32[2,128]{1,0:T(2,128)S(1)}, f32[2,128]{1,0:T(2,128)}, u32[]{:S(2)}) copy-start(f32[2,128]{1,0:T(2,128)} %in_gain.5) | copy-start | bytes 3076
  83.0 38.3 %copy-start.8 = (f32[2,128]{1,0:T(2,128)S(1)}, f32[2,128]{1,0:T(2,128)}, u32[]{:S(2)}) copy-start(f32[2,128]{1,0:T(2,128)} %out_gain.3) | copy-start | bytes 3076
  190.0 2.7 %collective-permute-start.1 = (bf16[8,16,32,128]{3,2,1,0:T(8,128)(2,1)S(1)}, bf16[8,16,32,128]{3,2,1,0:T(8,128)(2,1)S(1)}, u32[]{:S(2)}, u32[]{:S(2)}) collective-permute-start(bf16[8,16,32,128]{3,2,1,0:T(8,128)(2,1)S(1)} %slice_bitcast_fusion), channel_id=1, source_target_pairs={{0,1},{1,0},{2,3},{3,2},{4,5},{5,4},{6,7},{7,6},{8,9},{9,8},{10,11... | collective-permute-start | bytes 3145736 | tf_op jit(solution)/shard_map/ppermute | solution.py:240

commit v3 on v2

--- a/solution.py
+++ b/solution.py
@@ -41,31 +41,48 @@
 
 def spread_rows(source, scratch):
     def step(n, _):
-        for part in range(4):
-            at = n * 4 + part
+        for part in range(8):
+            at = n * 8 + part
             scratch[pl.ds(pl.multiple_of(at * PITCH, 8), 32), :] = source[at].astype(F32)
         return _
 
-    lax.fori_loop(0, 32, step, 0)
-
-
-def project(channels, gain, weights, hands, j):
-    normed = layer_norm(channels, gain).astype(BF16)
-    projected = dot(weights[...], normed)
-    at = pl.ds(pl.multiple_of(j * WIDE, 8), 128)
-    hands[0, at, :] = sigmoid(projected[0:128]) * projected[128:256]
-    hands[1, at, :] = sigmoid(projected[256:384]) * projected[384:512]
+    lax.fori_loop(0, 16, step, 0)
+
+
+def each(steps, body):
+    def step(j, _):
+        body(j)
+        return _
+
+    lax.fori_loop(0, steps, step, 0, unroll=8)
+
+
+def side_by_side(blocks, pair):
+    return jnp.concatenate([blocks[pair * 2], blocks[pair * 2 + 1]], axis=1)
+
+
+def project(normed, weights, hands):
+    def body(pair):
+        both = side_by_side(normed, pair)
+        for side in range(2):
+            projected = dot(weights[side * 256 : (side + 1) * 256, :], both)
+            hand = sigmoid(projected[0:128]) * projected[128:256]
+            for part in range(2):
+                at = pl.ds(pl.multiple_of((pair * 2 + part) * WIDE, 8), 128)
+                hands[side, at, :] = hand[:, part * 128 : (part + 1) * 128]
+
+    each(16, body)
 
 
 def gather_hands(hands, send):
     def step(n, _):
-        for part in range(4):
-            h = n * 4 + part
+        for part in range(8):
+            h = n * 8 + part
             for side in range(2):
                 send[h, side] = hands[side, pl.ds(h, 32, stride=WIDE), :].astype(BF16)
         return _
 
-    lax.fori_loop(0, 32, step, 0)
+    lax.fori_loop(0, 16, step, 0)
 
 
 def set_weights(weights, proj, update_index):
@@ -73,64 +90,84 @@
         weights[p * 128 : (p + 1) * 128, :] = turn(proj[update_index, p])
 
 
-def first_kernel(x, proj, in_gain, send, turned, rows, hands, weights):
+def first_kernel(x, proj, in_gain, send, turned, rows, hands, normed, weights, gains):
     set_weights(weights, proj, 0)
-    gain = column(in_gain[0:1, :])
+    gains[0] = column(in_gain[0:1, :])
     spread_rows(x, rows)
 
-    def step(j, _):
+    def body(j):
         channels = rows[pl.ds(j, 128, stride=PITCH), :].T
         turned[j] = channels.astype(BF16)
-        project(channels, gain, weights, hands, j)
-        return _
-
-    lax.fori_loop(0, 32, step, 0, unroll=2)
+        normed[j] = layer_norm(channels, gains[0]).astype(BF16)
+
+    each(32, body)
+    project(normed, weights, hands)
     gather_hands(hands, send)
 
 
-def new_channels(update_index, tri, turned, gain_in, gain_out, gate, out, j):
-    mixed = layer_norm(tri[pl.ds(j, 128, stride=PITCH), :], gain_out).astype(BF16)
-    change = dot(out, mixed)
-    old = turned[j].astype(F32)
-    normed = layer_norm(old, gain_in).astype(BF16)
-    return old + sigmoid(dot(gate, normed)) * change
-
-
-def middle_kernel(returned, turned, proj, gate_w, out_w, in_gain, out_gain, send, newer, tri, hands, weights):
+def norm_both(tri, turned, mixed, normed, gains):
+    def body(j):
+        mixed[j] = layer_norm(tri[pl.ds(j, 128, stride=PITCH), :], gains[1]).astype(BF16)
+        normed[j] = layer_norm(turned[j].astype(F32), gains[0]).astype(BF16)
+
+    each(32, body)
+
+
+def new_channels(turned, mixed, normed, gate, out, pair):
+    change = dot(out[...], side_by_side(mixed, pair))
+    gating = sigmoid(dot(gate[...], side_by_side(normed, pair)))
+    added = gating * change
+    return [
+        turned[pair * 2 + part].astype(F32) + added[:, part * 128 : (part + 1) * 128]
+        for part in range(2)
+    ]
+
+
+def middle_kernel(
+    returned, turned, proj, gate_w, out_w, in_gain, out_gain, send, newer,
+    tri, hands, mixed, normed, later, weights, gate, out, gains,
+):
     set_weights(weights, proj, 1)
-    gain_in, gain_out, gain_next = column(in_gain[0:1, :]), column(out_gain[0:1, :]), column(in_gain[1:2, :])
-    gate, out = turn(gate_w[0]), turn(out_w[0])
+    gate[...], out[...] = turn(gate_w[0]), turn(out_w[0])
+    gains[0], gains[1], gains[2] = column(in_gain[0:1, :]), column(out_gain[0:1, :]), column(in_gain[1:2, :])
     spread_rows(returned, tri)
-
-    def step(j, _):
-        channels = new_channels(0, tri, turned, gain_in, gain_out, gate, out, j).astype(BF16)
-        newer[j] = channels
-        project(channels.astype(F32), gain_next, weights, hands, j)
-        return _
-
-    lax.fori_loop(0, 32, step, 0, unroll=2)
+    norm_both(tri, turned, mixed, normed, gains)
+
+    def body(pair):
+        for part, channels in enumerate(new_channels(turned, mixed, normed, gate, out, pair)):
+            rounded = channels.astype(BF16)
+            newer[pair * 2 + part] = rounded
+            later[pair * 2 + part] = layer_norm(rounded.astype(F32), gains[2]).astype(BF16)
+
+    each(16, body)
+    project(later, weights, hands)
     gather_hands(hands, send)
 
 
-def last_kernel(returned, turned, gate_w, out_w, in_gain, out_gain, final, tri, rows):
-    gain_in, gain_out = column(in_gain[1:2, :]), column(out_gain[1:2, :])
-    gate, out = turn(gate_w[1]), turn(out_w[1])
+def last_kernel(returned, turned, gate_w, out_w, in_gain, out_gain, final, tri, rows, mixed, normed, newer, gate, out, gains):
+    gate[...], out[...] = turn(gate_w[1]), turn(out_w[1])
+    gains[0], gains[1] = column(in_gain[1:2, :]), column(out_gain[1:2, :])
     spread_rows(returned, tri)
-
-    def step(j, _):
-        channels = new_channels(1, tri, turned, gain_in, gain_out, gate, out, j)
-        rows[pl.ds(j, 128, stride=PITCH), :] = channels.T
-        return _
-
-    lax.fori_loop(0, 32, step, 0, unroll=2)
+    norm_both(tri, turned, mixed, normed, gains)
+
+    def body(pair):
+        for part, channels in enumerate(new_channels(turned, mixed, normed, gate, out, pair)):
+            newer[pair * 2 + part] = channels
+
+    each(16, body)
+
+    def back(j):
+        rows[pl.ds(j, 128, stride=PITCH), :] = newer[j].T
+
+    each(32, back)
 
     def collect(n, _):
-        for part in range(4):
-            at = n * 4 + part
+        for part in range(8):
+            at = n * 8 + part
             final[at] = rows[pl.ds(pl.multiple_of(at * PITCH, 8), 32), :].astype(BF16)
         return _
 
-    lax.fori_loop(0, 32, collect, 0)
+    lax.fori_loop(0, 16, collect, 0)
 
 
 def side_of(operands, r, side):
@@ -201,6 +238,9 @@
 
 
 ROWS = ((128 * PITCH, 128), F32)
+BLOCKS = ((32, 128, 128), BF16)
+SQUARE = ((128, 128), BF16)
+GAINS = ((3, 128, 128), F32)
 HANDS = ((2, 32 * WIDE, 128), F32)
 WEIGHTS = ((512, 128), BF16)
 SEND = shape((128, 2, 32, 128))
@@ -210,7 +250,8 @@
 
 def local(pair_rep, proj_weight, gate_weight, out_weight, in_gain, out_gain):
     core = lax.axis_index("core").astype(jnp.int32).reshape(1)
-    send, turned = call(first_kernel, [SEND, TURNED], [ROWS, HANDS, WEIGHTS], pair_rep, proj_weight, in_gain)
+    core, pair_rep = lax.optimization_barrier((core, pair_rep))
+    send, turned = call(first_kernel, [SEND, TURNED], [ROWS, HANDS, BLOCKS, WEIGHTS, GAINS], pair_rep, proj_weight, in_gain)
     operands = to_chips(send).reshape(8, 16, 2, 32, 128)
     given, kept_rows = call(
         given_kernel,
@@ -227,7 +268,7 @@
     send, turned = call(
         middle_kernel,
         [SEND, TURNED],
-        [ROWS, HANDS, WEIGHTS],
+        [ROWS, HANDS, BLOCKS, BLOCKS, BLOCKS, WEIGHTS, SQUARE, SQUARE, GAINS],
         returned,
         turned,
         proj_weight,
@@ -243,7 +284,7 @@
     (final,) = call(
         last_kernel,
         [shape((128, 32, 128))],
-        [ROWS, ROWS],
+        [ROWS, ROWS, BLOCKS, BLOCKS, ((32, 128, 128), F32), SQUARE, SQUARE, GAINS],
         returned,
         turned,
         gate_weight,

time: 240 us -> 228 us (0.950)
  blocking collectives: 135 us -> 202 us
  waiting for transfers between devices: 57.1 us -> 4.55 us
  starting transfers between devices: 15.2 us -> 0.19 us
  Pallas kernels: 27.7 us -> 17.5 us
    all_to_all x3 -> x4, blocking collectives: 135 us -> 202 us  [to_chips(): lax.all_to_all(pieces, CHIPS, split_axis=0, concat_axis=0, tiled=True)]
    all_to_all x1 -> x0, waiting for transfers between devices: 52.6 us -> none  [to_chips(): lax.all_to_all(pieces, CHIPS, split_axis=0, concat_axis=0, tiled=True)]
    all_to_all x1 -> x0, starting transfers between devices: 15 us -> none  [to_chips(): lax.all_to_all(pieces, CHIPS, split_axis=0, concat_axis=0, tiled=True)]
    pallas_call x6, Pallas kernels: 27.7 us -> 17.5 us  [call(): pl.pallas_call(body, out_shape=outs, in_specs=[smem] * scalars + [vmem] *...]
  transfers between devices with their start and end apart: 3 -> 2, of which waited for: 3 -> 2; matrix products, arithmetic and copies ran while one was open for 0% -> 0% of each run, Pallas kernels for 0% -> 0%
where the time goes in v3:
time: 228 us
  blocking collectives  202 us (89%)
  Pallas kernels  17.5 us (8%)
  waiting for transfers between devices  4.55 us (2%)
  local copies, waits for them, and re-layouts  3.33 us (1%)
    all_to_all x4, blocking collectives, to_chips(): lax.all_to_all(pieces, CHIPS, split_axis=0, concat_axis=0, tiled=True)  202 us
    pallas_call x6, Pallas kernels, call(): pl.pallas_call(body, out_shape=outs, in_specs=[smem] * scalars + [vmem] *...  17.5 us
  transfers between devices with their start and end apart: 2, of which 2 were waited for; matrix products, arithmetic and copies ran while one was open for 0% of the time, Pallas kernels for 0%

profile of v3, /device:TPU:32, one launch (start us, length us, event | category | flops | bytes accessed | tf_op | source)
XLA Modules:
  0.0 228.1 jit_solution(4871200084022624683)
XLA Ops:
  0.0 0.0 copy-start
  0.0 1.2 copy-done
  1.2 0.0 copy-start.1
  1.2 0.9 copy-done.1
  2.2 0.7 copy-done.5
  2.9 3.6 %first_kernel.1 = (bf16[128,2,32,128]{3,2,1,0:T(8,128)(2,1)S(1)}, bf16[32,128,128]{2,1,0:T(8,128)(2,1)S(1)}) custom-call(bf16[128,32,128]{2,1,0:T(8,128)(2,1)S(1)} %copy-done, bf16[2,4,128,128]{3,2,1,0:T(8,128)(2,1)S(1)} %copy-done.1, f32[2,128]{1,0:T(2,128)S(1)} %copy-done.5), custom_call_target="tpu_custom_call" | custom-call | tf_op jit(solution)/shard_map/first_kernel/pallas_call | solution.py:225
  6.5 67.4 %all_to_all.20 = bf16[128,2,32,128]{3,2,1,0:T(8,128)(2,1)S(1)} all-to-all(bf16[128,2,32,128]{3,2,1,0:T(8,128)(2,1)S(1)} %get-tuple-element.15), channel_id=1, replica_groups=mesh['row'=8,'half'=16,'core'=2] {'row','half'}, dimensions={0} | all-to-all | bytes 4194304 | tf_op jit(solution)/shard_map/all_to_all | solution.py:237
  73.8 1.1 given_kernel.1
  75.0 0.1 collective-permute-start
  75.1 0.7 kept_kernel.1
  75.8 1.9 collective-permute-done
  77.7 0.3 add_convert_fusion
  78.0 0.0 copy-start.2
  78.1 0.0 copy-start.3
  78.1 0.0 copy-start.4
  78.1 0.0 copy-start.6
  78.1 0.0 copy-start.7
  78.1 38.2 %all_to_all.21.returned = bf16[128,32,128]{2,1,0:T(8,128)(2,1)S(1)} all-to-all(bf16[128,32,128]{2,1,0:T(8,128)(2,1)S(1)} %bitcast.13), channel_id=1, replica_groups=mesh['row'=8,'half'=16,'core'=2] {'row','half'}, dimensions={0} | all-to-all | bytes 2097152 | tf_op jit(solution)/shard_map/all_to_all | solution.py:237
  116.3 0.0 copy-done.2
  116.3 0.0 copy-done.3
  116.4 0.0 copy-done.4
  116.4 0.0 copy-done.6
  116.4 0.0 copy-done.7
  116.4 5.5 %middle_kernel.1 = (bf16[128,2,32,128]{3,2,1,0:T(8,128)(2,1)S(1)}, bf16[32,128,128]{2,1,0:T(8,128)(2,1)S(1)}) custom-call(bf16[128,32,128]{2,1,0:T(8,128)(2,1)S(1)} %all_to_all.21.returned, bf16[32,128,128]{2,1,0:T(8,128)(2,1)S(1)} %get-tuple-element.18.turned, bf16[2,4,128,128]{3,2,1,0:T(8,128)(2,1)S(1)} %copy-done.2, bf16[2,128,128]{2,1,0:T(8,128)(2,1)S(1)} %copy-done.3, ...), custom_call_target="tpu_custom_call" | custom-call | tf_op jit(solution)/shard_map/middle_kernel/pallas_call | solution.py:225
  121.9 58.3 %all_to_all.22 = bf16[128,2,32,128]{3,2,1,0:T(8,128)(2,1)S(1)} all-to-all(bf16[128,2,32,128]{3,2,1,0:T(8,128)(2,1)S(1)} %get-tuple-element.19), channel_id=1, replica_groups=mesh['row'=8,'half'=16,'core'=2] {'row','half'}, dimensions={0} | all-to-all | bytes 4194304 | tf_op jit(solution)/shard_map/all_to_all | solution.py:237
  180.2 0.4 copy.7
  180.6 0.1 slice_bitcast_fusion
  180.7 0.1 collective-permute-start.1
  180.8 2.6 %collective-permute-done.1.other = bf16[8,16,32,128]{3,2,1,0:T(8,128)(2,1)S(1)} collective-permute-done((bf16[8,16,32,128]{3,2,1,0:T(8,128)(2,1)S(1)}, bf16[8,16,32,128]{3,2,1,0:T(8,128)(2,1)S(1)}, u32[]{:S(2)}, u32[]{:S(2)}) %collective-permute-start.1) | collective-permute-done | bytes 1048608 | tf_op jit(solution)/shard_map/ppermute | solution.py:281
  183.4 1.9 incoming_kernel.1
  185.3 38.2 %all_to_all.23.returned = bf16[128,32,128]{2,1,0:T(8,128)(2,1)S(1)} all-to-all(bf16[128,32,128]{2,1,0:T(8,128)(2,1)S(1)} %bitcast.11), channel_id=1, replica_groups=mesh['row'=8,'half'=16,'core'=2] {'row','half'}, dimensions={0} | all-to-all | bytes 2097152 | tf_op jit(solution)/shard_map/all_to_all | solution.py:237
  223.5 4.6 %last_kernel.1 = bf16[128,32,128]{2,1,0:T(8,128)(2,1)} custom-call(bf16[128,32,128]{2,1,0:T(8,128)(2,1)S(1)} %all_to_all.23.returned, bf16[32,128,128]{2,1,0:T(8,128)(2,1)S(1)} %get-tuple-element.20.turned, bf16[2,128,128]{2,1,0:T(8,128)(2,1)S(1)} %copy-done.3, bf16[2,128,128]{2,1,0:T(8,128)(2,1)S(1)} %copy-done.4, f32[2,128]{1,0:T(2,128)S(1)} %copy-done.6, ...), custom_call_target="tpu_custom_call" | custom-call | tf_op jit(solution)/shard_map/last_kernel/pallas_call | solution.py:225
  (1 shorter events, 0.0 us)
Async XLA Ops:
  0.0 1.2 copy-start
  1.2 0.9 copy-start.1
  2.2 0.7 copy-start.5
  75.0 2.7 %collective-permute-start = (bf16[8,16,32,128]{3,2,1,0:T(8,128)(2,1)S(1)}, bf16[8,16,32,128]{3,2,1,0:T(8,128)(2,1)S(1)}, u32[]{:S(2)}, u32[]{:S(2)}) collective-permute-start(bf16[8,16,32,128]{3,2,1,0:T(8,128)(2,1)S(1)} %get-tuple-element.17), channel_id=1, source_target_pairs={{0,1},{1,0},{2,3},{3,2},{4,5},{5,4},{6,7},{7,6},{8,9},{9,8},{10,11... | collective-permute-start | bytes 3145736 | tf_op jit(solution)/shard_map/ppermute | solution.py:264
  78.0 38.3 %copy-start.2 = (bf16[2,4,128,128]{3,2,1,0:T(8,128)(2,1)S(1)}, bf16[2,4,128,128]{3,2,1,0:T(8,128)(2,1)}, u32[]{:S(2)}) copy-start(bf16[2,4,128,128]{3,2,1,0:T(8,128)(2,1)} %proj.3) | copy-start | bytes 786436
  78.1 38.3 %copy-start.3 = (bf16[2,128,128]{2,1,0:T(8,128)(2,1)S(1)}, bf16[2,128,128]{2,1,0:T(8,128)(2,1)}, u32[]{:S(2)}) copy-start(bf16[2,128,128]{2,1,0:T(8,128)(2,1)} %gate_w.3) | copy-start | bytes 196612
  78.1 38.3 %copy-start.4 = (bf16[2,128,128]{2,1,0:T(8,128)(2,1)S(1)}, bf16[2,128,128]{2,1,0:T(8,128)(2,1)}, u32[]{:S(2)}) copy-start(bf16[2,128,128]{2,1,0:T(8,128)(2,1)} %out_w.3) | copy-start | bytes 196612
  78.1 38.3 %copy-start.6 = (f32[2,128]{1,0:T(2,128)S(1)}, f32[2,128]{1,0:T(2,128)}, u32[]{:S(2)}) copy-start(f32[2,128]{1,0:T(2,128)} %in_gain.5) | copy-start | bytes 3076
  78.1 38.3 %copy-start.7 = (f32[2,128]{1,0:T(2,128)S(1)}, f32[2,128]{1,0:T(2,128)}, u32[]{:S(2)}) copy-start(f32[2,128]{1,0:T(2,128)} %out_gain.3) | copy-start | bytes 3076
  180.7 2.7 %collective-permute-start.1 = (bf16[8,16,32,128]{3,2,1,0:T(8,128)(2,1)S(1)}, bf16[8,16,32,128]{3,2,1,0:T(8,128)(2,1)S(1)}, u32[]{:S(2)}, u32[]{:S(2)}) collective-permute-start(bf16[8,16,32,128]{3,2,1,0:T(8,128)(2,1)S(1)} %slice_bitcast_fusion), channel_id=1, source_target_pairs={{0,1},{1,0},{2,3},{3,2},{4,5},{5,4},{6,7},{7,6},{8,9},{9,8},{10,11... | collective-permute-start | bytes 3145736 | tf_op jit(solution)/shard_map/ppermute | solution.py:281

commit v4 on v3

--- a/solution.py
+++ b/solution.py
@@ -1,3 +1,5 @@
+import functools
+
 import jax
 import jax.numpy as jnp
 from jax import lax
@@ -39,14 +41,14 @@
     return matrix.astype(F32).T.astype(BF16)
 
 
-def spread_rows(source, scratch):
+def spread_rows(source, scratch, start, groups):
     def step(n, _):
         for part in range(8):
-            at = n * 8 + part
+            at = start + n * 8 + part
             scratch[pl.ds(pl.multiple_of(at * PITCH, 8), 32), :] = source[at].astype(F32)
         return _
 
-    lax.fori_loop(0, 16, step, 0)
+    lax.fori_loop(0, groups // 8, step, 0)
 
 
 def each(steps, body):
@@ -85,73 +87,110 @@
     lax.fori_loop(0, 16, step, 0)
 
 
-def set_weights(weights, proj, update_index):
+def fetch(pairs, arrived):
+    copies = [pltpu.make_async_copy(far, near, arrived.at[n]) for n, (far, near) in enumerate(pairs)]
+    for copy in copies:
+        copy.start()
+    return copies
+
+
+def first_kernel(x, proj, in_gain, send, turned, x_near, proj_near, gain_near, rows, hands, normed, weights, gains, arrived):
+    quarters = [pl.ds(n * 32, 32) for n in range(4)]
+    pairs = [(x.at[part], x_near.at[part]) for part in quarters]
+    pieces = fetch([*pairs, (proj.at[0], proj_near), (in_gain, gain_near)], arrived)
+    for n in range(4):
+        pieces[n].wait()
+        spread_rows(x_near, rows, n * 32, 32)
+    pieces[4].wait()
+    pieces[5].wait()
     for p in range(4):
-        weights[p * 128 : (p + 1) * 128, :] = turn(proj[update_index, p])
-
-
-def first_kernel(x, proj, in_gain, send, turned, rows, hands, normed, weights, gains):
-    set_weights(weights, proj, 0)
-    gains[0] = column(in_gain[0:1, :])
-    spread_rows(x, rows)
+        weights[p * 128 : (p + 1) * 128, :] = turn(proj_near[p])
+    gains[...] = column(gain_near[0:1, :])
 
     def body(j):
         channels = rows[pl.ds(j, 128, stride=PITCH), :].T
         turned[j] = channels.astype(BF16)
-        normed[j] = layer_norm(channels, gains[0]).astype(BF16)
+        normed[j] = layer_norm(channels, gains[...]).astype(BF16)
 
     each(32, body)
     project(normed, weights, hands)
     gather_hands(hands, send)
 
 
-def norm_both(tri, turned, mixed, normed, gains):
+def side_kernel(update_index, turned, proj, gate_w, out_w, in_gain, out_gain, gating, out, gains, weights, normed, gate):
+    gate[...], out[...] = turn(gate_w[update_index]), turn(out_w[update_index])
+    gains[0] = column(out_gain[update_index : update_index + 1, :])
+    gains[1] = column(in_gain[1:2, :])
+    gains[2] = column(in_gain[update_index : update_index + 1, :])
+    for p in range(4):
+        weights[p * 128 : (p + 1) * 128, :] = turn(proj[1, p])
+
+    def norm(j):
+        normed[j] = layer_norm(turned[j].astype(F32), gains[2]).astype(BF16)
+
+    each(32, norm)
+
+    def body(pair):
+        both = sigmoid(dot(gate[...], side_by_side(normed, pair)))
+        for part in range(2):
+            gating[pair * 2 + part] = both[:, part * 128 : (part + 1) * 128]
+
+    each(16, body)
+
+
+def mix(tri, mixed, gains):
     def body(j):
-        mixed[j] = layer_norm(tri[pl.ds(j, 128, stride=PITCH), :], gains[1]).astype(BF16)
-        normed[j] = layer_norm(turned[j].astype(F32), gains[0]).astype(BF16)
+        mixed[j] = layer_norm(tri[pl.ds(j, 128, stride=PITCH), :], gains[0]).astype(BF16)
 
     each(32, body)
 
 
-def new_channels(turned, mixed, normed, gate, out, pair):
+def new_channels(turned, gating, mixed, out, pair):
     change = dot(out[...], side_by_side(mixed, pair))
-    gating = sigmoid(dot(gate[...], side_by_side(normed, pair)))
-    added = gating * change
     return [
-        turned[pair * 2 + part].astype(F32) + added[:, part * 128 : (part + 1) * 128]
+        turned[pair * 2 + part].astype(F32) + gating[pair * 2 + part] * change[:, part * 128 : (part + 1) * 128]
         for part in range(2)
     ]
 
 
 def middle_kernel(
-    returned, turned, proj, gate_w, out_w, in_gain, out_gain, send, newer,
-    tri, hands, mixed, normed, later, weights, gate, out, gains,
+    far_gains, far_out, far_gating, far_turned, far_weights, returned, send, newer,
+    gains, out, gating, turned, weights, tri, hands, mixed, later, arrived,
 ):
-    set_weights(weights, proj, 1)
-    gate[...], out[...] = turn(gate_w[0]), turn(out_w[0])
-    gains[0], gains[1], gains[2] = column(in_gain[0:1, :]), column(out_gain[0:1, :]), column(in_gain[1:2, :])
-    spread_rows(returned, tri)
-    norm_both(tri, turned, mixed, normed, gains)
+    pieces = fetch(
+        [(far_gains, gains), (far_out, out), (far_gating, gating), (far_turned, turned), (far_weights, weights)],
+        arrived,
+    )
+    spread_rows(returned, tri, 0, 128)
+    pieces[0].wait()
+    mix(tri, mixed, gains)
+    for piece in pieces[1:]:
+        piece.wait()
 
     def body(pair):
-        for part, channels in enumerate(new_channels(turned, mixed, normed, gate, out, pair)):
+        for part, channels in enumerate(new_channels(turned, gating, mixed, out, pair)):
             rounded = channels.astype(BF16)
             newer[pair * 2 + part] = rounded
-            later[pair * 2 + part] = layer_norm(rounded.astype(F32), gains[2]).astype(BF16)
+            later[pair * 2 + part] = layer_norm(rounded.astype(F32), gains[1]).astype(BF16)
 
     each(16, body)
     project(later, weights, hands)
     gather_hands(hands, send)
 
 
-def last_kernel(returned, turned, gate_w, out_w, in_gain, out_gain, final, tri, rows, mixed, normed, newer, gate, out, gains):
-    gate[...], out[...] = turn(gate_w[1]), turn(out_w[1])
-    gains[0], gains[1] = column(in_gain[1:2, :]), column(out_gain[1:2, :])
-    spread_rows(returned, tri)
-    norm_both(tri, turned, mixed, normed, gains)
+def last_kernel(
+    far_gains, far_out, far_gating, far_turned, returned, final,
+    gains, out, gating, turned, tri, rows, mixed, newer, near, arrived, left,
+):
+    pieces = fetch([(far_gains, gains), (far_out, out), (far_gating, gating), (far_turned, turned)], arrived)
+    spread_rows(returned, tri, 0, 128)
+    pieces[0].wait()
+    mix(tri, mixed, gains)
+    for piece in pieces[1:]:
+        piece.wait()
 
     def body(pair):
-        for part, channels in enumerate(new_channels(turned, mixed, normed, gate, out, pair)):
+        for part, channels in enumerate(new_channels(turned, gating, mixed, out, pair)):
             newer[pair * 2 + part] = channels
 
     each(16, body)
@@ -160,14 +199,20 @@
         rows[pl.ds(j, 128, stride=PITCH), :] = newer[j].T
 
     each(32, back)
-
-    def collect(n, _):
-        for part in range(8):
-            at = n * 8 + part
-            final[at] = rows[pl.ds(pl.multiple_of(at * PITCH, 8), 32), :].astype(BF16)
-        return _
-
-    lax.fori_loop(0, 16, collect, 0)
+    pieces = []
+    for n in range(4):
+
+        def collect(m, _):
+            for part in range(8):
+                at = n * 32 + m * 8 + part
+                near[at] = rows[pl.ds(pl.multiple_of(at * PITCH, 8), 32), :].astype(BF16)
+            return _
+
+        lax.fori_loop(0, 4, collect, 0)
+        pieces.append(pltpu.make_async_copy(near.at[pl.ds(n * 32, 32)], final.at[pl.ds(n * 32, 32)], left.at[n]))
+        pieces[n].start()
+    for piece in pieces:
+        piece.wait()
 
 
 def side_of(operands, r, side):
@@ -219,17 +264,22 @@
     return jax.ShapeDtypeStruct(dims, kind)
 
 
-def call(body, outs, scratch, *args, scalars=0):
-    vmem = pl.BlockSpec(memory_space=pltpu.VMEM)
-    smem = pl.BlockSpec(memory_space=pltpu.SMEM)
+def call(body, outs, scratch, *args, scalars=0, far=0, far_out=False, name=None):
+    args = [
+        pltpu.with_memory_space_constraint(arg, pltpu.HBM) if scalars <= n < scalars + far else arg
+        for n, arg in enumerate(args)
+    ]
+    vmem, smem, hbm = (pl.BlockSpec(memory_space=space) for space in (pltpu.VMEM, pltpu.SMEM, pltpu.HBM))
     return pl.pallas_call(
         body,
         out_shape=outs,
-        in_specs=[smem] * scalars + [vmem] * (len(args) - scalars),
-        out_specs=[vmem] * len(outs),
-        scratch_shapes=[pltpu.VMEM(dims, kind) for dims, kind in scratch],
-        compiler_params=pltpu.CompilerParams(vmem_limit_bytes=48 * 1024 * 1024),
-        name=body.__name__,
+        in_specs=[smem] * scalars + [hbm] * far + [vmem] * (len(args) - scalars - far),
+        out_specs=[hbm if far_out else vmem] * len(outs),
+        scratch_shapes=[
+            dims if kind is None else pltpu.VMEM(dims, kind) for dims, kind in scratch
+        ],
+        compiler_params=pltpu.CompilerParams(vmem_limit_bytes=20 * 1024 * 1024),
+        name=name or body.__name__,
     )(*args)
 
 
@@ -239,20 +289,52 @@
 
 ROWS = ((128 * PITCH, 128), F32)
 BLOCKS = ((32, 128, 128), BF16)
+WHOLE = ((128, 32, 128), BF16)
 SQUARE = ((128, 128), BF16)
 GAINS = ((3, 128, 128), F32)
 HANDS = ((2, 32 * WIDE, 128), F32)
 WEIGHTS = ((512, 128), BF16)
 SEND = shape((128, 2, 32, 128))
-TURNED = shape((32, 128, 128))
+TURNED = shape(*BLOCKS)
 HALF = (8, 16, 32, 128)
+
+
+def first(pair_rep, proj_weight, in_gain):
+    near = [WHOLE, ((4, 128, 128), BF16), ((2, 128), F32)]
+    scratch = [*near, ROWS, HANDS, BLOCKS, WEIGHTS, ((128, 128), F32), (pltpu.SemaphoreType.DMA((6,)), None)]
+    return call(first_kernel, [SEND, TURNED], scratch, pair_rep, proj_weight, in_gain, far=3)
+
+
+def side(update_index, *args):
+    outs = [shape(BLOCKS[0], F32), shape(*SQUARE), shape(*GAINS), shape(*WEIGHTS)]
+    body = functools.partial(side_kernel, update_index)
+    return call(body, outs, [BLOCKS, SQUARE], *args, name="side_kernel")
+
+
+NEAR = [GAINS, SQUARE, (BLOCKS[0], F32), BLOCKS]
+
+
+def copies(number):
+    return (pltpu.SemaphoreType.DMA((number,)), None)
+
+
+def middle(returned, turned, gating, out, gains, weights):
+    scratch = [*NEAR, WEIGHTS, ROWS, HANDS, BLOCKS, BLOCKS, copies(5)]
+    return call(middle_kernel, [SEND, TURNED], scratch, gains, out, gating, turned, weights, returned, far=5)
+
+
+def last(returned, turned, gating, out, gains):
+    scratch = [*NEAR, ROWS, ROWS, BLOCKS, (BLOCKS[0], F32), WHOLE, copies(4), copies(4)]
+    return call(last_kernel, [shape(*WHOLE)], scratch, gains, out, gating, turned, returned, far=4, far_out=True)[0]
 
 
 def local(pair_rep, proj_weight, gate_weight, out_weight, in_gain, out_gain):
     core = lax.axis_index("core").astype(jnp.int32).reshape(1)
     core, pair_rep = lax.optimization_barrier((core, pair_rep))
-    send, turned = call(first_kernel, [SEND, TURNED], [ROWS, HANDS, BLOCKS, WEIGHTS, GAINS], pair_rep, proj_weight, in_gain)
+    parameters = (proj_weight, gate_weight, out_weight, in_gain, out_gain)
+    send, turned = first(pair_rep, proj_weight, in_gain)
     operands = to_chips(send).reshape(8, 16, 2, 32, 128)
+    gating, out, gains, weights = side(0, turned, *parameters)
     given, kept_rows = call(
         given_kernel,
         [shape(HALF), shape((512, 512))],
@@ -265,34 +347,13 @@
     (kept,) = call(kept_kernel, [shape(HALF, F32)], [], kept_rows, operands)
     triangle = (kept + taken.astype(F32)).astype(BF16)
     returned = to_chips(triangle.reshape(128, 32, 128))
-    send, turned = call(
-        middle_kernel,
-        [SEND, TURNED],
-        [ROWS, HANDS, BLOCKS, BLOCKS, BLOCKS, WEIGHTS, SQUARE, SQUARE, GAINS],
-        returned,
-        turned,
-        proj_weight,
-        gate_weight,
-        out_weight,
-        in_gain,
-        out_gain,
-    )
+    send, turned = middle(returned, turned, gating, out, gains, weights)
     operands = to_chips(send).reshape(8, 16, 2, 32, 128)
+    gating, out, gains, _ = side(1, turned, *parameters)
     other = lax.ppermute(operands[:, :, 0], "core", SWAP)
     (triangle,) = call(incoming_kernel, [shape(HALF)], [((1024, 1024), BF16)], core, operands, other, scalars=1)
     returned = to_chips(triangle.reshape(128, 32, 128))
-    (final,) = call(
-        last_kernel,
-        [shape((128, 32, 128))],
-        [ROWS, ROWS, BLOCKS, BLOCKS, ((32, 128, 128), F32), SQUARE, SQUARE, GAINS],
-        returned,
-        turned,
-        gate_weight,
-        out_weight,
-        in_gain,
-        out_gain,
-    )
-    return final
+    return last(returned, turned, gating, out, gains)
 
 
 def solution(mesh):

time: 228 us -> 229 us (level)
  blocking collectives: 202 us -> 126 us
  waiting for transfers between devices: 4.55 us -> 57.1 us
  starting transfers between devices: 0.19 us -> 14.9 us
  Pallas kernels: 17.5 us -> 22.8 us
  local copies, waits for them, and re-layouts: 3.33 us -> 6.38 us
    all_to_all x4 -> x2, blocking collectives: 202 us -> 126 us  [to_chips(): lax.all_to_all(pieces, CHIPS, split_axis=0, concat_axis=0, tiled=True)]
    all_to_all x0 -> x2, waiting for transfers between devices: none -> 52.6 us  [to_chips(): lax.all_to_all(pieces, CHIPS, split_axis=0, concat_axis=0, tiled=True)]
    all_to_all x0 -> x2, starting transfers between devices: none -> 14.7 us  [to_chips(): lax.all_to_all(pieces, CHIPS, split_axis=0, concat_axis=0, tiled=True)]
    pallas_call x6 -> x8, Pallas kernels: 17.5 us -> 22.8 us  [call(): pl.pallas_call(body, out_shape=outs, in_specs=[smem] * scalars + [hbm] *...]
    unnamed x16 -> x28, local copies, waits for them, and re-layouts: 2.88 us -> 5.92 us
  transfers between devices with their start and end apart: 2 -> 4, of which waited for: 2 -> 4; matrix products, arithmetic and copies ran while one was open for 0% -> 0% of each run, Pallas kernels for 0% -> 2%
where the time goes in v4:
time: 229 us
  blocking collectives  126 us (55%)
  waiting for transfers between devices  57.1 us (25%)
  Pallas kernels  22.8 us (10%)
  starting transfers between devices  14.9 us (7%)
  local copies, waits for them, and re-layouts  6.38 us (3%)
    all_to_all x2, blocking collectives, to_chips(): lax.all_to_all(pieces, CHIPS, split_axis=0, concat_axis=0, tiled=True)  126 us
    all_to_all x2, waiting for transfers between devices, to_chips(): lax.all_to_all(pieces, CHIPS, split_axis=0, concat_axis=0, tiled=True)  52.6 us
    pallas_call x8, Pallas kernels, call(): pl.pallas_call(body, out_shape=outs, in_specs=[smem] * scalars + [hbm] *...  22.8 us
    all_to_all x2, starting transfers between devices, to_chips(): lax.all_to_all(pieces, CHIPS, split_axis=0, concat_axis=0, tiled=True)  14.7 us
    unnamed x28, local copies, waits for them, and re-layouts  5.92 us
  transfers between devices with their start and end apart: 4, of which 4 were waited for; matrix products, arithmetic and copies ran while one was open for 0% of the time, Pallas kernels for 2%

profile of v4, /device:TPU:32, one launch (start us, length us, event | category | flops | bytes accessed | tf_op | source)
XLA Modules:
  0.0 228.6 jit_solution(8833408640950312897)
XLA Ops:
  0.0 4.7 %first_kernel.1 = (bf16[128,2,32,128]{3,2,1,0:T(8,128)(2,1)S(1)}, bf16[32,128,128]{2,1,0:T(8,128)(2,1)S(1)}) custom-call(bf16[128,32,128]{2,1,0:T(8,128)(2,1)} %x, bf16[2,4,128,128]{3,2,1,0:T(8,128)(2,1)} %proj.5, f32[2,128]{1,0:T(2,128)} %in_gain.5), custom_call_target="tpu_custom_call" | custom-call | tf_op jit(solution)/shard_map/first_kernel/pallas_call | solution.py:273
  4.7 0.0 copy-start
  4.7 67.4 %all_to_all.20 = bf16[128,2,32,128]{3,2,1,0:T(8,128)(2,1)S(1)} all-to-all(bf16[128,2,32,128]{3,2,1,0:T(8,128)(2,1)S(1)} %get-tuple-element.27), channel_id=1, replica_groups=mesh['row'=8,'half'=16,'core'=2] {'row','half'}, dimensions={0} | all-to-all | bytes 4194304 | tf_op jit(solution)/shard_map/all_to_all | solution.py:287
  72.1 1.1 given_kernel.1
  73.3 0.1 collective-permute-start
  73.4 0.7 kept_kernel.1
  74.1 1.9 collective-permute-done
  76.0 1.3 add_convert_fusion
  77.3 0.0 copy-start.13
  77.3 7.4 %all-to-all-start.1 = ((bf16[128,32,128]{2,1,0:T(8,128)(2,1)}), bf16[128,32,128]{2,1,0:T(8,128)(2,1)S(1)}, u32[]{:S(2)}, u32[]{:S(2)}) async-start(bf16[128,32,128]{2,1,0:T(8,128)(2,1)} %bitcast.2), calls=%async_computation.1 | async-start | bytes 2097152 | tf_op jit(solution)/shard_map/all_to_all | solution.py:287
  84.8 0.0 copy-done
  84.8 1.6 side_kernel.2
  86.4 0.0 copy-start.3
  86.4 1.3 copy-done.3
  87.7 0.7 copy-done.7
  88.4 0.7 copy-done.9
  89.1 0.6 copy-done.10
  89.7 26.1 %all-to-all-done.1.returned = bf16[128,32,128]{2,1,0:T(8,128)(2,1)S(1)} async-done(((bf16[128,32,128]{2,1,0:T(8,128)(2,1)}), bf16[128,32,128]{2,1,0:T(8,128)(2,1)S(1)}, u32[]{:S(2)}, u32[]{:S(2)}) %all-to-all-start.1) | async-done | bytes 1048608 | tf_op jit(solution)/shard_map/all_to_all | solution.py:287
  115.8 5.4 %middle_kernel.1 = (bf16[128,2,32,128]{3,2,1,0:T(8,128)(2,1)S(1)}, bf16[32,128,128]{2,1,0:T(8,128)(2,1)S(1)}) custom-call(f32[3,128,128]{2,1,0:T(8,128)} %copy-done.7, bf16[128,128]{1,0:T(8,128)(2,1)} %copy-done.10, f32[32,128,128]{2,1,0:T(8,128)} %copy-done.3, bf16[32,128,128]{2,1,0:T(8,128)(2,1)} %copy-done, bf16[512,128]{1,0:T(8,128)(2,1)} %copy-done.9, ...), custom_call_target="tpu_custom_call" | custom-call | tf_op jit(solution)/shard_map/middle_kernel/pallas_call | solution.py:273
  121.2 58.3 %all_to_all.21 = bf16[128,2,32,128]{3,2,1,0:T(8,128)(2,1)S(1)} all-to-all(bf16[128,2,32,128]{3,2,1,0:T(8,128)(2,1)S(1)} %get-tuple-element.34), channel_id=1, replica_groups=mesh['row'=8,'half'=16,'core'=2] {'row','half'}, dimensions={0} | all-to-all | bytes 4194304 | tf_op jit(solution)/shard_map/all_to_all | solution.py:287
  179.5 0.4 copy.7
  179.9 0.1 slice_bitcast_fusion
  180.0 0.1 collective-permute-start.1
  180.1 2.6 %collective-permute-done.1.other = bf16[8,16,32,128]{3,2,1,0:T(8,128)(2,1)S(1)} collective-permute-done((bf16[8,16,32,128]{3,2,1,0:T(8,128)(2,1)S(1)}, bf16[8,16,32,128]{3,2,1,0:T(8,128)(2,1)S(1)}, u32[]{:S(2)}, u32[]{:S(2)}) %collective-permute-start.1) | collective-permute-done | bytes 1048608 | tf_op jit(solution)/shard_map/ppermute | solution.py:353
  182.7 2.8 %incoming_kernel.1 = bf16[8,16,32,128]{3,2,1,0:T(8,128)(2,1)} custom-call(s32[1]{0:T(128)} %bitcast.core, bf16[8,16,2,32,128]{4,3,2,1,0:T(8,128)(2,1)S(1)} %bitcast.8, bf16[8,16,32,128]{3,2,1,0:T(8,128)(2,1)S(1)} %collective-permute-done.1.other), custom_call_target="tpu_custom_call" | custom-call | tf_op jit(solution)/shard_map/incoming_kernel/pallas_call | solution.py:273
  185.6 7.3 %all-to-all-start.3 = ((bf16[128,32,128]{2,1,0:T(8,128)(2,1)}), bf16[128,32,128]{2,1,0:T(8,128)(2,1)S(1)}, u32[]{:S(2)}, u32[]{:S(2)}) async-start(bf16[128,32,128]{2,1,0:T(8,128)(2,1)} %bitcast.6), calls=%async_computation.3 | async-start | bytes 2097152 | tf_op jit(solution)/shard_map/all_to_all | solution.py:287
  192.9 1.9 side_kernel.3
  194.9 1.3 copy-done.4
  196.2 0.7 copy-done.8
  196.9 0.6 copy-done.11
  197.5 26.5 %all-to-all-done.3.returned = bf16[128,32,128]{2,1,0:T(8,128)(2,1)S(1)} async-done(((bf16[128,32,128]{2,1,0:T(8,128)(2,1)}), bf16[128,32,128]{2,1,0:T(8,128)(2,1)S(1)}, u32[]{:S(2)}, u32[]{:S(2)}) %all-to-all-start.3) | async-done | bytes 1048608 | tf_op jit(solution)/shard_map/all_to_all | solution.py:287
  224.0 4.4 %last_kernel.1 = bf16[128,32,128]{2,1,0:T(8,128)(2,1)} custom-call(f32[3,128,128]{2,1,0:T(8,128)} %copy-done.8, bf16[128,128]{1,0:T(8,128)(2,1)} %copy-done.11, f32[32,128,128]{2,1,0:T(8,128)} %copy-done.4, bf16[32,128,128]{2,1,0:T(8,128)(2,1)} %copy-done.1, bf16[128,32,128]{2,1,0:T(8,128)(2,1)S(1)} %all-to-all-done.3.returned), custom_call_target="tpu_custom_call" | custom-call | tf_op jit(solution)/shard_map/last_kernel/pallas_call | solution.py:273
  (17 shorter events, 0.0 us)
Async XLA Ops:
  4.7 80.0 %copy-start = (bf16[32,128,128]{2,1,0:T(8,128)(2,1)}, bf16[32,128,128]{2,1,0:T(8,128)(2,1)S(1)}, u32[]{:S(2)}) copy-start(bf16[32,128,128]{2,1,0:T(8,128)(2,1)S(1)} %get-tuple-element.21.turned.far_turned) | copy-start | bytes 3145732
  73.3 2.7 %collective-permute-start = (bf16[8,16,32,128]{3,2,1,0:T(8,128)(2,1)S(1)}, bf16[8,16,32,128]{3,2,1,0:T(8,128)(2,1)S(1)}, u32[]{:S(2)}, u32[]{:S(2)}) collective-permute-start(bf16[8,16,32,128]{3,2,1,0:T(8,128)(2,1)S(1)} %get-tuple-element.29), channel_id=1, source_target_pairs={{0,1},{1,0},{2,3},{3,2},{4,5},{5,4},{6,7},{7,6},{8,9},{9,8},{10,11... | collective-permute-start | bytes 3145736 | tf_op jit(solution)/shard_map/ppermute | solution.py:346
  77.3 7.4 %copy-start.2 = (bf16[2,4,128,128]{3,2,1,0:T(8,128)(2,1)S(1)}, bf16[2,4,128,128]{3,2,1,0:T(8,128)(2,1)}, u32[]{:S(2)}) copy-start(bf16[2,4,128,128]{3,2,1,0:T(8,128)(2,1)} %proj.5) | copy-start | bytes 786436
  77.3 7.5 %copy-start.5 = (bf16[2,128,128]{2,1,0:T(8,128)(2,1)S(1)}, bf16[2,128,128]{2,1,0:T(8,128)(2,1)}, u32[]{:S(2)}) copy-start(bf16[2,128,128]{2,1,0:T(8,128)(2,1)} %gate_w.3) | copy-start | bytes 196612
  77.3 7.5 %copy-start.6 = (bf16[2,128,128]{2,1,0:T(8,128)(2,1)S(1)}, bf16[2,128,128]{2,1,0:T(8,128)(2,1)}, u32[]{:S(2)}) copy-start(bf16[2,128,128]{2,1,0:T(8,128)(2,1)} %out_w.3) | copy-start | bytes 196612
  77.3 7.5 %copy-start.12 = (f32[2,128]{1,0:T(2,128)S(1)}, f32[2,128]{1,0:T(2,128)}, u32[]{:S(2)}) copy-start(f32[2,128]{1,0:T(2,128)} %in_gain.5) | copy-start | bytes 3076
  77.3 7.5 %copy-start.13 = (f32[2,128]{1,0:T(2,128)S(1)}, f32[2,128]{1,0:T(2,128)}, u32[]{:S(2)}) copy-start(f32[2,128]{1,0:T(2,128)} %out_gain.3) | copy-start | bytes 3076
  77.3 38.4 %all-to-all-start.1 = ((bf16[128,32,128]{2,1,0:T(8,128)(2,1)}), bf16[128,32,128]{2,1,0:T(8,128)(2,1)S(1)}, u32[]{:S(2)}, u32[]{:S(2)}) async-start(bf16[128,32,128]{2,1,0:T(8,128)(2,1)} %bitcast.2), calls=%async_computation.1 | async-start | bytes 2097152 | tf_op jit(solution)/shard_map/all_to_all | solution.py:287
  86.4 1.3 copy-start.3
  87.7 0.7 copy-start.7
  88.4 0.7 copy-start.9
  89.1 0.6 copy-start.10
  121.2 71.7 %copy-start.1 = (bf16[32,128,128]{2,1,0:T(8,128)(2,1)}, bf16[32,128,128]{2,1,0:T(8,128)(2,1)S(1)}, u32[]{:S(2)}) copy-start(bf16[32,128,128]{2,1,0:T(8,128)(2,1)S(1)} %get-tuple-element.30.turned.far_turned) | copy-start | bytes 3145732
  180.0 2.7 %collective-permute-start.1 = (bf16[8,16,32,128]{3,2,1,0:T(8,128)(2,1)S(1)}, bf16[8,16,32,128]{3,2,1,0:T(8,128)(2,1)S(1)}, u32[]{:S(2)}, u32[]{:S(2)}) collective-permute-start(bf16[8,16,32,128]{3,2,1,0:T(8,128)(2,1)S(1)} %slice_bitcast_fusion), channel_id=1, source_target_pairs={{0,1},{1,0},{2,3},{3,2},{4,5},{5,4},{6,7},{7,6},{8,9},{9,8},{10,11... | collective-permute-start | bytes 3145736 | tf_op jit(solution)/shard_map/ppermute | solution.py:353
  185.6 38.4 %all-to-all-start.3 = ((bf16[128,32,128]{2,1,0:T(8,128)(2,1)}), bf16[128,32,128]{2,1,0:T(8,128)(2,1)S(1)}, u32[]{:S(2)}, u32[]{:S(2)}) async-start(bf16[128,32,128]{2,1,0:T(8,128)(2,1)} %bitcast.6), calls=%async_computation.3 | async-start | bytes 2097152 | tf_op jit(solution)/shard_map/all_to_all | solution.py:287
  194.9 1.3 copy-start.4
  196.2 0.7 copy-start.8
  196.9 0.6 copy-start.11

commit v5 on v4

--- a/solution.py
+++ b/solution.py
@@ -7,6 +7,7 @@
 from jax.experimental.pallas import tpu as pltpu
 from jax.sharding import Mesh
 from jax.sharding import PartitionSpec as P
+
 
 CHIPS = ("row", "half")
 SWAP = [(0, 1), (1, 0)]
@@ -153,19 +154,9 @@
     ]
 
 
-def middle_kernel(
-    far_gains, far_out, far_gating, far_turned, far_weights, returned, send, newer,
-    gains, out, gating, turned, weights, tri, hands, mixed, later, arrived,
-):
-    pieces = fetch(
-        [(far_gains, gains), (far_out, out), (far_gating, gating), (far_turned, turned), (far_weights, weights)],
-        arrived,
-    )
+def middle_kernel(returned, turned, gating, out, gains, weights, send, newer, tri, hands, mixed, later):
     spread_rows(returned, tri, 0, 128)
-    pieces[0].wait()
     mix(tri, mixed, gains)
-    for piece in pieces[1:]:
-        piece.wait()
 
     def body(pair):
         for part, channels in enumerate(new_channels(turned, gating, mixed, out, pair)):
@@ -178,16 +169,9 @@
     gather_hands(hands, send)
 
 
-def last_kernel(
-    far_gains, far_out, far_gating, far_turned, returned, final,
-    gains, out, gating, turned, tri, rows, mixed, newer, near, arrived, left,
-):
-    pieces = fetch([(far_gains, gains), (far_out, out), (far_gating, gating), (far_turned, turned)], arrived)
+def last_kernel(returned, turned, gating, out, gains, final, tri, rows, mixed, newer, near, left):
     spread_rows(returned, tri, 0, 128)
-    pieces[0].wait()
     mix(tri, mixed, gains)
-    for piece in pieces[1:]:
-        piece.wait()
 
     def body(pair):
         for part, channels in enumerate(new_channels(turned, gating, mixed, out, pair)):
@@ -264,7 +248,7 @@
     return jax.ShapeDtypeStruct(dims, kind)
 
 
-def call(body, outs, scratch, *args, scalars=0, far=0, far_out=False, name=None):
+def call(body, outs, scratch, *args, scalars=0, far=0, far_out=False):
     args = [
         pltpu.with_memory_space_constraint(arg, pltpu.HBM) if scalars <= n < scalars + far else arg
         for n, arg in enumerate(args)
@@ -279,7 +263,6 @@
             dims if kind is None else pltpu.VMEM(dims, kind) for dims, kind in scratch
         ],
         compiler_params=pltpu.CompilerParams(vmem_limit_bytes=20 * 1024 * 1024),
-        name=name or body.__name__,
     )(*args)
 
 
@@ -308,10 +291,7 @@
 def side(update_index, *args):
     outs = [shape(BLOCKS[0], F32), shape(*SQUARE), shape(*GAINS), shape(*WEIGHTS)]
     body = functools.partial(side_kernel, update_index)
-    return call(body, outs, [BLOCKS, SQUARE], *args, name="side_kernel")
-
-
-NEAR = [GAINS, SQUARE, (BLOCKS[0], F32), BLOCKS]
+    return call(body, outs, [BLOCKS, SQUARE], *args)
 
 
 def copies(number):
@@ -319,16 +299,20 @@
 
 
 def middle(returned, turned, gating, out, gains, weights):
-    scratch = [*NEAR, WEIGHTS, ROWS, HANDS, BLOCKS, BLOCKS, copies(5)]
-    return call(middle_kernel, [SEND, TURNED], scratch, gains, out, gating, turned, weights, returned, far=5)
+    scratch = [ROWS, HANDS, BLOCKS, BLOCKS]
+    return call(middle_kernel, [SEND, TURNED], scratch, returned, turned, gating, out, gains, weights)
 
 
 def last(returned, turned, gating, out, gains):
-    scratch = [*NEAR, ROWS, ROWS, BLOCKS, (BLOCKS[0], F32), WHOLE, copies(4), copies(4)]
-    return call(last_kernel, [shape(*WHOLE)], scratch, gains, out, gating, turned, returned, far=4, far_out=True)[0]
-
-
-def local(pair_rep, proj_weight, gate_weight, out_weight, in_gain, out_gain):
+    scratch = [ROWS, ROWS, BLOCKS, (BLOCKS[0], F32), WHOLE, copies(4)]
+    return call(last_kernel, [shape(*WHOLE)], scratch, returned, turned, gating, out, gains, far_out=True)[0]
+
+
+def exchanged(pieces):
+    return lax.ppermute(pieces, "core", SWAP)
+
+
+def steps(pair_rep, proj_weight, gate_weight, out_weight, in_gain, out_gain):
     core = lax.axis_index("core").astype(jnp.int32).reshape(1)
     core, pair_rep = lax.optimization_barrier((core, pair_rep))
     parameters = (proj_weight, gate_weight, out_weight, in_gain, out_gain)
@@ -343,14 +327,14 @@
         operands,
         scalars=1,
     )
-    taken = lax.ppermute(given, "core", SWAP)
+    taken = exchanged(given)
     (kept,) = call(kept_kernel, [shape(HALF, F32)], [], kept_rows, operands)
     triangle = (kept + taken.astype(F32)).astype(BF16)
     returned = to_chips(triangle.reshape(128, 32, 128))
     send, turned = middle(returned, turned, gating, out, gains, weights)
     operands = to_chips(send).reshape(8, 16, 2, 32, 128)
     gating, out, gains, _ = side(1, turned, *parameters)
-    other = lax.ppermute(operands[:, :, 0], "core", SWAP)
+    other = exchanged(operands[:, :, 0])
     (triangle,) = call(incoming_kernel, [shape(HALF)], [((1024, 1024), BF16)], core, operands, other, scalars=1)
     returned = to_chips(triangle.reshape(128, 32, 128))
     return last(returned, turned, gating, out, gains)
@@ -360,5 +344,5 @@
     finer = Mesh(mesh.devices.reshape(8, 16, 2), ("row", "half", "core"))
     placed = (P("row", ("half", "core"), None), P(), P(), P(), P(), P())
     return jax.shard_map(
-        local, mesh=finer, in_specs=placed, out_specs=P("row", ("half", "core"), None), check_vma=False
+        steps, mesh=finer, in_specs=placed, out_specs=P("row", ("half", "core"), None), check_vma=False
     )

time: 229 us -> 233 us (1.017)
  local copies, waits for them, and re-layouts: 6.38 us -> 10.8 us
    unnamed x28 -> x30, local copies, waits for them, and re-layouts: 5.92 us -> 10.4 us
where the time goes in v5:
time: 233 us; the launch traced here: 232 us
  blocking collectives  126 us (54%)
  waiting for transfers between devices  58.4 us (25%)
  Pallas kernels  20.7 us (9%)
  starting transfers between devices  14.9 us (6%)
  local copies, waits for them, and re-layouts  10.8 us (5%)
    all_to_all x2, blocking collectives, to_chips(): lax.all_to_all(pieces, CHIPS, split_axis=0, concat_axis=0, tiled=True)  126 us
    all_to_all x2, waiting for transfers between devices, to_chips(): lax.all_to_all(pieces, CHIPS, split_axis=0, concat_axis=0, tiled=True)  53.9 us
    pallas_call x8, Pallas kernels, call(): pl.pallas_call(body, out_shape=outs, in_specs=[smem] * scalars + [hbm] *...  20.7 us
    all_to_all x2, starting transfers between devices, to_chips(): lax.all_to_all(pieces, CHIPS, split_axis=0, concat_axis=0, tiled=True)  14.7 us
    unnamed x30, local copies, waits for them, and re-layouts  10.4 us
  transfers between devices with their start and end apart: 4, of which 4 were waited for; matrix products, arithmetic and copies ran while one was open for 0% of the time, Pallas kernels for 2%

profile of v5, /device:TPU:32, one launch (start us, length us, event | category | flops | bytes accessed | tf_op | source)
XLA Modules:
  0.0 232.2 jit_solution(1253538448104036509)
XLA Ops:
  0.0 4.7 %shard_map.64 = (bf16[128,2,32,128]{3,2,1,0:T(8,128)(2,1)S(1)}, bf16[32,128,128]{2,1,0:T(8,128)(2,1)S(1)}) custom-call(bf16[128,32,128]{2,1,0:T(8,128)(2,1)} %x, bf16[2,4,128,128]{3,2,1,0:T(8,128)(2,1)} %proj.5, f32[2,128]{1,0:T(2,128)} %in_gain.5), custom_call_target="tpu_custom_call" | custom-call | tf_op jit(solution)/shard_map/pallas_call | solution.py:257
  4.7 67.4 %all_to_all.20 = bf16[128,2,32,128]{3,2,1,0:T(8,128)(2,1)S(1)} all-to-all(bf16[128,2,32,128]{3,2,1,0:T(8,128)(2,1)S(1)} %get-tuple-element.22), channel_id=1, replica_groups=mesh['row'=8,'half'=16,'core'=2] {'row','half'}, dimensions={0} | all-to-all | bytes 4194304 | tf_op jit(solution)/shard_map/all_to_all | solution.py:270
  72.1 1.1 shard_map.65
  73.2 0.1 collective-permute-start
  73.3 0.7 shard_map.66
  74.1 1.9 collective-permute-done
  76.0 1.3 add_convert_fusion
  77.3 0.0 copy-start.14
  77.3 7.4 %all-to-all-start.1 = ((bf16[128,32,128]{2,1,0:T(8,128)(2,1)}), bf16[128,32,128]{2,1,0:T(8,128)(2,1)S(1)}, u32[]{:S(2)}, u32[]{:S(2)}) async-start(bf16[128,32,128]{2,1,0:T(8,128)(2,1)} %bitcast.2), calls=%async_computation.1 | async-start | bytes 2097152 | tf_op jit(solution)/shard_map/all_to_all | solution.py:270
  84.7 1.6 shard_map.67
  86.3 1.3 copy-done.1
  87.7 0.7 copy-done.7
  88.3 0.6 copy-done.9
  89.0 0.6 copy-done.11
  89.6 26.1 %all-to-all-done.1.returned = bf16[128,32,128]{2,1,0:T(8,128)(2,1)S(1)} async-done(((bf16[128,32,128]{2,1,0:T(8,128)(2,1)}), bf16[128,32,128]{2,1,0:T(8,128)(2,1)S(1)}, u32[]{:S(2)}, u32[]{:S(2)}) %all-to-all-start.1) | async-done | bytes 1048608 | tf_op jit(solution)/shard_map/all_to_all | solution.py:270
  115.7 1.6 copy-done.2
  117.3 0.9 copy-done.8
  118.2 0.9 copy-done.10
  119.2 0.8 copy-done.12
  119.9 4.3 %shard_map.68 = (bf16[128,2,32,128]{3,2,1,0:T(8,128)(2,1)S(1)}, bf16[32,128,128]{2,1,0:T(8,128)(2,1)S(1)}) custom-call(bf16[128,32,128]{2,1,0:T(8,128)(2,1)S(1)} %all-to-all-done.1.returned, bf16[32,128,128]{2,1,0:T(8,128)(2,1)S(1)} %get-tuple-element.25.turned, f32[32,128,128]{2,1,0:T(8,128)S(1)} %copy-done.2, bf16[128,128]{1,0:T(8,128)(2,1)S(1)} %copy-done.12, ...), custom_call_target="tpu_custom_call" | custom-call | tf_op jit(solution)/shard_map/pallas_call | solution.py:257
  124.3 58.3 %all_to_all.21 = bf16[128,2,32,128]{3,2,1,0:T(8,128)(2,1)S(1)} all-to-all(bf16[128,2,32,128]{3,2,1,0:T(8,128)(2,1)S(1)} %get-tuple-element.30), channel_id=1, replica_groups=mesh['row'=8,'half'=16,'core'=2] {'row','half'}, dimensions={0} | all-to-all | bytes 4194304 | tf_op jit(solution)/shard_map/all_to_all | solution.py:270
  182.6 0.4 copy.7
  183.0 0.1 slice_bitcast_fusion
  183.1 0.1 collective-permute-start.1
  183.2 2.6 %collective-permute-done.1.other = bf16[8,16,32,128]{3,2,1,0:T(8,128)(2,1)S(1)} collective-permute-done((bf16[8,16,32,128]{3,2,1,0:T(8,128)(2,1)S(1)}, bf16[8,16,32,128]{3,2,1,0:T(8,128)(2,1)S(1)}, u32[]{:S(2)}, u32[]{:S(2)}) %collective-permute-start.1) | collective-permute-done | bytes 1048608 | tf_op jit(solution)/shard_map/ppermute | solution.py:312
  185.8 2.8 %shard_map.69 = bf16[8,16,32,128]{3,2,1,0:T(8,128)(2,1)} custom-call(s32[1]{0:T(128)} %bitcast.core, bf16[8,16,2,32,128]{4,3,2,1,0:T(8,128)(2,1)S(1)} %bitcast.8, bf16[8,16,32,128]{3,2,1,0:T(8,128)(2,1)S(1)} %collective-permute-done.1.other), custom_call_target="tpu_custom_call" | custom-call | tf_op jit(solution)/shard_map/pallas_call | solution.py:257
  188.7 7.3 %all-to-all-start.3 = ((bf16[128,32,128]{2,1,0:T(8,128)(2,1)}), bf16[128,32,128]{2,1,0:T(8,128)(2,1)S(1)}, u32[]{:S(2)}, u32[]{:S(2)}) async-start(bf16[128,32,128]{2,1,0:T(8,128)(2,1)} %bitcast.6), calls=%async_computation.3 | async-start | bytes 2097152 | tf_op jit(solution)/shard_map/all_to_all | solution.py:270
  196.0 1.9 shard_map.70
  197.9 1.3 copy-done.3
  199.3 27.8 %all-to-all-done.3.returned = bf16[128,32,128]{2,1,0:T(8,128)(2,1)S(1)} async-done(((bf16[128,32,128]{2,1,0:T(8,128)(2,1)}), bf16[128,32,128]{2,1,0:T(8,128)(2,1)S(1)}, u32[]{:S(2)}, u32[]{:S(2)}) %all-to-all-start.3) | async-done | bytes 1048608 | tf_op jit(solution)/shard_map/all_to_all | solution.py:270
  227.0 1.6 copy-done.4
  228.6 3.4 %shard_map.71 = bf16[128,32,128]{2,1,0:T(8,128)(2,1)} custom-call(bf16[128,32,128]{2,1,0:T(8,128)(2,1)S(1)} %all-to-all-done.3.returned, bf16[32,128,128]{2,1,0:T(8,128)(2,1)S(1)} %get-tuple-element.31.turned, f32[32,128,128]{2,1,0:T(8,128)S(1)} %copy-done.4, bf16[128,128]{1,0:T(8,128)(2,1)S(1)} %get-tuple-element.33.out, ...), custom_call_target="tpu_custom_call" | custom-call | tf_op jit(solution)/shard_map/pallas_call | solution.py:257
  (19 shorter events, 0.0 us)
Async XLA Ops:
  73.2 2.7 %collective-permute-start = (bf16[8,16,32,128]{3,2,1,0:T(8,128)(2,1)S(1)}, bf16[8,16,32,128]{3,2,1,0:T(8,128)(2,1)S(1)}, u32[]{:S(2)}, u32[]{:S(2)}) collective-permute-start(bf16[8,16,32,128]{3,2,1,0:T(8,128)(2,1)S(1)} %get-tuple-element.24), channel_id=1, source_target_pairs={{0,1},{1,0},{2,3},{3,2},{4,5},{5,4},{6,7},{7,6},{8,9},{9,8},{10,11... | collective-permute-start | bytes 3145736 | tf_op jit(solution)/shard_map/ppermute | solution.py:312
  77.3 7.4 %copy-start = (bf16[2,4,128,128]{3,2,1,0:T(8,128)(2,1)S(1)}, bf16[2,4,128,128]{3,2,1,0:T(8,128)(2,1)}, u32[]{:S(2)}) copy-start(bf16[2,4,128,128]{3,2,1,0:T(8,128)(2,1)} %proj.5) | copy-start | bytes 786436
  77.3 7.4 %copy-start.5 = (bf16[2,128,128]{2,1,0:T(8,128)(2,1)S(1)}, bf16[2,128,128]{2,1,0:T(8,128)(2,1)}, u32[]{:S(2)}) copy-start(bf16[2,128,128]{2,1,0:T(8,128)(2,1)} %gate_w.3) | copy-start | bytes 196612
  77.3 7.5 %copy-start.6 = (bf16[2,128,128]{2,1,0:T(8,128)(2,1)S(1)}, bf16[2,128,128]{2,1,0:T(8,128)(2,1)}, u32[]{:S(2)}) copy-start(bf16[2,128,128]{2,1,0:T(8,128)(2,1)} %out_w.3) | copy-start | bytes 196612
  77.3 7.5 %copy-start.13 = (f32[2,128]{1,0:T(2,128)S(1)}, f32[2,128]{1,0:T(2,128)}, u32[]{:S(2)}) copy-start(f32[2,128]{1,0:T(2,128)} %in_gain.5) | copy-start | bytes 3076
  77.3 7.5 %copy-start.14 = (f32[2,128]{1,0:T(2,128)S(1)}, f32[2,128]{1,0:T(2,128)}, u32[]{:S(2)}) copy-start(f32[2,128]{1,0:T(2,128)} %out_gain.3) | copy-start | bytes 3076
  77.3 38.4 %all-to-all-start.1 = ((bf16[128,32,128]{2,1,0:T(8,128)(2,1)}), bf16[128,32,128]{2,1,0:T(8,128)(2,1)S(1)}, u32[]{:S(2)}, u32[]{:S(2)}) async-start(bf16[128,32,128]{2,1,0:T(8,128)(2,1)} %bitcast.2), calls=%async_computation.1 | async-start | bytes 2097152 | tf_op jit(solution)/shard_map/all_to_all | solution.py:270
  86.3 1.3 copy-start.1
  87.7 0.7 copy-start.7
  88.3 0.6 copy-start.9
  89.0 0.6 copy-start.11
  115.7 1.6 copy-start.2
  117.3 0.9 copy-start.8
  118.2 0.9 copy-start.10
  119.2 0.8 copy-start.12
  183.1 2.7 %collective-permute-start.1 = (bf16[8,16,32,128]{3,2,1,0:T(8,128)(2,1)S(1)}, bf16[8,16,32,128]{3,2,1,0:T(8,128)(2,1)S(1)}, u32[]{:S(2)}, u32[]{:S(2)}) collective-permute-start(bf16[8,16,32,128]{3,2,1,0:T(8,128)(2,1)S(1)} %slice_bitcast_fusion), channel_id=1, source_target_pairs={{0,1},{1,0},{2,3},{3,2},{4,5},{5,4},{6,7},{7,6},{8,9},{9,8},{10,11... | collective-permute-start | bytes 3145736 | tf_op jit(solution)/shard_map/ppermute | solution.py:312
  188.7 38.4 %all-to-all-start.3 = ((bf16[128,32,128]{2,1,0:T(8,128)(2,1)}), bf16[128,32,128]{2,1,0:T(8,128)(2,1)S(1)}, u32[]{:S(2)}, u32[]{:S(2)}) async-start(bf16[128,32,128]{2,1,0:T(8,128)(2,1)} %bitcast.6), calls=%async_computation.3 | async-start | bytes 2097152 | tf_op jit(solution)/shard_map/all_to_all | solution.py:270
  197.9 1.3 copy-start.3
  227.0 1.6 copy-start.4

commit v6 on v5

--- a/solution.py
+++ b/solution.py
@@ -15,6 +15,7 @@
 BF16 = jnp.bfloat16
 PITCH = 40
 WIDE = 136
+STAGGER = 3100
 
 
 epsilon = 1e-05
@@ -226,6 +227,12 @@
         product = dot(kept_rows[q * 32 : (q + 4) * 32, :], lefts)
         for r in range(8):
             kept[r, q : q + 4] = product[:, r * 128 : (r + 1) * 128].reshape(4, 32, 128)
+
+
+def joined_kernel(core, kept, taken, joined, spun):
+    spun[...] = lax.fori_loop(0, core[0] * STAGGER, lambda _, a: a * 0.5 + 0.25, jnp.ones((8, 128), F32))
+    for r in range(8):
+        joined[r] = (kept[r] + taken[r].astype(F32)).astype(BF16)
 
 
 def incoming_kernel(core, operands, other, products, lefts):
@@ -329,7 +336,7 @@
     )
     taken = exchanged(given)
     (kept,) = call(kept_kernel, [shape(HALF, F32)], [], kept_rows, operands)
-    triangle = (kept + taken.astype(F32)).astype(BF16)
+    triangle, _ = call(joined_kernel, [shape(HALF), shape((8, 128), F32)], [], core, kept, taken, scalars=1)
     returned = to_chips(triangle.reshape(128, 32, 128))
     send, turned = middle(returned, turned, gating, out, gains, weights)
     operands = to_chips(send).reshape(8, 16, 2, 32, 128)

time: 233 us -> 224 us (0.961)
  starting transfers between devices: 14.9 us -> 28.2 us
  blocking collectives: 126 us -> 114 us
  waiting for transfers between devices: 58.4 us -> 48.1 us
    ppermute x2, starting transfers between devices: 0.19 us -> 13.7 us  [exchanged(): return lax.ppermute(pieces, 'core', SWAP)]
    all_to_all x2, blocking collectives: 126 us -> 114 us  [to_chips(): lax.all_to_all(pieces, CHIPS, split_axis=0, concat_axis=0, tiled=True)]
    all_to_all x2, waiting for transfers between devices: 53.9 us -> 44 us  [to_chips(): lax.all_to_all(pieces, CHIPS, split_axis=0, concat_axis=0, tiled=True)]
    pallas_call x8 -> x9, Pallas kernels: 20.7 us -> 21.9 us  [call(): pl.pallas_call(body, out_shape=outs, in_specs=[smem] * scalars + [hbm] *...]
where the time goes in v6:
time: 224 us
  blocking collectives  114 us (51%)
  waiting for transfers between devices  48.1 us (21%)
  starting transfers between devices  28.2 us (13%)
  Pallas kernels  21.9 us (10%)
  local copies, waits for them, and re-layouts  10.9 us (5%)
    all_to_all x2, blocking collectives, to_chips(): lax.all_to_all(pieces, CHIPS, split_axis=0, concat_axis=0, tiled=True)  114 us
    all_to_all x2, waiting for transfers between devices, to_chips(): lax.all_to_all(pieces, CHIPS, split_axis=0, concat_axis=0, tiled=True)  44 us
    pallas_call x9, Pallas kernels, call(): pl.pallas_call(body, out_shape=outs, in_specs=[smem] * scalars + [hbm] *...  21.9 us
    all_to_all x2, starting transfers between devices, to_chips(): lax.all_to_all(pieces, CHIPS, split_axis=0, concat_axis=0, tiled=True)  14.4 us
    ppermute x2, starting transfers between devices, exchanged(): return lax.ppermute(pieces, 'core', SWAP)  13.7 us
    unnamed x30, local copies, waits for them, and re-layouts  10.4 us
  transfers between devices with their start and end apart: 4, of which 4 were waited for; matrix products, arithmetic and copies ran while one was open for 0% of the time, Pallas kernels for 2%

profile of v6, /device:TPU:32, one launch (start us, length us, event | category | flops | bytes accessed | tf_op | source)
XLA Modules:
  0.0 223.7 jit_solution(1036539767068422604)
XLA Ops:
  0.0 4.7 %shard_map.64 = (bf16[128,2,32,128]{3,2,1,0:T(8,128)(2,1)S(1)}, bf16[32,128,128]{2,1,0:T(8,128)(2,1)S(1)}) custom-call(bf16[128,32,128]{2,1,0:T(8,128)(2,1)} %x, bf16[2,4,128,128]{3,2,1,0:T(8,128)(2,1)} %proj.5, f32[2,128]{1,0:T(2,128)} %in_gain.5), custom_call_target="tpu_custom_call" | custom-call | tf_op jit(solution)/shard_map/pallas_call | solution.py:264
  4.7 67.4 %all_to_all.20 = bf16[128,2,32,128]{3,2,1,0:T(8,128)(2,1)S(1)} all-to-all(bf16[128,2,32,128]{3,2,1,0:T(8,128)(2,1)S(1)} %get-tuple-element.23), channel_id=1, replica_groups=mesh['row'=8,'half'=16,'core'=2] {'row','half'}, dimensions={0} | all-to-all | bytes 4194304 | tf_op jit(solution)/shard_map/all_to_all | solution.py:277
  72.1 1.1 shard_map.65
  73.2 0.1 collective-permute-start
  73.3 0.7 shard_map.66.kept
  74.1 0.0 copy-start
  74.1 1.8 collective-permute-done.taken
  76.0 1.3 shard_map.67
  77.2 7.3 %all-to-all-start.1 = ((bf16[128,32,128]{2,1,0:T(8,128)(2,1)}), bf16[128,32,128]{2,1,0:T(8,128)(2,1)S(1)}, u32[]{:S(2)}, u32[]{:S(2)}) async-start(bf16[128,32,128]{2,1,0:T(8,128)(2,1)} %bitcast.2), calls=%async_computation.1 | async-start | bytes 2097152 | tf_op jit(solution)/shard_map/all_to_all | solution.py:277
  84.6 1.6 shard_map.68
  86.1 1.3 copy-done.1
  87.5 0.7 copy-done.7
  88.2 0.7 copy-done.9
  88.8 0.6 copy-done.11
  89.4 16.0 %all-to-all-done.1.returned = bf16[128,32,128]{2,1,0:T(8,128)(2,1)S(1)} async-done(((bf16[128,32,128]{2,1,0:T(8,128)(2,1)}), bf16[128,32,128]{2,1,0:T(8,128)(2,1)S(1)}, u32[]{:S(2)}, u32[]{:S(2)}) %all-to-all-start.1) | async-done | bytes 1048608 | tf_op jit(solution)/shard_map/all_to_all | solution.py:277
  105.4 1.6 copy-done.2
  107.0 0.9 copy-done.8
  107.9 0.9 copy-done.10
  108.8 0.8 copy-done.12
  109.6 4.3 %shard_map.69 = (bf16[128,2,32,128]{3,2,1,0:T(8,128)(2,1)S(1)}, bf16[32,128,128]{2,1,0:T(8,128)(2,1)S(1)}) custom-call(bf16[128,32,128]{2,1,0:T(8,128)(2,1)S(1)} %all-to-all-done.1.returned, bf16[32,128,128]{2,1,0:T(8,128)(2,1)S(1)} %get-tuple-element.27.turned, f32[32,128,128]{2,1,0:T(8,128)S(1)} %copy-done.2, bf16[128,128]{1,0:T(8,128)(2,1)S(1)} %copy-done.12, ...), custom_call_target="tpu_custom_call" | custom-call | tf_op jit(solution)/shard_map/pallas_call | solution.py:264
  114.0 46.8 %all_to_all.21 = bf16[128,2,32,128]{3,2,1,0:T(8,128)(2,1)S(1)} all-to-all(bf16[128,2,32,128]{3,2,1,0:T(8,128)(2,1)S(1)} %get-tuple-element.32), channel_id=1, replica_groups=mesh['row'=8,'half'=16,'core'=2] {'row','half'}, dimensions={0} | all-to-all | bytes 4194304 | tf_op jit(solution)/shard_map/all_to_all | solution.py:277
  160.8 0.4 copy.7
  161.1 0.1 slice_bitcast_fusion
  161.2 13.6 %collective-permute-start.1 = (bf16[8,16,32,128]{3,2,1,0:T(8,128)(2,1)S(1)}, bf16[8,16,32,128]{3,2,1,0:T(8,128)(2,1)S(1)}, u32[]{:S(2)}, u32[]{:S(2)}) collective-permute-start(bf16[8,16,32,128]{3,2,1,0:T(8,128)(2,1)S(1)} %slice_bitcast_fusion), channel_id=1, source_target_pairs={{0,1},{1,0},{2,3},{3,2},{4,5},{5,4},{6,7},{7,6},{8,9},{9,8},{10,11... | collective-permute-start | bytes 3145736 | tf_op jit(solution)/shard_map/ppermute | solution.py:319
  174.9 2.3 %collective-permute-done.1.other = bf16[8,16,32,128]{3,2,1,0:T(8,128)(2,1)S(1)} collective-permute-done((bf16[8,16,32,128]{3,2,1,0:T(8,128)(2,1)S(1)}, bf16[8,16,32,128]{3,2,1,0:T(8,128)(2,1)S(1)}, u32[]{:S(2)}, u32[]{:S(2)}) %collective-permute-start.1) | collective-permute-done | bytes 1048608 | tf_op jit(solution)/shard_map/ppermute | solution.py:319
  177.2 2.8 %shard_map.70 = bf16[8,16,32,128]{3,2,1,0:T(8,128)(2,1)} custom-call(s32[1]{0:T(128)} %bitcast.core, bf16[8,16,2,32,128]{4,3,2,1,0:T(8,128)(2,1)S(1)} %bitcast.8, bf16[8,16,32,128]{3,2,1,0:T(8,128)(2,1)S(1)} %collective-permute-done.1.other), custom_call_target="tpu_custom_call" | custom-call | tf_op jit(solution)/shard_map/pallas_call | solution.py:264
  180.0 7.2 %all-to-all-start.3 = ((bf16[128,32,128]{2,1,0:T(8,128)(2,1)}), bf16[128,32,128]{2,1,0:T(8,128)(2,1)S(1)}, u32[]{:S(2)}, u32[]{:S(2)}) async-start(bf16[128,32,128]{2,1,0:T(8,128)(2,1)} %bitcast.6), calls=%async_computation.3 | async-start | bytes 2097152 | tf_op jit(solution)/shard_map/all_to_all | solution.py:277
  187.2 1.9 shard_map.71
  189.2 1.3 copy-done.3
  190.5 28.0 %all-to-all-done.3.returned = bf16[128,32,128]{2,1,0:T(8,128)(2,1)S(1)} async-done(((bf16[128,32,128]{2,1,0:T(8,128)(2,1)}), bf16[128,32,128]{2,1,0:T(8,128)(2,1)S(1)}, u32[]{:S(2)}, u32[]{:S(2)}) %all-to-all-start.3) | async-done | bytes 1048608 | tf_op jit(solution)/shard_map/all_to_all | solution.py:277
  218.5 1.6 copy-done.4
  220.1 3.4 %shard_map.72 = bf16[128,32,128]{2,1,0:T(8,128)(2,1)} custom-call(bf16[128,32,128]{2,1,0:T(8,128)(2,1)S(1)} %all-to-all-done.3.returned, bf16[32,128,128]{2,1,0:T(8,128)(2,1)S(1)} %get-tuple-element.33.turned, f32[32,128,128]{2,1,0:T(8,128)S(1)} %copy-done.4, bf16[128,128]{1,0:T(8,128)(2,1)S(1)} %get-tuple-element.35.out, ...), custom_call_target="tpu_custom_call" | custom-call | tf_op jit(solution)/shard_map/pallas_call | solution.py:264
  (19 shorter events, 0.0 us)
Async XLA Ops:
  73.2 2.7 %collective-permute-start = (bf16[8,16,32,128]{3,2,1,0:T(8,128)(2,1)S(1)}, bf16[8,16,32,128]{3,2,1,0:T(8,128)(2,1)S(1)}, u32[]{:S(2)}, u32[]{:S(2)}) collective-permute-start(bf16[8,16,32,128]{3,2,1,0:T(8,128)(2,1)S(1)} %get-tuple-element.25), channel_id=1, source_target_pairs={{0,1},{1,0},{2,3},{3,2},{4,5},{5,4},{6,7},{7,6},{8,9},{9,8},{10,11... | collective-permute-start | bytes 3145736 | tf_op jit(solution)/shard_map/ppermute | solution.py:319
  74.1 10.4 %copy-start = (bf16[2,4,128,128]{3,2,1,0:T(8,128)(2,1)S(1)}, bf16[2,4,128,128]{3,2,1,0:T(8,128)(2,1)}, u32[]{:S(2)}) copy-start(bf16[2,4,128,128]{3,2,1,0:T(8,128)(2,1)} %proj.5) | copy-start | bytes 786436
  74.1 10.4 %copy-start.5 = (bf16[2,128,128]{2,1,0:T(8,128)(2,1)S(1)}, bf16[2,128,128]{2,1,0:T(8,128)(2,1)}, u32[]{:S(2)}) copy-start(bf16[2,128,128]{2,1,0:T(8,128)(2,1)} %gate_w.3) | copy-start | bytes 196612
  74.1 10.4 %copy-start.6 = (bf16[2,128,128]{2,1,0:T(8,128)(2,1)S(1)}, bf16[2,128,128]{2,1,0:T(8,128)(2,1)}, u32[]{:S(2)}) copy-start(bf16[2,128,128]{2,1,0:T(8,128)(2,1)} %out_w.3) | copy-start | bytes 196612
  74.1 10.4 %copy-start.13 = (f32[2,128]{1,0:T(2,128)S(1)}, f32[2,128]{1,0:T(2,128)}, u32[]{:S(2)}) copy-start(f32[2,128]{1,0:T(2,128)} %in_gain.5) | copy-start | bytes 3076
  74.1 10.4 %copy-start.14 = (f32[2,128]{1,0:T(2,128)S(1)}, f32[2,128]{1,0:T(2,128)}, u32[]{:S(2)}) copy-start(f32[2,128]{1,0:T(2,128)} %out_gain.3) | copy-start | bytes 3076
  77.2 28.2 %all-to-all-start.1 = ((bf16[128,32,128]{2,1,0:T(8,128)(2,1)}), bf16[128,32,128]{2,1,0:T(8,128)(2,1)S(1)}, u32[]{:S(2)}, u32[]{:S(2)}) async-start(bf16[128,32,128]{2,1,0:T(8,128)(2,1)} %bitcast.2), calls=%async_computation.1 | async-start | bytes 2097152 | tf_op jit(solution)/shard_map/all_to_all | solution.py:277
  86.1 1.3 copy-start.1
  87.5 0.7 copy-start.7
  88.2 0.7 copy-start.9
  88.8 0.6 copy-start.11
  105.4 1.6 copy-start.2
  107.0 0.9 copy-start.8
  107.9 0.9 copy-start.10
  108.8 0.8 copy-start.12
  161.2 15.9 %collective-permute-start.1 = (bf16[8,16,32,128]{3,2,1,0:T(8,128)(2,1)S(1)}, bf16[8,16,32,128]{3,2,1,0:T(8,128)(2,1)S(1)}, u32[]{:S(2)}, u32[]{:S(2)}) collective-permute-start(bf16[8,16,32,128]{3,2,1,0:T(8,128)(2,1)S(1)} %slice_bitcast_fusion), channel_id=1, source_target_pairs={{0,1},{1,0},{2,3},{3,2},{4,5},{5,4},{6,7},{7,6},{8,9},{9,8},{10,11... | collective-permute-start | bytes 3145736 | tf_op jit(solution)/shard_map/ppermute | solution.py:319
  180.0 38.5 %all-to-all-start.3 = ((bf16[128,32,128]{2,1,0:T(8,128)(2,1)}), bf16[128,32,128]{2,1,0:T(8,128)(2,1)S(1)}, u32[]{:S(2)}, u32[]{:S(2)}) async-start(bf16[128,32,128]{2,1,0:T(8,128)(2,1)} %bitcast.6), calls=%async_computation.3 | async-start | bytes 2097152 | tf_op jit(solution)/shard_map/all_to_all | solution.py:277
  189.2 1.3 copy-start.3
  218.5 1.6 copy-start.4

commit v7 on v6

--- a/solution.py
+++ b/solution.py
@@ -15,7 +15,7 @@
 BF16 = jnp.bfloat16
 PITCH = 40
 WIDE = 136
-STAGGER = 3100
+STAGGER = 2600
 
 
 epsilon = 1e-05
@@ -78,15 +78,14 @@
     each(16, body)
 
 
-def gather_hands(hands, send):
+def gather_side(hands, side, target, start, number):
     def step(n, _):
         for part in range(8):
-            h = n * 8 + part
-            for side in range(2):
-                send[h, side] = hands[side, pl.ds(h, 32, stride=WIDE), :].astype(BF16)
+            h = start + n * 8 + part
+            target[h] = hands[side, pl.ds(h, 32, stride=WIDE), :].astype(BF16)
         return _
 
-    lax.fori_loop(0, 16, step, 0)
+    lax.fori_loop(0, number // 8, step, 0)
 
 
 def fetch(pairs, arrived):
@@ -99,15 +98,15 @@
 def first_kernel(x, proj, in_gain, send, turned, x_near, proj_near, gain_near, rows, hands, normed, weights, gains, arrived):
     quarters = [pl.ds(n * 32, 32) for n in range(4)]
     pairs = [(x.at[part], x_near.at[part]) for part in quarters]
-    pieces = fetch([*pairs, (proj.at[0], proj_near), (in_gain, gain_near)], arrived)
-    for n in range(4):
-        pieces[n].wait()
-        spread_rows(x_near, rows, n * 32, 32)
-    pieces[4].wait()
-    pieces[5].wait()
+    pieces = fetch([(proj.at[0], proj_near), (in_gain, gain_near), *pairs], arrived)
+    pieces[0].wait()
+    pieces[1].wait()
     for p in range(4):
         weights[p * 128 : (p + 1) * 128, :] = turn(proj_near[p])
     gains[...] = column(gain_near[0:1, :])
+    for n in range(4):
+        pieces[2 + n].wait()
+        spread_rows(x_near, rows, n * 32, 32)
 
     def body(j):
         channels = rows[pl.ds(j, 128, stride=PITCH), :].T
@@ -116,7 +115,8 @@
 
     each(32, body)
     project(normed, weights, hands)
-    gather_hands(hands, send)
+    for side in range(2):
+        gather_side(hands, side, send.at[:, side], 0, 128)
 
 
 def side_kernel(update_index, turned, proj, gate_w, out_w, in_gain, out_gain, gating, out, gains, weights, normed, gate):
@@ -155,7 +155,7 @@
     ]
 
 
-def middle_kernel(returned, turned, gating, out, gains, weights, send, newer, tri, hands, mixed, later):
+def middle_kernel(returned, turned, gating, out, gains, weights, left, right, newer, tri, hands, mixed, later, right_near, leaving):
     spread_rows(returned, tri, 0, 128)
     mix(tri, mixed, gains)
 
@@ -167,18 +167,39 @@
 
     each(16, body)
     project(later, weights, hands)
-    gather_hands(hands, send)
-
-
-def last_kernel(returned, turned, gating, out, gains, final, tri, rows, mixed, newer, near, left):
+    pieces = []
+    for n in range(2):
+        part = pl.ds(n * 64, 64)
+        gather_side(hands, 1, right_near, n * 64, 64)
+        pieces.append(pltpu.make_async_copy(right_near.at[part], right.at[part], leaving.at[n]))
+        pieces[n].start()
+    gather_side(hands, 0, left, 0, 128)
+    for piece in pieces:
+        piece.wait()
+
+
+def last_kernel(
+    far_gains, far_out, far_gating, far_turned, returned, final,
+    gains, out, gating, turned, tri, rows, mixed, newer, near, arrived, left,
+):
+    halves = [pl.ds(0, 16), pl.ds(16, 16)]
+    pairs = [(far_gains, gains), (far_out, out)]
+    for part in halves:
+        pairs += [(far_gating.at[part], gating.at[part]), (far_turned.at[part], turned.at[part])]
+    pieces = fetch(pairs, arrived)
     spread_rows(returned, tri, 0, 128)
+    pieces[0].wait()
     mix(tri, mixed, gains)
+    pieces[1].wait()
 
     def body(pair):
         for part, channels in enumerate(new_channels(turned, gating, mixed, out, pair)):
             newer[pair * 2 + part] = channels
 
-    each(16, body)
+    for n in range(2):
+        pieces[2 + 2 * n].wait()
+        pieces[3 + 2 * n].wait()
+        each(8, lambda pair, n=n: body(n * 8 + pair))
 
     def back(j):
         rows[pl.ds(j, 128, stride=PITCH), :] = newer[j].T
@@ -235,17 +256,24 @@
         joined[r] = (kept[r] + taken[r].astype(F32)).astype(BF16)
 
 
-def incoming_kernel(core, operands, other, products, lefts):
-    for r in range(8):
-        for q in range(16):
-            own = pl.multiple_of(q * 64 + core[0] * 32, 32)
-            swapped = pl.multiple_of(q * 64 + 32 - core[0] * 32, 32)
-            lefts[pl.ds(own, 32), r * 128 : (r + 1) * 128] = operands[r, q, 0]
-            lefts[pl.ds(swapped, 32), r * 128 : (r + 1) * 128] = other[r, q]
-    rights = jnp.concatenate([side_of(operands, r, 1) for r in range(8)], axis=1)
+def incoming_kernel(core, own, other, operand, products, lefts, arrived):
+    pairs = []
+    for q in (0, 8):
+        for r in range(8):
+            lanes = pl.ds(r * 128, 128)
+            pairs.append((own.at[r, pl.ds(q, 8)], lefts.at[pl.ds(q, 8), core[0], :, lanes]))
+            pairs.append((other.at[r, pl.ds(q, 8)], lefts.at[pl.ds(q, 8), 1 - core[0], :, lanes]))
+    pieces = fetch(pairs, arrived)
+    rights = jnp.concatenate([operand[r].reshape(512, 128) for r in range(8)], axis=1)
     for b in range(0, 8, 2):
+        if b % 4 == 0:
+            for piece in pieces[b * 4 : b * 4 + 16]:
+                piece.wait()
         product = lax.dot_general(
-            rights, lefts[b * 128 : (b + 2) * 128, :], (((1,), (1,)), ((), ())), preferred_element_type=F32
+            rights,
+            lefts[b * 2 : b * 2 + 4].reshape(256, 1024),
+            (((1,), (1,)), ((), ())),
+            preferred_element_type=F32,
         ).astype(BF16)
         for part in range(2):
             products[b + part] = product[:, part * 128 : (part + 1) * 128].reshape(16, 32, 128)
@@ -255,7 +283,7 @@
     return jax.ShapeDtypeStruct(dims, kind)
 
 
-def call(body, outs, scratch, *args, scalars=0, far=0, far_out=False):
+def call(body, outs, scratch, *args, scalars=0, far=0, far_outs=()):
     args = [
         pltpu.with_memory_space_constraint(arg, pltpu.HBM) if scalars <= n < scalars + far else arg
         for n, arg in enumerate(args)
@@ -265,7 +293,7 @@
         body,
         out_shape=outs,
         in_specs=[smem] * scalars + [hbm] * far + [vmem] * (len(args) - scalars - far),
-        out_specs=[hbm if far_out else vmem] * len(outs),
+        out_specs=[hbm if n in far_outs else vmem for n in range(len(outs))],
         scratch_shapes=[
             dims if kind is None else pltpu.VMEM(dims, kind) for dims, kind in scratch
         ],
@@ -306,13 +334,15 @@
 
 
 def middle(returned, turned, gating, out, gains, weights):
-    scratch = [ROWS, HANDS, BLOCKS, BLOCKS]
-    return call(middle_kernel, [SEND, TURNED], scratch, returned, turned, gating, out, gains, weights)
+    scratch = [ROWS, HANDS, BLOCKS, BLOCKS, WHOLE, copies(2)]
+    outs = [shape(*WHOLE), pltpu.HBM(*WHOLE), TURNED]
+    return call(middle_kernel, outs, scratch, returned, turned, gating, out, gains, weights, far_outs=(1,))
 
 
 def last(returned, turned, gating, out, gains):
-    scratch = [ROWS, ROWS, BLOCKS, (BLOCKS[0], F32), WHOLE, copies(4)]
-    return call(last_kernel, [shape(*WHOLE)], scratch, returned, turned, gating, out, gains, far_out=True)[0]
+    near = [GAINS, SQUARE, (BLOCKS[0], F32), BLOCKS]
+    scratch = [*near, ROWS, ROWS, BLOCKS, (BLOCKS[0], F32), WHOLE, copies(6), copies(4)]
+    return call(last_kernel, [shape(*WHOLE)], scratch, gains, out, gating, turned, returned, far=4, far_outs=(0,))[0]
 
 
 def exchanged(pieces):
@@ -338,11 +368,22 @@
     (kept,) = call(kept_kernel, [shape(HALF, F32)], [], kept_rows, operands)
     triangle, _ = call(joined_kernel, [shape(HALF), shape((8, 128), F32)], [], core, kept, taken, scalars=1)
     returned = to_chips(triangle.reshape(128, 32, 128))
-    send, turned = middle(returned, turned, gating, out, gains, weights)
-    operands = to_chips(send).reshape(8, 16, 2, 32, 128)
+    left, right, turned = middle(returned, turned, gating, out, gains, weights)
+    left = to_chips(left).reshape(HALF)
+    right = to_chips(right).reshape(HALF)
     gating, out, gains, _ = side(1, turned, *parameters)
-    other = exchanged(operands[:, :, 0])
-    (triangle,) = call(incoming_kernel, [shape(HALF)], [((1024, 1024), BF16)], core, operands, other, scalars=1)
+    other = exchanged(left)
+    (triangle,) = call(
+        incoming_kernel,
+        [shape(HALF)],
+        [((16, 2, 32, 1024), BF16), copies(32)],
+        core,
+        left,
+        other,
+        right,
+        scalars=1,
+        far=2,
+    )
     returned = to_chips(triangle.reshape(128, 32, 128))
     return last(returned, turned, gating, out, gains)
 

time: 224 us -> 220 us (0.982)
  the two profiles are of different devices: /device:TPU:32 before, /device:TPU:33 now
where the time goes in v7:
time: 220 us
  blocking collectives  91 us (41%)
  waiting for transfers between devices  57.6 us (26%)
  Pallas kernels  38.1 us (17%)
  starting transfers between devices  22.6 us (10%)
  local copies, waits for them, and re-layouts  10.1 us (5%)
    all_to_all x2, blocking collectives, to_chips(): lax.all_to_all(pieces, CHIPS, split_axis=0, concat_axis=0, tiled=True)  91 us
    all_to_all x3, waiting for transfers between devices, to_chips(): lax.all_to_all(pieces, CHIPS, split_axis=0, concat_axis=0, tiled=True)  56.1 us
    pallas_call x9, Pallas kernels, call(): pl.pallas_call(body, out_shape=outs, in_specs=[smem] * scalars + [hbm] *...  38.1 us
    all_to_all x3, starting transfers between devices, to_chips(): lax.all_to_all(pieces, CHIPS, split_axis=0, concat_axis=0, tiled=True)  19.6 us
    unnamed x36, local copies, waits for them, and re-layouts  10.1 us
  transfers between devices with their start and end apart: 5, of which 4 were waited for; matrix products, arithmetic and copies ran while one was open for 0% of the time, Pallas kernels for 2%

profile of v7, /device:TPU:33, one launch (start us, length us, event | category | flops | bytes accessed | tf_op | source)
XLA Modules:
  0.0 219.7 jit_solution(2232293187334312445)
XLA Ops:
  0.0 4.7 %shard_map.64 = (bf16[128,2,32,128]{3,2,1,0:T(8,128)(2,1)S(1)}, bf16[32,128,128]{2,1,0:T(8,128)(2,1)S(1)}) custom-call(bf16[128,32,128]{2,1,0:T(8,128)(2,1)} %x, bf16[2,4,128,128]{3,2,1,0:T(8,128)(2,1)} %proj.5, f32[2,128]{1,0:T(2,128)} %in_gain.5), custom_call_target="tpu_custom_call" | custom-call | tf_op jit(solution)/shard_map/pallas_call | solution.py:292
  4.8 65.2 %all_to_all.25 = bf16[128,2,32,128]{3,2,1,0:T(8,128)(2,1)S(1)} all-to-all(bf16[128,2,32,128]{3,2,1,0:T(8,128)(2,1)S(1)} %get-tuple-element.24), channel_id=1, replica_groups=mesh['row'=8,'half'=16,'core'=2] {'row','half'}, dimensions={0} | all-to-all | bytes 4194304 | tf_op jit(solution)/shard_map/all_to_all | solution.py:305
  70.0 1.2 shard_map.65
  71.1 2.9 %collective-permute-start = (bf16[8,16,32,128]{3,2,1,0:T(8,128)(2,1)S(1)}, bf16[8,16,32,128]{3,2,1,0:T(8,128)(2,1)S(1)}, u32[]{:S(2)}, u32[]{:S(2)}) collective-permute-start(bf16[8,16,32,128]{3,2,1,0:T(8,128)(2,1)S(1)} %get-tuple-element.26), channel_id=1, source_target_pairs={{0,1},{1,0},{2,3},{3,2},{4,5},{5,4},{6,7},{7,6},{8,9},{9,8},{10,11... | collective-permute-start | bytes 3145736 | tf_op jit(solution)/shard_map/ppermute | solution.py:349
  74.0 0.7 shard_map.66.kept
  74.8 0.0 copy-start.6
  74.8 1.5 collective-permute-done.taken
  76.3 14.8 %shard_map.67 = (bf16[8,16,32,128]{3,2,1,0:T(8,128)(2,1)}, f32[8,128]{1,0:T(8,128)}) custom-call(s32[1]{0:T(128)} %bitcast.core, f32[8,16,32,128]{3,2,1,0:T(8,128)S(1)} %shard_map.66.kept, bf16[8,16,32,128]{3,2,1,0:T(8,128)(2,1)S(1)} %collective-permute-done.taken), custom_call_target="tpu_custom_call" | custom-call | tf_op jit(solution)/shard_map/pallas_call | solution.py:292
  91.1 6.7 %all-to-all-start.1 = ((bf16[128,32,128]{2,1,0:T(8,128)(2,1)}), bf16[128,32,128]{2,1,0:T(8,128)(2,1)S(1)}, u32[]{:S(2)}, u32[]{:S(2)}) async-start(bf16[128,32,128]{2,1,0:T(8,128)(2,1)} %bitcast.2), calls=%async_computation.1 | async-start | bytes 2097152 | tf_op jit(solution)/shard_map/all_to_all | solution.py:305
  97.9 1.6 shard_map.68
  99.5 1.3 copy-done.2
  100.8 0.7 copy-done.7
  101.5 0.7 copy-done.10
  102.2 0.6 copy-done.12
  102.8 15.2 %all-to-all-done.1.returned = bf16[128,32,128]{2,1,0:T(8,128)(2,1)S(1)} async-done(((bf16[128,32,128]{2,1,0:T(8,128)(2,1)}), bf16[128,32,128]{2,1,0:T(8,128)(2,1)S(1)}, u32[]{:S(2)}, u32[]{:S(2)}) %all-to-all-start.1) | async-done | bytes 1048608 | tf_op jit(solution)/shard_map/all_to_all | solution.py:305
  117.9 1.6 copy-done.3
  119.5 0.9 copy-done.8
  120.5 0.9 copy-done.11
  121.4 0.8 copy-done.13
  122.1 4.9 %shard_map.69 = (bf16[128,32,128]{2,1,0:T(8,128)(2,1)S(1)}, bf16[128,32,128]{2,1,0:T(8,128)(2,1)}, bf16[32,128,128]{2,1,0:T(8,128)(2,1)S(1)}) custom-call(bf16[128,32,128]{2,1,0:T(8,128)(2,1)S(1)} %all-to-all-done.1.returned, bf16[32,128,128]{2,1,0:T(8,128)(2,1)S(1)} %get-tuple-element.28.turned, f32[32,128,128]{2,1,0:T(8,128)S(1)} %copy-done.3, ...), custom_call_target="tpu_custom_call" | custom-call | tf_op jit(solution)/shard_map/pallas_call | solution.py:292
  127.1 25.8 %all_to_all.26 = bf16[128,32,128]{2,1,0:T(8,128)(2,1)S(1)} all-to-all(bf16[128,32,128]{2,1,0:T(8,128)(2,1)S(1)} %get-tuple-element.37), channel_id=1, replica_groups=mesh['row'=8,'half'=16,'core'=2] {'row','half'}, dimensions={0} | all-to-all | bytes 2097152 | tf_op jit(solution)/shard_map/all_to_all | solution.py:305
  152.9 6.6 %all-to-all-start.3 = ((bf16[128,32,128]{2,1,0:T(8,128)(2,1)}), bf16[128,32,128]{2,1,0:T(8,128)(2,1)S(1)}, u32[]{:S(2)}, u32[]{:S(2)}) async-start(bf16[128,32,128]{2,1,0:T(8,128)(2,1)} %get-tuple-element.38), calls=%async_computation.3 | async-start | bytes 2097152 | tf_op jit(solution)/shard_map/all_to_all | solution.py:305
  159.5 0.1 collective-permute-start.1
  159.6 21.5 %all-to-all-done.3 = bf16[128,32,128]{2,1,0:T(8,128)(2,1)S(1)} async-done(((bf16[128,32,128]{2,1,0:T(8,128)(2,1)}), bf16[128,32,128]{2,1,0:T(8,128)(2,1)S(1)}, u32[]{:S(2)}, u32[]{:S(2)}) %all-to-all-start.3) | async-done | bytes 1048608 | tf_op jit(solution)/shard_map/all_to_all | solution.py:305
  181.1 4.0 %shard_map.71 = bf16[8,16,32,128]{3,2,1,0:T(8,128)(2,1)} custom-call(s32[1]{0:T(128)} %bitcast.core, bf16[8,16,32,128]{3,2,1,0:T(8,128)(2,1)} %bitcast.10, bf16[8,16,32,128]{3,2,1,0:T(8,128)(2,1)} %collective-permute-done.1.other, bf16[8,16,32,128]{3,2,1,0:T(8,128)(2,1)S(1)} %bitcast.8), custom_call_target="tpu_custom_call" | custom-call | tf_op jit(solution)/shard_map/pallas_call | solution.py:292
  185.2 6.3 %all-to-all-start.4 = ((bf16[128,32,128]{2,1,0:T(8,128)(2,1)}), bf16[128,32,128]{2,1,0:T(8,128)(2,1)S(1)}, u32[]{:S(2)}, u32[]{:S(2)}) async-start(bf16[128,32,128]{2,1,0:T(8,128)(2,1)} %bitcast.5), calls=%async_computation.4 | async-start | bytes 2097152 | tf_op jit(solution)/shard_map/all_to_all | solution.py:305
  191.4 2.0 shard_map.70
  193.4 1.3 copy-done.4
  194.8 0.7 copy-done.9
  195.4 0.6 copy-done.14
  196.0 19.3 %all-to-all-done.4.returned = bf16[128,32,128]{2,1,0:T(8,128)(2,1)S(1)} async-done(((bf16[128,32,128]{2,1,0:T(8,128)(2,1)}), bf16[128,32,128]{2,1,0:T(8,128)(2,1)S(1)}, u32[]{:S(2)}, u32[]{:S(2)}) %all-to-all-start.4) | async-done | bytes 1048608 | tf_op jit(solution)/shard_map/all_to_all | solution.py:305
  215.4 4.2 %shard_map.72 = bf16[128,32,128]{2,1,0:T(8,128)(2,1)} custom-call(f32[3,128,128]{2,1,0:T(8,128)} %copy-done.9, bf16[128,128]{1,0:T(8,128)(2,1)} %copy-done.14, f32[32,128,128]{2,1,0:T(8,128)} %copy-done.4, bf16[32,128,128]{2,1,0:T(8,128)(2,1)} %copy-done, bf16[128,32,128]{2,1,0:T(8,128)(2,1)S(1)} %all-to-all-done.4.returned), custom_call_target="tpu_custom_call" | custom-call | tf_op jit(solution)/shard_map/pallas_call | solution.py:292
  (25 shorter events, 0.1 us)
Async XLA Ops:
  71.1 5.2 %collective-permute-start = (bf16[8,16,32,128]{3,2,1,0:T(8,128)(2,1)S(1)}, bf16[8,16,32,128]{3,2,1,0:T(8,128)(2,1)S(1)}, u32[]{:S(2)}, u32[]{:S(2)}) collective-permute-start(bf16[8,16,32,128]{3,2,1,0:T(8,128)(2,1)S(1)} %get-tuple-element.26), channel_id=1, source_target_pairs={{0,1},{1,0},{2,3},{3,2},{4,5},{5,4},{6,7},{7,6},{8,9},{9,8},{10,11... | collective-permute-start | bytes 3145736 | tf_op jit(solution)/shard_map/ppermute | solution.py:349
  74.8 23.1 %copy-start.1 = (bf16[2,4,128,128]{3,2,1,0:T(8,128)(2,1)S(1)}, bf16[2,4,128,128]{3,2,1,0:T(8,128)(2,1)}, u32[]{:S(2)}) copy-start(bf16[2,4,128,128]{3,2,1,0:T(8,128)(2,1)} %proj.5) | copy-start | bytes 786436
  74.8 23.1 %copy-start.5 = (bf16[2,128,128]{2,1,0:T(8,128)(2,1)S(1)}, bf16[2,128,128]{2,1,0:T(8,128)(2,1)}, u32[]{:S(2)}) copy-start(bf16[2,128,128]{2,1,0:T(8,128)(2,1)} %gate_w.3) | copy-start | bytes 196612
  74.8 23.1 %copy-start.6 = (bf16[2,128,128]{2,1,0:T(8,128)(2,1)S(1)}, bf16[2,128,128]{2,1,0:T(8,128)(2,1)}, u32[]{:S(2)}) copy-start(bf16[2,128,128]{2,1,0:T(8,128)(2,1)} %out_w.3) | copy-start | bytes 196612
  74.8 23.1 %copy-start.15 = (f32[2,128]{1,0:T(2,128)S(1)}, f32[2,128]{1,0:T(2,128)}, u32[]{:S(2)}) copy-start(f32[2,128]{1,0:T(2,128)} %in_gain.5) | copy-start | bytes 3076
  74.8 23.1 %copy-start.16 = (f32[2,128]{1,0:T(2,128)S(1)}, f32[2,128]{1,0:T(2,128)}, u32[]{:S(2)}) copy-start(f32[2,128]{1,0:T(2,128)} %out_gain.3) | copy-start | bytes 3076
  91.1 26.8 %all-to-all-start.1 = ((bf16[128,32,128]{2,1,0:T(8,128)(2,1)}), bf16[128,32,128]{2,1,0:T(8,128)(2,1)S(1)}, u32[]{:S(2)}, u32[]{:S(2)}) async-start(bf16[128,32,128]{2,1,0:T(8,128)(2,1)} %bitcast.2), calls=%async_computation.1 | async-start | bytes 2097152 | tf_op jit(solution)/shard_map/all_to_all | solution.py:305
  99.5 1.3 copy-start.2
  100.8 0.7 copy-start.7
  101.5 0.7 copy-start.10
  102.2 0.6 copy-start.12
  117.9 1.6 copy-start.3
  119.5 0.9 copy-start.8
  120.5 0.9 copy-start.11
  121.4 0.8 copy-start.13
  127.0 64.4 %copy-start = (bf16[32,128,128]{2,1,0:T(8,128)(2,1)}, bf16[32,128,128]{2,1,0:T(8,128)(2,1)S(1)}, u32[]{:S(2)}) copy-start(bf16[32,128,128]{2,1,0:T(8,128)(2,1)S(1)} %get-tuple-element.33.turned.far_turned) | copy-start | bytes 3145732
  152.9 28.3 %copy-start.17 = (bf16[128,32,128]{2,1,0:T(8,128)(2,1)}, bf16[128,32,128]{2,1,0:T(8,128)(2,1)S(1)}, u32[]{:S(2)}) copy-start(bf16[128,32,128]{2,1,0:T(8,128)(2,1)S(1)} %all_to_all.26) | copy-start | bytes 3145732
  152.9 28.3 %all-to-all-start.3 = ((bf16[128,32,128]{2,1,0:T(8,128)(2,1)}), bf16[128,32,128]{2,1,0:T(8,128)(2,1)S(1)}, u32[]{:S(2)}, u32[]{:S(2)}) async-start(bf16[128,32,128]{2,1,0:T(8,128)(2,1)} %get-tuple-element.38), calls=%async_computation.3 | async-start | bytes 2097152 | tf_op jit(solution)/shard_map/all_to_all | solution.py:305
  159.5 21.7 %collective-permute-start.1 = (bf16[8,16,32,128]{3,2,1,0:T(8,128)(2,1)S(1)}, bf16[8,16,32,128]{3,2,1,0:T(8,128)(2,1)}, u32[]{:S(2)}, u32[]{:S(2)}) collective-permute-start(bf16[8,16,32,128]{3,2,1,0:T(8,128)(2,1)S(1)} %bitcast.9), channel_id=1, source_target_pairs={{0,1},{1,0},{2,3},{3,2},{4,5},{5,4},{6,7},{7,6},{8,9},{9,8},{10,11... | collective-permute-start | bytes 3145736 | tf_op jit(solution)/shard_map/ppermute | solution.py:349
  185.2 30.2 %all-to-all-start.4 = ((bf16[128,32,128]{2,1,0:T(8,128)(2,1)}), bf16[128,32,128]{2,1,0:T(8,128)(2,1)S(1)}, u32[]{:S(2)}, u32[]{:S(2)}) async-start(bf16[128,32,128]{2,1,0:T(8,128)(2,1)} %bitcast.5), calls=%async_computation.4 | async-start | bytes 2097152 | tf_op jit(solution)/shard_map/all_to_all | solution.py:305
  193.4 1.3 copy-start.4
  194.7 0.7 copy-start.9
  195.4 0.6 copy-start.14

commit v8 on v7

--- a/solution.py
+++ b/solution.py
@@ -15,7 +15,7 @@
 BF16 = jnp.bfloat16
 PITCH = 40
 WIDE = 136
-STAGGER = 2600
+STAGGER = 2750
 
 
 epsilon = 1e-05
@@ -178,28 +178,15 @@
         piece.wait()
 
 
-def last_kernel(
-    far_gains, far_out, far_gating, far_turned, returned, final,
-    gains, out, gating, turned, tri, rows, mixed, newer, near, arrived, left,
-):
-    halves = [pl.ds(0, 16), pl.ds(16, 16)]
-    pairs = [(far_gains, gains), (far_out, out)]
-    for part in halves:
-        pairs += [(far_gating.at[part], gating.at[part]), (far_turned.at[part], turned.at[part])]
-    pieces = fetch(pairs, arrived)
+def last_kernel(returned, turned, gating, out, gains, final, tri, rows, mixed, newer, near, left):
     spread_rows(returned, tri, 0, 128)
-    pieces[0].wait()
     mix(tri, mixed, gains)
-    pieces[1].wait()
 
     def body(pair):
         for part, channels in enumerate(new_channels(turned, gating, mixed, out, pair)):
             newer[pair * 2 + part] = channels
 
-    for n in range(2):
-        pieces[2 + 2 * n].wait()
-        pieces[3 + 2 * n].wait()
-        each(8, lambda pair, n=n: body(n * 8 + pair))
+    each(16, body)
 
     def back(j):
         rows[pl.ds(j, 128, stride=PITCH), :] = newer[j].T
@@ -340,9 +327,8 @@
 
 
 def last(returned, turned, gating, out, gains):
-    near = [GAINS, SQUARE, (BLOCKS[0], F32), BLOCKS]
-    scratch = [*near, ROWS, ROWS, BLOCKS, (BLOCKS[0], F32), WHOLE, copies(6), copies(4)]
-    return call(last_kernel, [shape(*WHOLE)], scratch, gains, out, gating, turned, returned, far=4, far_outs=(0,))[0]
+    scratch = [ROWS, ROWS, BLOCKS, (BLOCKS[0], F32), WHOLE, copies(4)]
+    return call(last_kernel, [shape(*WHOLE)], scratch, returned, turned, gating, out, gains, far_outs=(0,))[0]
 
 
 def exchanged(pieces):

time: 220 us -> 220 us (level)
    unnamed x36 -> x32, local copies, waits for them, and re-layouts: 10.1 us -> 10.4 us
where the time goes in v8:
time: 220 us; the launch traced here: 219 us
  blocking collectives  90.8 us (41%)
  waiting for transfers between devices  56.8 us (26%)
  Pallas kernels  38.1 us (17%)
  starting transfers between devices  22.6 us (10%)
  local copies, waits for them, and re-layouts  10.4 us (5%)
    all_to_all x2, blocking collectives, to_chips(): lax.all_to_all(pieces, CHIPS, split_axis=0, concat_axis=0, tiled=True)  90.8 us
    all_to_all x3, waiting for transfers between devices, to_chips(): lax.all_to_all(pieces, CHIPS, split_axis=0, concat_axis=0, tiled=True)  55.3 us
    pallas_call x9, Pallas kernels, call(): pl.pallas_call(body, out_shape=outs, in_specs=[smem] * scalars + [hbm] *...  38.1 us
    all_to_all x3, starting transfers between devices, to_chips(): lax.all_to_all(pieces, CHIPS, split_axis=0, concat_axis=0, tiled=True)  19.6 us
    unnamed x32, local copies, waits for them, and re-layouts  10.4 us
  transfers between devices with their start and end apart: 5, of which 4 were waited for; matrix products, arithmetic and copies ran while one was open for 0% of the time, Pallas kernels for 2%

profile of v8, /device:TPU:33, one launch (start us, length us, event | category | flops | bytes accessed | tf_op | source)
XLA Modules:
  0.0 219.0 jit_solution(15671234561840569100)
XLA Ops:
  0.0 4.7 %shard_map.64 = (bf16[128,2,32,128]{3,2,1,0:T(8,128)(2,1)S(1)}, bf16[32,128,128]{2,1,0:T(8,128)(2,1)S(1)}) custom-call(bf16[128,32,128]{2,1,0:T(8,128)(2,1)} %x, bf16[2,4,128,128]{3,2,1,0:T(8,128)(2,1)} %proj.5, f32[2,128]{1,0:T(2,128)} %in_gain.5), custom_call_target="tpu_custom_call" | custom-call | tf_op jit(solution)/shard_map/pallas_call | solution.py:279
  4.8 65.2 %all_to_all.25 = bf16[128,2,32,128]{3,2,1,0:T(8,128)(2,1)S(1)} all-to-all(bf16[128,2,32,128]{3,2,1,0:T(8,128)(2,1)S(1)} %get-tuple-element.24), channel_id=1, replica_groups=mesh['row'=8,'half'=16,'core'=2] {'row','half'}, dimensions={0} | all-to-all | bytes 4194304 | tf_op jit(solution)/shard_map/all_to_all | solution.py:292
  70.0 1.2 shard_map.65
  71.1 2.9 %collective-permute-start = (bf16[8,16,32,128]{3,2,1,0:T(8,128)(2,1)S(1)}, bf16[8,16,32,128]{3,2,1,0:T(8,128)(2,1)S(1)}, u32[]{:S(2)}, u32[]{:S(2)}) collective-permute-start(bf16[8,16,32,128]{3,2,1,0:T(8,128)(2,1)S(1)} %get-tuple-element.26), channel_id=1, source_target_pairs={{0,1},{1,0},{2,3},{3,2},{4,5},{5,4},{6,7},{7,6},{8,9},{9,8},{10,11... | collective-permute-start | bytes 3145736 | tf_op jit(solution)/shard_map/ppermute | solution.py:335
  74.0 0.7 shard_map.66.kept
  74.8 0.0 copy-start.6
  74.8 0.0 copy-start.13
  74.8 1.5 collective-permute-done.taken
  76.3 15.6 %shard_map.67 = (bf16[8,16,32,128]{3,2,1,0:T(8,128)(2,1)}, f32[8,128]{1,0:T(8,128)}) custom-call(s32[1]{0:T(128)} %bitcast.core, f32[8,16,32,128]{3,2,1,0:T(8,128)S(1)} %shard_map.66.kept, bf16[8,16,32,128]{3,2,1,0:T(8,128)(2,1)S(1)} %collective-permute-done.taken), custom_call_target="tpu_custom_call" | custom-call | tf_op jit(solution)/shard_map/pallas_call | solution.py:279
  91.9 6.7 %all-to-all-start.1 = ((bf16[128,32,128]{2,1,0:T(8,128)(2,1)}), bf16[128,32,128]{2,1,0:T(8,128)(2,1)S(1)}, u32[]{:S(2)}, u32[]{:S(2)}) async-start(bf16[128,32,128]{2,1,0:T(8,128)(2,1)} %bitcast.2), calls=%async_computation.1 | async-start | bytes 2097152 | tf_op jit(solution)/shard_map/all_to_all | solution.py:292
  98.7 1.6 shard_map.68
  100.3 1.3 copy-done.1
  101.6 0.7 copy-done.7
  102.3 0.7 copy-done.9
  102.9 0.6 copy-done.11
  103.5 15.2 %all-to-all-done.1.returned = bf16[128,32,128]{2,1,0:T(8,128)(2,1)S(1)} async-done(((bf16[128,32,128]{2,1,0:T(8,128)(2,1)}), bf16[128,32,128]{2,1,0:T(8,128)(2,1)S(1)}, u32[]{:S(2)}, u32[]{:S(2)}) %all-to-all-start.1) | async-done | bytes 1048608 | tf_op jit(solution)/shard_map/all_to_all | solution.py:292
  118.7 1.6 copy-done.2
  120.3 0.9 copy-done.8
  121.3 0.9 copy-done.10
  122.2 0.8 copy-done.12
  122.9 4.9 %shard_map.69 = (bf16[128,32,128]{2,1,0:T(8,128)(2,1)S(1)}, bf16[128,32,128]{2,1,0:T(8,128)(2,1)}, bf16[32,128,128]{2,1,0:T(8,128)(2,1)S(1)}) custom-call(bf16[128,32,128]{2,1,0:T(8,128)(2,1)S(1)} %all-to-all-done.1.returned, bf16[32,128,128]{2,1,0:T(8,128)(2,1)S(1)} %get-tuple-element.28.turned, f32[32,128,128]{2,1,0:T(8,128)S(1)} %copy-done.2, ...), custom_call_target="tpu_custom_call" | custom-call | tf_op jit(solution)/shard_map/pallas_call | solution.py:279
  127.8 25.6 %all_to_all.26 = bf16[128,32,128]{2,1,0:T(8,128)(2,1)S(1)} all-to-all(bf16[128,32,128]{2,1,0:T(8,128)(2,1)S(1)} %get-tuple-element.33), channel_id=1, replica_groups=mesh['row'=8,'half'=16,'core'=2] {'row','half'}, dimensions={0} | all-to-all | bytes 2097152 | tf_op jit(solution)/shard_map/all_to_all | solution.py:292
  153.4 6.6 %all-to-all-start.3 = ((bf16[128,32,128]{2,1,0:T(8,128)(2,1)}), bf16[128,32,128]{2,1,0:T(8,128)(2,1)S(1)}, u32[]{:S(2)}, u32[]{:S(2)}) async-start(bf16[128,32,128]{2,1,0:T(8,128)(2,1)} %get-tuple-element.34), calls=%async_computation.3 | async-start | bytes 2097152 | tf_op jit(solution)/shard_map/all_to_all | solution.py:292
  160.0 0.1 collective-permute-start.1
  160.1 20.8 %all-to-all-done.3 = bf16[128,32,128]{2,1,0:T(8,128)(2,1)S(1)} async-done(((bf16[128,32,128]{2,1,0:T(8,128)(2,1)}), bf16[128,32,128]{2,1,0:T(8,128)(2,1)S(1)}, u32[]{:S(2)}, u32[]{:S(2)}) %all-to-all-start.3) | async-done | bytes 1048608 | tf_op jit(solution)/shard_map/all_to_all | solution.py:292
  180.9 4.0 %shard_map.70 = bf16[8,16,32,128]{3,2,1,0:T(8,128)(2,1)} custom-call(s32[1]{0:T(128)} %bitcast.core, bf16[8,16,32,128]{3,2,1,0:T(8,128)(2,1)} %bitcast.10, bf16[8,16,32,128]{3,2,1,0:T(8,128)(2,1)} %collective-permute-done.1.other, bf16[8,16,32,128]{3,2,1,0:T(8,128)(2,1)S(1)} %bitcast.8), custom_call_target="tpu_custom_call" | custom-call | tf_op jit(solution)/shard_map/pallas_call | solution.py:279
  184.9 6.3 %all-to-all-start.4 = ((bf16[128,32,128]{2,1,0:T(8,128)(2,1)}), bf16[128,32,128]{2,1,0:T(8,128)(2,1)S(1)}, u32[]{:S(2)}, u32[]{:S(2)}) async-start(bf16[128,32,128]{2,1,0:T(8,128)(2,1)} %bitcast.5), calls=%async_computation.4 | async-start | bytes 2097152 | tf_op jit(solution)/shard_map/all_to_all | solution.py:292
  191.2 2.0 shard_map.71
  193.2 1.3 copy-done.3
  194.5 19.4 %all-to-all-done.4.returned = bf16[128,32,128]{2,1,0:T(8,128)(2,1)S(1)} async-done(((bf16[128,32,128]{2,1,0:T(8,128)(2,1)}), bf16[128,32,128]{2,1,0:T(8,128)(2,1)S(1)}, u32[]{:S(2)}, u32[]{:S(2)}) %all-to-all-start.4) | async-done | bytes 1048608 | tf_op jit(solution)/shard_map/all_to_all | solution.py:292
  213.9 1.6 copy-done.4
  215.5 3.4 %shard_map.72 = bf16[128,32,128]{2,1,0:T(8,128)(2,1)} custom-call(bf16[128,32,128]{2,1,0:T(8,128)(2,1)S(1)} %all-to-all-done.4.returned, bf16[32,128,128]{2,1,0:T(8,128)(2,1)S(1)} %get-tuple-element.35.turned, f32[32,128,128]{2,1,0:T(8,128)S(1)} %copy-done.4, bf16[128,128]{1,0:T(8,128)(2,1)S(1)} %get-tuple-element.37.out, ...), custom_call_target="tpu_custom_call" | custom-call | tf_op jit(solution)/shard_map/pallas_call | solution.py:279
  (21 shorter events, 0.0 us)
Async XLA Ops:
  71.1 5.2 %collective-permute-start = (bf16[8,16,32,128]{3,2,1,0:T(8,128)(2,1)S(1)}, bf16[8,16,32,128]{3,2,1,0:T(8,128)(2,1)S(1)}, u32[]{:S(2)}, u32[]{:S(2)}) collective-permute-start(bf16[8,16,32,128]{3,2,1,0:T(8,128)(2,1)S(1)} %get-tuple-element.26), channel_id=1, source_target_pairs={{0,1},{1,0},{2,3},{3,2},{4,5},{5,4},{6,7},{7,6},{8,9},{9,8},{10,11... | collective-permute-start | bytes 3145736 | tf_op jit(solution)/shard_map/ppermute | solution.py:335
  74.8 23.9 %copy-start = (bf16[2,4,128,128]{3,2,1,0:T(8,128)(2,1)S(1)}, bf16[2,4,128,128]{3,2,1,0:T(8,128)(2,1)}, u32[]{:S(2)}) copy-start(bf16[2,4,128,128]{3,2,1,0:T(8,128)(2,1)} %proj.5) | copy-start | bytes 786436
  74.8 23.9 %copy-start.5 = (bf16[2,128,128]{2,1,0:T(8,128)(2,1)S(1)}, bf16[2,128,128]{2,1,0:T(8,128)(2,1)}, u32[]{:S(2)}) copy-start(bf16[2,128,128]{2,1,0:T(8,128)(2,1)} %gate_w.3) | copy-start | bytes 196612
  74.8 23.9 %copy-start.6 = (bf16[2,128,128]{2,1,0:T(8,128)(2,1)S(1)}, bf16[2,128,128]{2,1,0:T(8,128)(2,1)}, u32[]{:S(2)}) copy-start(bf16[2,128,128]{2,1,0:T(8,128)(2,1)} %out_w.3) | copy-start | bytes 196612
  74.8 23.9 %copy-start.13 = (f32[2,128]{1,0:T(2,128)S(1)}, f32[2,128]{1,0:T(2,128)}, u32[]{:S(2)}) copy-start(f32[2,128]{1,0:T(2,128)} %in_gain.5) | copy-start | bytes 3076
  74.8 23.9 %copy-start.14 = (f32[2,128]{1,0:T(2,128)S(1)}, f32[2,128]{1,0:T(2,128)}, u32[]{:S(2)}) copy-start(f32[2,128]{1,0:T(2,128)} %out_gain.3) | copy-start | bytes 3076
  91.9 26.8 %all-to-all-start.1 = ((bf16[128,32,128]{2,1,0:T(8,128)(2,1)}), bf16[128,32,128]{2,1,0:T(8,128)(2,1)S(1)}, u32[]{:S(2)}, u32[]{:S(2)}) async-start(bf16[128,32,128]{2,1,0:T(8,128)(2,1)} %bitcast.2), calls=%async_computation.1 | async-start | bytes 2097152 | tf_op jit(solution)/shard_map/all_to_all | solution.py:292
  100.3 1.3 copy-start.1
  101.6 0.7 copy-start.7
  102.3 0.7 copy-start.9
  102.9 0.6 copy-start.11
  118.7 1.6 copy-start.2
  120.3 0.9 copy-start.8
  121.3 0.9 copy-start.10
  122.2 0.8 copy-start.12
  153.4 27.5 %copy-start.15 = (bf16[128,32,128]{2,1,0:T(8,128)(2,1)}, bf16[128,32,128]{2,1,0:T(8,128)(2,1)S(1)}, u32[]{:S(2)}) copy-start(bf16[128,32,128]{2,1,0:T(8,128)(2,1)S(1)} %all_to_all.26) | copy-start | bytes 3145732
  153.4 27.5 %all-to-all-start.3 = ((bf16[128,32,128]{2,1,0:T(8,128)(2,1)}), bf16[128,32,128]{2,1,0:T(8,128)(2,1)S(1)}, u32[]{:S(2)}, u32[]{:S(2)}) async-start(bf16[128,32,128]{2,1,0:T(8,128)(2,1)} %get-tuple-element.34), calls=%async_computation.3 | async-start | bytes 2097152 | tf_op jit(solution)/shard_map/all_to_all | solution.py:292
  160.0 20.9 %collective-permute-start.1 = (bf16[8,16,32,128]{3,2,1,0:T(8,128)(2,1)S(1)}, bf16[8,16,32,128]{3,2,1,0:T(8,128)(2,1)}, u32[]{:S(2)}, u32[]{:S(2)}) collective-permute-start(bf16[8,16,32,128]{3,2,1,0:T(8,128)(2,1)S(1)} %bitcast.9), channel_id=1, source_target_pairs={{0,1},{1,0},{2,3},{3,2},{4,5},{5,4},{6,7},{7,6},{8,9},{9,8},{10,11... | collective-permute-start | bytes 3145736 | tf_op jit(solution)/shard_map/ppermute | solution.py:335
  184.9 28.9 %all-to-all-start.4 = ((bf16[128,32,128]{2,1,0:T(8,128)(2,1)}), bf16[128,32,128]{2,1,0:T(8,128)(2,1)S(1)}, u32[]{:S(2)}, u32[]{:S(2)}) async-start(bf16[128,32,128]{2,1,0:T(8,128)(2,1)} %bitcast.5), calls=%async_computation.4 | async-start | bytes 2097152 | tf_op jit(solution)/shard_map/all_to_all | solution.py:292
  193.2 1.3 copy-start.3
  213.9 1.6 copy-start.4

commit v9 on v8

--- a/solution.py
+++ b/solution.py
@@ -243,19 +243,24 @@
         joined[r] = (kept[r] + taken[r].astype(F32)).astype(BF16)
 
 
-def incoming_kernel(core, own, other, operand, products, lefts, arrived):
+def lefts_kernel(core, own, other, far_lefts, lefts, arrived, leaving):
     pairs = []
-    for q in (0, 8):
-        for r in range(8):
-            lanes = pl.ds(r * 128, 128)
-            pairs.append((own.at[r, pl.ds(q, 8)], lefts.at[pl.ds(q, 8), core[0], :, lanes]))
-            pairs.append((other.at[r, pl.ds(q, 8)], lefts.at[pl.ds(q, 8), 1 - core[0], :, lanes]))
-    pieces = fetch(pairs, arrived)
+    for r in range(8):
+        lanes = pl.ds(r * 128, 128)
+        pairs.append((own.at[r], lefts.at[:, core[0], :, lanes]))
+        pairs.append((other.at[r], lefts.at[:, 1 - core[0], :, lanes]))
+    for piece in fetch(pairs, arrived):
+        piece.wait()
+    for piece in fetch([(lefts, far_lefts)], leaving):
+        piece.wait()
+
+
+def incoming_kernel(far_lefts, operand, products, lefts, arrived):
+    chunks = [pl.ds(q, 4) for q in range(0, 16, 4)]
+    pieces = fetch([(far_lefts.at[chunk], lefts.at[chunk]) for chunk in chunks], arrived)
     rights = jnp.concatenate([operand[r].reshape(512, 128) for r in range(8)], axis=1)
     for b in range(0, 8, 2):
-        if b % 4 == 0:
-            for piece in pieces[b * 4 : b * 4 + 16]:
-                piece.wait()
+        pieces[b // 2].wait()
         product = lax.dot_general(
             rights,
             lefts[b * 2 : b * 2 + 4].reshape(256, 1024),
@@ -359,17 +364,11 @@
     right = to_chips(right).reshape(HALF)
     gating, out, gains, _ = side(1, turned, *parameters)
     other = exchanged(left)
-    (triangle,) = call(
-        incoming_kernel,
-        [shape(HALF)],
-        [((16, 2, 32, 1024), BF16), copies(32)],
-        core,
-        left,
-        other,
-        right,
-        scalars=1,
-        far=2,
+    rows = ((16, 2, 32, 1024), BF16)
+    (lefts,) = call(
+        lefts_kernel, [pltpu.HBM(*rows)], [rows, copies(16), copies(1)], core, left, other, scalars=1, far=2, far_outs=(0,)
     )
+    (triangle,) = call(incoming_kernel, [shape(HALF)], [rows, copies(4)], lefts, right, far=1)
     returned = to_chips(triangle.reshape(128, 32, 128))
     return last(returned, turned, gating, out, gains)
 

time: 220 us -> 223 us (1.014)
  Pallas kernels: 38.1 us -> 42.1 us
    all_to_all x3, waiting for transfers between devices: 55.3 us -> 50.9 us  [to_chips(): lax.all_to_all(pieces, CHIPS, split_axis=0, concat_axis=0, tiled=True)]
    pallas_call x9 -> x10, Pallas kernels: 38.1 us -> 42.1 us  [call(): pl.pallas_call(body, out_shape=outs, in_specs=[smem] * scalars + [hbm] *...]
    ppermute x2, waiting for transfers between devices: 1.51 us -> 4.15 us  [exchanged(): return lax.ppermute(pieces, 'core', SWAP)]
    unnamed x32 -> x34, local copies, waits for them, and re-layouts: 10.4 us -> 11.4 us
  transfers between devices with their start and end apart: 5 -> 5, of which waited for: 4 -> 5; matrix products, arithmetic and copies ran while one was open for 0% -> 0% of each run, Pallas kernels for 2% -> 3%
where the time goes in v9:
time: 223 us; the launch traced here: 222 us
  blocking collectives  90.8 us (41%)
  waiting for transfers between devices  55 us (25%)
  Pallas kernels  42.1 us (19%)
  starting transfers between devices  22.6 us (10%)
  local copies, waits for them, and re-layouts  11.4 us (5%)
    all_to_all x2, blocking collectives, to_chips(): lax.all_to_all(pieces, CHIPS, split_axis=0, concat_axis=0, tiled=True)  90.8 us
    all_to_all x3, waiting for transfers between devices, to_chips(): lax.all_to_all(pieces, CHIPS, split_axis=0, concat_axis=0, tiled=True)  50.9 us
    pallas_call x10, Pallas kernels, call(): pl.pallas_call(body, out_shape=outs, in_specs=[smem] * scalars + [hbm] *...  42.1 us
    all_to_all x3, starting transfers between devices, to_chips(): lax.all_to_all(pieces, CHIPS, split_axis=0, concat_axis=0, tiled=True)  19.6 us
    unnamed x34, local copies, waits for them, and re-layouts  11.4 us
  transfers between devices with their start and end apart: 5, of which 5 were waited for; matrix products, arithmetic and copies ran while one was open for 0% of the time, Pallas kernels for 3%

profile of v9, /device:TPU:33, one launch (start us, length us, event | category | flops | bytes accessed | tf_op | source)
XLA Modules:
  0.0 222.3 jit_solution(7846054794132191622)
XLA Ops:
  0.0 4.7 %shard_map.64 = (bf16[128,2,32,128]{3,2,1,0:T(8,128)(2,1)S(1)}, bf16[32,128,128]{2,1,0:T(8,128)(2,1)S(1)}) custom-call(bf16[128,32,128]{2,1,0:T(8,128)(2,1)} %x, bf16[2,4,128,128]{3,2,1,0:T(8,128)(2,1)} %proj.5, f32[2,128]{1,0:T(2,128)} %in_gain.5), custom_call_target="tpu_custom_call" | custom-call | tf_op jit(solution)/shard_map/pallas_call | solution.py:284
  4.8 65.2 %all_to_all.25 = bf16[128,2,32,128]{3,2,1,0:T(8,128)(2,1)S(1)} all-to-all(bf16[128,2,32,128]{3,2,1,0:T(8,128)(2,1)S(1)} %get-tuple-element.24), channel_id=1, replica_groups=mesh['row'=8,'half'=16,'core'=2] {'row','half'}, dimensions={0} | all-to-all | bytes 4194304 | tf_op jit(solution)/shard_map/all_to_all | solution.py:297
  70.0 1.2 shard_map.65
  71.1 2.9 %collective-permute-start = (bf16[8,16,32,128]{3,2,1,0:T(8,128)(2,1)S(1)}, bf16[8,16,32,128]{3,2,1,0:T(8,128)(2,1)S(1)}, u32[]{:S(2)}, u32[]{:S(2)}) collective-permute-start(bf16[8,16,32,128]{3,2,1,0:T(8,128)(2,1)S(1)} %get-tuple-element.26), channel_id=1, source_target_pairs={{0,1},{1,0},{2,3},{3,2},{4,5},{5,4},{6,7},{7,6},{8,9},{9,8},{10,11... | collective-permute-start | bytes 3145736 | tf_op jit(solution)/shard_map/ppermute | solution.py:340
  74.0 0.7 shard_map.66.kept
  74.8 1.5 collective-permute-done.taken
  76.3 15.6 %shard_map.67 = (bf16[8,16,32,128]{3,2,1,0:T(8,128)(2,1)}, f32[8,128]{1,0:T(8,128)}) custom-call(s32[1]{0:T(128)} %bitcast.core, f32[8,16,32,128]{3,2,1,0:T(8,128)S(1)} %shard_map.66.kept, bf16[8,16,32,128]{3,2,1,0:T(8,128)(2,1)S(1)} %collective-permute-done.taken), custom_call_target="tpu_custom_call" | custom-call | tf_op jit(solution)/shard_map/pallas_call | solution.py:284
  91.9 6.7 %all-to-all-start.1 = ((bf16[128,32,128]{2,1,0:T(8,128)(2,1)}), bf16[128,32,128]{2,1,0:T(8,128)(2,1)S(1)}, u32[]{:S(2)}, u32[]{:S(2)}) async-start(bf16[128,32,128]{2,1,0:T(8,128)(2,1)} %bitcast.2), calls=%async_computation.1 | async-start | bytes 2097152 | tf_op jit(solution)/shard_map/all_to_all | solution.py:297
  98.7 1.6 shard_map.68
  100.3 1.3 copy-done.1
  101.6 0.7 copy-done.7
  102.3 0.7 copy-done.9
  103.0 0.6 copy-done.11
  103.6 15.2 %all-to-all-done.1.returned = bf16[128,32,128]{2,1,0:T(8,128)(2,1)S(1)} async-done(((bf16[128,32,128]{2,1,0:T(8,128)(2,1)}), bf16[128,32,128]{2,1,0:T(8,128)(2,1)S(1)}, u32[]{:S(2)}, u32[]{:S(2)}) %all-to-all-start.1) | async-done | bytes 1048608 | tf_op jit(solution)/shard_map/all_to_all | solution.py:297
  118.7 1.6 copy-done.2
  120.3 0.9 copy-done.8
  121.3 0.9 copy-done.10
  122.2 0.8 copy-done.12
  122.9 4.9 %shard_map.69 = (bf16[128,32,128]{2,1,0:T(8,128)(2,1)S(1)}, bf16[128,32,128]{2,1,0:T(8,128)(2,1)}, bf16[32,128,128]{2,1,0:T(8,128)(2,1)S(1)}) custom-call(bf16[128,32,128]{2,1,0:T(8,128)(2,1)S(1)} %all-to-all-done.1.returned, bf16[32,128,128]{2,1,0:T(8,128)(2,1)S(1)} %get-tuple-element.28.turned, f32[32,128,128]{2,1,0:T(8,128)S(1)} %copy-done.2, ...), custom_call_target="tpu_custom_call" | custom-call | tf_op jit(solution)/shard_map/pallas_call | solution.py:284
  127.8 25.6 %all_to_all.26 = bf16[128,32,128]{2,1,0:T(8,128)(2,1)S(1)} all-to-all(bf16[128,32,128]{2,1,0:T(8,128)(2,1)S(1)} %get-tuple-element.33), channel_id=1, replica_groups=mesh['row'=8,'half'=16,'core'=2] {'row','half'}, dimensions={0} | all-to-all | bytes 2097152 | tf_op jit(solution)/shard_map/all_to_all | solution.py:297
  153.4 6.6 %all-to-all-start.3 = ((bf16[128,32,128]{2,1,0:T(8,128)(2,1)}), bf16[128,32,128]{2,1,0:T(8,128)(2,1)S(1)}, u32[]{:S(2)}, u32[]{:S(2)}) async-start(bf16[128,32,128]{2,1,0:T(8,128)(2,1)} %get-tuple-element.34), calls=%async_computation.3 | async-start | bytes 2097152 | tf_op jit(solution)/shard_map/all_to_all | solution.py:297
  160.1 2.6 %collective-permute-done.1.other = bf16[8,16,32,128]{3,2,1,0:T(8,128)(2,1)S(1)} collective-permute-done((bf16[8,16,32,128]{3,2,1,0:T(8,128)(2,1)S(1)}, bf16[8,16,32,128]{3,2,1,0:T(8,128)(2,1)S(1)}, u32[]{:S(2)}, u32[]{:S(2)}) %collective-permute-start.1) | collective-permute-done | bytes 1048608 | tf_op jit(solution)/shard_map/ppermute | solution.py:340
  162.8 1.0 copy-done.16
  163.8 3.1 %shard_map.70.far_lefts = bf16[16,2,32,1024]{3,2,1,0:T(8,128)(2,1)} custom-call(s32[1]{0:T(128)} %bitcast.core, bf16[8,16,32,128]{3,2,1,0:T(8,128)(2,1)} %bitcast.10, bf16[8,16,32,128]{3,2,1,0:T(8,128)(2,1)} %copy-done.16), custom_call_target="tpu_custom_call" | custom-call | tf_op jit(solution)/shard_map/pallas_call | solution.py:284
  166.9 14.1 %all-to-all-done.3 = bf16[128,32,128]{2,1,0:T(8,128)(2,1)S(1)} async-done(((bf16[128,32,128]{2,1,0:T(8,128)(2,1)}), bf16[128,32,128]{2,1,0:T(8,128)(2,1)S(1)}, u32[]{:S(2)}, u32[]{:S(2)}) %all-to-all-start.3) | async-done | bytes 1048608 | tf_op jit(solution)/shard_map/all_to_all | solution.py:297
  180.9 4.9 %shard_map.71 = bf16[8,16,32,128]{3,2,1,0:T(8,128)(2,1)} custom-call(bf16[16,2,32,1024]{3,2,1,0:T(8,128)(2,1)} %shard_map.70.far_lefts, bf16[8,16,32,128]{3,2,1,0:T(8,128)(2,1)S(1)} %bitcast.8), custom_call_target="tpu_custom_call" | custom-call | tf_op jit(solution)/shard_map/pallas_call | solution.py:284
  185.9 6.3 %all-to-all-start.4 = ((bf16[128,32,128]{2,1,0:T(8,128)(2,1)}), bf16[128,32,128]{2,1,0:T(8,128)(2,1)S(1)}, u32[]{:S(2)}, u32[]{:S(2)}) async-start(bf16[128,32,128]{2,1,0:T(8,128)(2,1)} %bitcast.5), calls=%async_computation.4 | async-start | bytes 2097152 | tf_op jit(solution)/shard_map/all_to_all | solution.py:297
  192.1 2.0 shard_map.72
  194.1 1.4 copy-done.3
  195.5 21.7 %all-to-all-done.4.returned = bf16[128,32,128]{2,1,0:T(8,128)(2,1)S(1)} async-done(((bf16[128,32,128]{2,1,0:T(8,128)(2,1)}), bf16[128,32,128]{2,1,0:T(8,128)(2,1)S(1)}, u32[]{:S(2)}, u32[]{:S(2)}) %all-to-all-start.4) | async-done | bytes 1048608 | tf_op jit(solution)/shard_map/all_to_all | solution.py:297
  217.1 1.6 copy-done.4
  218.7 3.4 %shard_map.73 = bf16[128,32,128]{2,1,0:T(8,128)(2,1)} custom-call(bf16[128,32,128]{2,1,0:T(8,128)(2,1)S(1)} %all-to-all-done.4.returned, bf16[32,128,128]{2,1,0:T(8,128)(2,1)S(1)} %get-tuple-element.35.turned, f32[32,128,128]{2,1,0:T(8,128)S(1)} %copy-done.4, bf16[128,128]{1,0:T(8,128)(2,1)S(1)} %get-tuple-element.37.out, ...), custom_call_target="tpu_custom_call" | custom-call | tf_op jit(solution)/shard_map/pallas_call | solution.py:284
  (24 shorter events, 0.1 us)
Async XLA Ops:
  71.1 5.2 %collective-permute-start = (bf16[8,16,32,128]{3,2,1,0:T(8,128)(2,1)S(1)}, bf16[8,16,32,128]{3,2,1,0:T(8,128)(2,1)S(1)}, u32[]{:S(2)}, u32[]{:S(2)}) collective-permute-start(bf16[8,16,32,128]{3,2,1,0:T(8,128)(2,1)S(1)} %get-tuple-element.26), channel_id=1, source_target_pairs={{0,1},{1,0},{2,3},{3,2},{4,5},{5,4},{6,7},{7,6},{8,9},{9,8},{10,11... | collective-permute-start | bytes 3145736 | tf_op jit(solution)/shard_map/ppermute | solution.py:340
  74.8 23.9 %copy-start = (bf16[2,4,128,128]{3,2,1,0:T(8,128)(2,1)S(1)}, bf16[2,4,128,128]{3,2,1,0:T(8,128)(2,1)}, u32[]{:S(2)}) copy-start(bf16[2,4,128,128]{3,2,1,0:T(8,128)(2,1)} %proj.5) | copy-start | bytes 786436
  74.8 23.9 %copy-start.5 = (bf16[2,128,128]{2,1,0:T(8,128)(2,1)S(1)}, bf16[2,128,128]{2,1,0:T(8,128)(2,1)}, u32[]{:S(2)}) copy-start(bf16[2,128,128]{2,1,0:T(8,128)(2,1)} %gate_w.3) | copy-start | bytes 196612
  74.8 23.9 %copy-start.6 = (bf16[2,128,128]{2,1,0:T(8,128)(2,1)S(1)}, bf16[2,128,128]{2,1,0:T(8,128)(2,1)}, u32[]{:S(2)}) copy-start(bf16[2,128,128]{2,1,0:T(8,128)(2,1)} %out_w.3) | copy-start | bytes 196612
  74.8 23.9 %copy-start.13 = (f32[2,128]{1,0:T(2,128)S(1)}, f32[2,128]{1,0:T(2,128)}, u32[]{:S(2)}) copy-start(f32[2,128]{1,0:T(2,128)} %in_gain.5) | copy-start | bytes 3076
  74.8 23.9 %copy-start.14 = (f32[2,128]{1,0:T(2,128)S(1)}, f32[2,128]{1,0:T(2,128)}, u32[]{:S(2)}) copy-start(f32[2,128]{1,0:T(2,128)} %out_gain.3) | copy-start | bytes 3076
  91.9 26.8 %all-to-all-start.1 = ((bf16[128,32,128]{2,1,0:T(8,128)(2,1)}), bf16[128,32,128]{2,1,0:T(8,128)(2,1)S(1)}, u32[]{:S(2)}, u32[]{:S(2)}) async-start(bf16[128,32,128]{2,1,0:T(8,128)(2,1)} %bitcast.2), calls=%async_computation.1 | async-start | bytes 2097152 | tf_op jit(solution)/shard_map/all_to_all | solution.py:297
  100.3 1.4 copy-start.1
  101.6 0.7 copy-start.7
  102.3 0.7 copy-start.9
  103.0 0.6 copy-start.11
  118.7 1.6 copy-start.2
  120.3 0.9 copy-start.8
  121.3 0.9 copy-start.10
  122.2 0.8 copy-start.12
  153.4 9.4 %copy-start.15 = (bf16[128,32,128]{2,1,0:T(8,128)(2,1)}, bf16[128,32,128]{2,1,0:T(8,128)(2,1)S(1)}, u32[]{:S(2)}) copy-start(bf16[128,32,128]{2,1,0:T(8,128)(2,1)S(1)} %all_to_all.26) | copy-start | bytes 3145732
  153.4 27.5 %all-to-all-start.3 = ((bf16[128,32,128]{2,1,0:T(8,128)(2,1)}), bf16[128,32,128]{2,1,0:T(8,128)(2,1)S(1)}, u32[]{:S(2)}, u32[]{:S(2)}) async-start(bf16[128,32,128]{2,1,0:T(8,128)(2,1)} %get-tuple-element.34), calls=%async_computation.3 | async-start | bytes 2097152 | tf_op jit(solution)/shard_map/all_to_all | solution.py:297
  160.0 2.7 %collective-permute-start.1 = (bf16[8,16,32,128]{3,2,1,0:T(8,128)(2,1)S(1)}, bf16[8,16,32,128]{3,2,1,0:T(8,128)(2,1)S(1)}, u32[]{:S(2)}, u32[]{:S(2)}) collective-permute-start(bf16[8,16,32,128]{3,2,1,0:T(8,128)(2,1)S(1)} %bitcast.9), channel_id=1, source_target_pairs={{0,1},{1,0},{2,3},{3,2},{4,5},{5,4},{6,7},{7,6},{8,9},{9,8},{10,11... | collective-permute-start | bytes 3145736 | tf_op jit(solution)/shard_map/ppermute | solution.py:340
  162.8 1.0 copy-start.16
  185.9 31.2 %all-to-all-start.4 = ((bf16[128,32,128]{2,1,0:T(8,128)(2,1)}), bf16[128,32,128]{2,1,0:T(8,128)(2,1)S(1)}, u32[]{:S(2)}, u32[]{:S(2)}) async-start(bf16[128,32,128]{2,1,0:T(8,128)(2,1)} %bitcast.5), calls=%async_computation.4 | async-start | bytes 2097152 | tf_op jit(solution)/shard_map/all_to_all | solution.py:297
  194.1 1.4 copy-start.3
  217.1 1.6 copy-start.4
